TPU v7x, 32 devices: a whole 2x2x4 slice. The times are simulated.
32 devices in a mesh: dp: 16 (over z, x, core), tensor: 2 (over y).
Axes of the slice: x: 2, y: 2, z: 4, core: 2. Of those that a mesh axis runs over, the one named last changes fastest.
Arguments:
- tokens: bfloat16 [32768, 768], P(('dp', 'tensor')), may hold values from -6 to 6
- grad_tokens: bfloat16 [32768, 768], P(('dp', 'tensor')), may hold values from -6 to 6
- dealing: int32 [32, 1024], P(('dp', 'tensor')), may hold values from 0 to 1023, each once within a row
- segment_ids: int32 [32768], P('dp'), may hold values from 0 to 1, as said below
- ln1_gain: float32 [768], P('dp'), may hold values from 0.5 to 1.5
- ln1_bias: float32 [768], P('dp'), may hold values from -1.5 to 1.5
- w_qkv: bfloat16 [768, 3, 768], P('dp', None, 'tensor'), may hold values from -0.21875 to 0.21875
- b_qv: float32 [2, 768], P(None, 'tensor'), may hold values from -2.5 to 2.5
- w_out: bfloat16 [768, 768], P('tensor', 'dp'), may hold values from -0.875 to 0.875
- b_out: float32 [768], P('dp'), may hold values from -2.5 to 2.5
- ln2_gain: float32 [768], P('dp'), may hold values from 0.5 to 1.5
- ln2_bias: float32 [768], P('dp'), may hold values from -1.5 to 1.5
- w_up: bfloat16 [768, 3072], P('dp', 'tensor'), may hold values from -0.21875 to 0.21875
- b_up: float32 [3072], P('tensor'), may hold values from -2.5 to 2.5
- w_down: bfloat16 [3072, 768], P('tensor', 'dp'), may hold values from -0.109375 to 0.109375
- b_down: float32 [768], P('dp'), may hold values from -2.5 to 2.5
Outputs:
- output: bfloat16 [32768, 768], P(('dp', 'tensor'))
- input_grad: bfloat16 [32768, 768], P(('dp', 'tensor'))
- ln1_gain_grad: float32 [768], P('dp')
- ln1_bias_grad: float32 [768], P('dp')
- w_qkv_grad: float32 [768, 3, 768], P('dp', None, 'tensor')
- b_qv_grad: float32 [2, 768], P(None, 'tensor')
- w_out_grad: float32 [768, 768], P('tensor', 'dp')
- b_out_grad: float32 [768], P('dp')
- ln2_gain_grad: float32 [768], P('dp')
- ln2_bias_grad: float32 [768], P('dp')
- w_up_grad: float32 [768, 3072], P('dp', 'tensor')
- b_up_grad: float32 [3072], P('tensor')
- w_down_grad: float32 [3072, 768], P('tensor', 'dp')
- b_down_grad: float32 [768], P('dp')
Inputs may be any that keep to these rules, and one draw needn't show every extreme that they name: Each row of dealing orders 0 to 1023, each number once. `segment_ids`: in dealt order, the 2048 rows of each group are one sequence (all 0) or two sequences of 1024 rows (0s, then 1s); both kinds of group occur.
All inputs are finite; a program needn't handle non-finite values.
Results may differ from a plain program's by a relative error of at most 0.03.
Values may be sent and summed in bfloat16 or wider, within the bound.
A program may use at most 256 MiB of HBM per device.

v0:
```python
import jax
import jax.numpy as jnp
from jax import lax
from jax.sharding import PartitionSpec as P

HD = 64


EPS = 1e-06
MASKED = -1e30


def normalize(values, gain_row, bias_row):
    centred = values - jnp.mean(values, axis=-1, keepdims=True)
    factor = lax.rsqrt(jnp.mean(centred * centred, axis=-1, keepdims=True) + EPS)
    normed = centred * factor
    return (normed * gain_row + bias_row, normed, factor)


def norm_back(grad_rows, normed, factor, gain_row):
    scaled = grad_rows * gain_row
    centred = scaled - jnp.mean(scaled, axis=-1, keepdims=True)
    return factor * (centred - normed * jnp.mean(scaled * normed, axis=-1, keepdims=True))


def masked_scores(queries, key_rows, seg_rows, seg_cols, score_scale):
    scores = (
        jnp.einsum("qhd,khd->hqk", queries, key_rows, preferred_element_type=jnp.float32)
        * score_scale
    )
    allowed = seg_rows[:, None] == seg_cols[None, :]
    return jnp.where(allowed[None], scores, MASKED)


def attend_forward(pieces, key_rows, value_rows, seg_cols, score_scale):
    queries, seg_rows = pieces
    scores = masked_scores(queries, key_rows, seg_rows, seg_cols, score_scale)
    row_max = jnp.max(scores, axis=-1, keepdims=True)
    weights = jnp.exp(scores - row_max)
    totals = jnp.sum(weights, axis=-1, keepdims=True)
    weights_low = (weights / totals).astype(jnp.bfloat16)
    mixed_heads = jnp.einsum(
        "hqk,khd->qhd", weights_low, value_rows, preferred_element_type=jnp.float32
    )
    return (mixed_heads, row_max + jnp.log(totals))


def attend_backward(sums_so_far, pieces, key_rows, value_rows, seg_cols, score_scale):
    key_sum, value_sum = sums_so_far
    queries, seg_rows, grad_mixed, log_totals = pieces
    weights = jnp.exp(
        masked_scores(queries, key_rows, seg_rows, seg_cols, score_scale) - log_totals
    )
    value_sum = value_sum + jnp.einsum(
        "hqk,qhd->khd", weights.astype(jnp.bfloat16), grad_mixed, preferred_element_type=jnp.float32
    )
    grad_weights = jnp.einsum(
        "qhd,khd->hqk", grad_mixed, value_rows, preferred_element_type=jnp.float32
    )
    inner = jnp.sum(weights * grad_weights, axis=-1, keepdims=True)
    grad_scores = (weights * (grad_weights - inner)).astype(jnp.bfloat16)
    grad_query = (
        jnp.einsum("hqk,khd->qhd", grad_scores, key_rows, preferred_element_type=jnp.float32)
        * score_scale
    )
    key_sum = (
        key_sum
        + jnp.einsum("hqk,qhd->khd", grad_scores, queries, preferred_element_type=jnp.float32)
        * score_scale
    )
    return ((key_sum, value_sum), grad_query)


def reduce_pair(by_rows, by_cols):
    return (
        lax.psum_scatter(by_rows, "dp", scatter_dimension=0, tiled=True),
        lax.psum_scatter(by_cols, "dp", scatter_dimension=1, tiled=True),
    )


def per_device(
    tokens,
    grad_tokens,
    dealing,
    segment_ids,
    ln1_gain,
    ln1_bias,
    w_qkv,
    b_qv,
    w_out,
    b_out,
    ln2_gain,
    ln2_bias,
    w_up,
    b_up,
    w_down,
    b_down,
):
    row_order = dealing[0]
    dealt_rows, dealt_grads = (
        lax.all_to_all(
            jnp.take(tokens, row_order, axis=0), "dp", split_axis=0, concat_axis=0, tiled=True
        ),
        lax.all_to_all(
            jnp.take(grad_tokens, row_order, axis=0), "dp", split_axis=0, concat_axis=0, tiled=True
        ),
    )
    width = dealt_rows.shape[1]
    group_rows = segment_ids.shape[0]
    head_count = w_qkv.shape[2] // HD
    score_scale = HD ** (-0.5)
    qblock = min(512, group_rows)
    blocks = group_rows // qblock
    small_params = jnp.stack([ln1_gain, ln1_bias, b_out, ln2_gain, ln2_bias, b_down])
    wqkv_full, wout_part, wup_part, wdown_part, small_full = (
        lax.all_gather(w_qkv, "dp", axis=0, tiled=True),
        lax.all_gather(w_out, "dp", axis=1, tiled=True),
        lax.all_gather(w_up, "dp", axis=0, tiled=True),
        lax.all_gather(w_down, "dp", axis=1, tiled=True),
        lax.all_gather(small_params.astype(jnp.bfloat16), "dp", axis=1, tiled=True).astype(
            small_params.dtype
        ),
    )
    resid = dealt_rows.astype(jnp.float32)
    ln_one, normed_one, factor_one = normalize(resid, small_full[0], small_full[1])
    ln_one_full = lax.all_gather(ln_one.astype(jnp.bfloat16), "tensor", axis=0, tiled=True)
    qkv = jnp.einsum("nd,dce->nce", ln_one_full, wqkv_full, preferred_element_type=jnp.float32)
    queries = (qkv[:, 0] + b_qv[0]).astype(jnp.bfloat16).reshape(blocks, qblock, head_count, HD)
    key_rows = qkv[:, 1].astype(jnp.bfloat16).reshape(group_rows, head_count, HD)
    value_rows = (qkv[:, 2] + b_qv[1]).astype(jnp.bfloat16).reshape(group_rows, head_count, HD)
    seg_blocks = segment_ids.reshape(blocks, qblock)
    mixed_heads, log_totals = lax.map(
        lambda pieces: attend_forward(pieces, key_rows, value_rows, segment_ids, score_scale),
        (queries, seg_blocks),
    )
    attended = mixed_heads.reshape(group_rows, head_count * HD).astype(jnp.bfloat16)
    attn_branch = lax.psum_scatter(
        jnp.dot(attended, wout_part, preferred_element_type=jnp.float32).astype(jnp.bfloat16),
        "tensor",
        scatter_dimension=0,
        tiled=True,
    ).astype(jnp.float32)
    hidden = resid + attn_branch + small_full[2]
    ln_two, normed_two, factor_two = normalize(hidden, small_full[3], small_full[4])
    ln_two_full = lax.all_gather(ln_two.astype(jnp.bfloat16), "tensor", axis=0, tiled=True)
    pre_act = jnp.dot(ln_two_full, wup_part, preferred_element_type=jnp.float32) + b_up
    activated, gelu_pull = jax.vjp(lambda values: jax.nn.gelu(values, approximate=True), pre_act)
    act_low = activated.astype(jnp.bfloat16)
    output = (
        hidden
        + lax.psum_scatter(
            jnp.dot(act_low, wdown_part, preferred_element_type=jnp.float32).astype(jnp.bfloat16),
            "tensor",
            scatter_dimension=0,
            tiled=True,
        ).astype(jnp.float32)
        + small_full[5]
    )
    grad_out = dealt_grads.astype(jnp.float32)
    grad_out_full = lax.all_gather(dealt_grads, "tensor", axis=0, tiled=True)
    grad_down = jnp.einsum("nf,nd->fd", act_low, grad_out_full, preferred_element_type=jnp.float32)
    grad_act = jnp.einsum(
        "nd,fd->nf", grad_out_full, wdown_part, preferred_element_type=jnp.float32
    )
    grad_pre = gelu_pull(grad_act)[0].astype(jnp.bfloat16)
    bias_up_grad = jnp.sum(grad_pre, axis=0, dtype=jnp.float32)
    grad_up = jnp.einsum("nd,nf->df", ln_two_full, grad_pre, preferred_element_type=jnp.float32)
    grad_ln_two = lax.psum_scatter(
        jnp.einsum("nf,df->nd", grad_pre, wup_part, preferred_element_type=jnp.float32).astype(
            jnp.bfloat16
        ),
        "tensor",
        scatter_dimension=0,
        tiled=True,
    ).astype(jnp.float32)
    gain_two_grad = jnp.sum(grad_ln_two * normed_two, axis=0)
    bias_two_grad = jnp.sum(grad_ln_two, axis=0)
    grad_hidden = grad_out + norm_back(grad_ln_two, normed_two, factor_two, small_full[3])
    grad_hidden_full = lax.all_gather(
        grad_hidden.astype(jnp.bfloat16), "tensor", axis=0, tiled=True
    )
    grad_wout = jnp.einsum(
        "ne,nd->ed", attended, grad_hidden_full, preferred_element_type=jnp.float32
    )
    grad_att = jnp.einsum(
        "nd,ed->ne", grad_hidden_full, wout_part, preferred_element_type=jnp.float32
    ).astype(jnp.bfloat16)
    grad_att = grad_att.reshape(blocks, qblock, head_count, HD)
    empty_sum = jnp.zeros((group_rows, head_count, HD), jnp.float32)
    (key_grad, value_grad), query_grad = lax.scan(
        lambda sums_so_far, pieces: attend_backward(
            sums_so_far, pieces, key_rows, value_rows, segment_ids, score_scale
        ),
        (empty_sum, empty_sum),
        (queries, seg_blocks, grad_att, log_totals),
    )
    qkv_grad = jnp.stack(
        [
            query_grad.reshape(group_rows, -1),
            key_grad.reshape(group_rows, -1),
            value_grad.reshape(group_rows, -1),
        ],
        axis=1,
    ).astype(jnp.bfloat16)
    bias_qv_grad = jnp.stack(
        [
            jnp.sum(qkv_grad[:, 0], axis=0, dtype=jnp.float32),
            jnp.sum(qkv_grad[:, 2], axis=0, dtype=jnp.float32),
        ]
    )
    grad_wqkv = jnp.einsum("nd,nce->dce", ln_one_full, qkv_grad, preferred_element_type=jnp.float32)
    grad_ln_one = lax.psum_scatter(
        jnp.einsum("nce,dce->nd", qkv_grad, wqkv_full, preferred_element_type=jnp.float32).astype(
            jnp.bfloat16
        ),
        "tensor",
        scatter_dimension=0,
        tiled=True,
    ).astype(jnp.float32)
    gain_one_grad = jnp.sum(grad_ln_one * normed_one, axis=0)
    bias_one_grad = jnp.sum(grad_ln_one, axis=0)
    grad_input = grad_hidden + norm_back(grad_ln_one, normed_one, factor_one, small_full[0])
    qkv_part, wout_grad_part = reduce_pair(grad_wqkv, grad_wout)
    up_part, down_part = reduce_pair(grad_up, grad_down)
    tensor_index = lax.axis_index("tensor")
    zero_index = jnp.zeros((), jnp.int32)
    head_width = b_qv.shape[1]
    hidden_width = b_up.shape[0]
    small_grads = jnp.stack(
        [
            gain_one_grad,
            bias_one_grad,
            jnp.sum(grad_hidden, axis=0),
            gain_two_grad,
            bias_two_grad,
            jnp.sum(grad_out, axis=0),
        ]
    )
    qv_spread = lax.dynamic_update_slice(
        jnp.zeros((2, head_width * lax.axis_size("tensor")), jnp.float32),
        bias_qv_grad,
        (zero_index, tensor_index * head_width),
    )
    up_spread = lax.dynamic_update_slice(
        jnp.zeros((hidden_width * lax.axis_size("tensor"),), jnp.float32),
        bias_up_grad,
        (tensor_index * hidden_width,),
    )
    small_total, qv_total, up_total = lax.psum(
        (small_grads, qv_spread, up_spread), ("dp", "tensor")
    )
    piece_width = width // lax.axis_size("dp")
    small_part = lax.dynamic_slice_in_dim(
        small_total, lax.axis_index("dp") * piece_width, piece_width, 1
    )
    qv_part = lax.dynamic_slice_in_dim(qv_total, tensor_index * head_width, head_width, 1)
    bias_up_part = lax.dynamic_slice_in_dim(up_total, tensor_index * hidden_width, hidden_width, 0)
    sent_out, sent_grad = (
        lax.all_to_all(output.astype(jnp.bfloat16), "dp", split_axis=0, concat_axis=0, tiled=True),
        lax.all_to_all(
            grad_input.astype(jnp.bfloat16), "dp", split_axis=0, concat_axis=0, tiled=True
        ),
    )
    restored_out = jnp.zeros_like(sent_out).at[row_order].set(sent_out)
    restored_grad = jnp.zeros_like(sent_grad).at[row_order].set(sent_grad)
    return (
        restored_out,
        restored_grad,
        small_part[0],
        small_part[1],
        qkv_part,
        qv_part,
        wout_grad_part,
        small_part[2],
        small_part[3],
        small_part[4],
        up_part,
        bias_up_part,
        down_part,
        small_part[5],
    )


def solution(mesh):
    placed = (
        P(("dp", "tensor"), None),
        P(("dp", "tensor"), None),
        P(("dp", "tensor"), None),
        P("dp"),
        P("dp"),
        P("dp"),
        P("dp", None, "tensor"),
        P(None, "tensor"),
        P("tensor", "dp"),
        P("dp"),
        P("dp"),
        P("dp"),
        P("dp", "tensor"),
        P("tensor"),
        P("tensor", "dp"),
        P("dp"),
    )
    return jax.shard_map(
        per_device,
        mesh=mesh,
        in_specs=placed,
        out_specs=(
            P(("dp", "tensor"), None),
            P(("dp", "tensor"), None),
            P("dp"),
            P("dp"),
            P("dp", None, "tensor"),
            P(None, "tensor"),
            P("tensor", "dp"),
            P("dp"),
            P("dp"),
            P("dp"),
            P("dp", "tensor"),
            P("tensor"),
            P("tensor", "dp"),
            P("dp"),
        ),
        check_vma=False,
    )
```

profile of v0, /device:TPU:0, one launch (start us, length us, event | category | flops | bytes accessed | tf_op | source)
XLA Modules:
  0.0 1448.8 jit_solution(14021299486769475517)
XLA Ops:
  31.1 44.8 %all-gather = bf16[16,48,6]{1,2,0:T(8,128)(2,1)S(1)} all-gather(bf16[1,48,6]{1,2,0:T(8,128)(2,1)S(1)} %bitcast.228), channel_id=1, replica_groups=mesh['dp'=16,'tensor'=2] {'dp'}, dimensions={0}, use_global_device_ids=true | all-gather | bytes 9792 | tf_op jit(solution)/shard_map/all_gather | solution.py:120
  79.7 29.7 %all_gather.30 = bf16[384,768]{0,1:T(8,128)(2,1)} all-gather(bf16[384,48]{0,1:T(8,128)(2,1)S(1)} %copy-done.30), channel_id=1, replica_groups=mesh['dp'=16,'tensor'=2] {'dp'}, dimensions={1}, use_global_device_ids=true | all-gather | bytes 626688 | tf_op jit(solution)/shard_map/all_gather | solution.py:117
  109.4 21.5 %all-gather.9.cloned.1.call-done = bf16[2048,768]{1,0:T(8,128)(2,1)} async-done(((bf16[1024,768]{1,0:T(8,128)(2,1)}), bf16[2048,768]{1,0:T(8,128)(2,1)}) %all-gather.9.cloned.1.call-update) | async-done | bytes 3145744 | tf_op jit(solution)/shard_map/all_gather | solution.py:126
  153.1 149.2 %while.27 = (s32[]{:T(128)}, bf16[4,512,6,64]{1,3,2,0:T(8,128)(2,1)}, f32[4,6,512,1]{2,1,3,0:T(8,128)S(1)}, s32[4,512]{1,0:T(4,128)S(1)}, s32[2048]{0:T(1024)S(1...) while((s32[]{:T(128)}, ...), condition=%wide.region_5.7_spmd, body=%wide.region_2.6_spmd.sunk | while | flops 1687155712 | bytes 103024832 | solution.py:132
  310.8 43.0 %reduce-scatter.9.cloned.1.call-done = bf16[1024,768]{1,0:T(8,128)(2,1)} async-done(((bf16[2048,768]{1,0:T(8,128)(2,1)}), bf16[1024,768]{1,0:T(8,128)(2,1)}) %reduce-scatter.9.cloned.1.call-update) | async-done | bytes 1572880 | tf_op jit(solution)/shard_map/reduce_scatter | solution.py:137
  359.5 55.0 %all_to_all.45 = bf16[16,64,768]{2,1,0:T(8,128)(2,1)} all-to-all(bf16[16,64,768]{2,1,0:T(8,128)(2,1)} %bitcast.220), channel_id=1, replica_groups=mesh['dp'=16,'tensor'=2] {'dp'}, dimensions={0} | all-to-all | bytes 3145728 | tf_op jit(solution)/shard_map/all_to_all | solution.py:104
  414.6 41.3 %all-gather.13.cloned.1.call-done = bf16[2048,768]{1,0:T(8,128)(2,1)} async-done(((bf16[1024,768]{1,0:T(8,128)(2,1)}), bf16[2048,768]{1,0:T(8,128)(2,1)}) %all-gather.13.cloned.1.call-update) | async-done | bytes 3145744 | tf_op jit(solution)/shard_map/all_gather | solution.py:145
  469.7 30.7 %all-gather.17.cloned.1.call-done = bf16[1536,768]{0,1:T(8,128)(2,1)} async-done(((bf16[1536,48]{0,1:T(8,128)(2,1)}), bf16[1536,768]{0,1:T(8,128)(2,1)}) %all-gather.17.cloned.1.call-update) | async-done | bytes 2359312 | tf_op jit(solution)/shard_map/all_gather | solution.py:119
  500.4 45.2 %all-gather.19.cloned.1.call-done = bf16[2048,768]{1,0:T(8,128)(2,1)} async-done(((bf16[1024,768]{1,0:T(8,128)(2,1)}), bf16[2048,768]{1,0:T(8,128)(2,1)}) %all-gather.19.cloned.1.call-update) | async-done | bytes 3145744 | tf_op jit(solution)/shard_map/all_gather | solution.py:160
  581.6 34.0 %reduce-scatter.13.cloned.1.call-done = bf16[1024,768]{1,0:T(8,128)(2,1)} async-done(((bf16[2048,768]{1,0:T(8,128)(2,1)}), bf16[1024,768]{1,0:T(8,128)(2,1)}) %reduce-scatter.13.cloned.1.call-update) | async-done | bytes 1572880 | tf_op jit(solution)/shard_map/reduce_scatter | solution.py:168
  619.6 41.7 %reduce-scatter.11.cloned.1.call-done = bf16[1024,768]{1,0:T(8,128)(2,1)} async-done(((bf16[2048,768]{1,0:T(8,128)(2,1)}), bf16[1024,768]{1,0:T(8,128)(2,1)}) %reduce-scatter.11.cloned.1.call-update) | async-done | bytes 1572880 | tf_op jit(solution)/shard_map/reduce_scatter | solution.py:151
  669.8 45.0 %all-gather.21.cloned.1.call-done = bf16[2048,768]{1,0:T(8,128)(2,1)} async-done(((bf16[1024,768]{1,0:T(8,128)(2,1)}), bf16[2048,768]{1,0:T(8,128)(2,1)}) %all-gather.21.cloned.1.call-update) | async-done | bytes 3145744 | tf_op jit(solution)/shard_map/all_gather | solution.py:179
  727.9 334.1 %while.28 = (s32[]{:T(128)}, f32[2048,6,64]{0,2,1:T(8,128)}, f32[2048,6,64]{0,2,1:T(8,128)}, bf16[4,512,6,64]{1,3,2,0:T(8,128)(2,1)}, bf16[4,512,6,64]{1,3,2,0:T...) while((s32[]{:T(128)}, f32[2048,6,64]{0,2,1:T(8,128)}, ...), condition=%wide.region_16.18_spmd.clone, body=%wide.region_14.17_spmd.clone.sunk | while | flops 4126077952 | bytes 212699312 | solution.py:190
  770.8 21.3 %multiply_convert_fusion.3 = bf16[6,512,2048]{2,1,0:T(8,128)(2,1)} fusion(f32[6,512,2048]{2,1,0:T(8,128)} %get-tuple-element.408, f32[6,512,2048]{2,1,0:T(8,128)} %fusion.143, f32[6,512]{1,0:T(8,128)S(1)} %get-tuple-element.409, f32[6,512]{1,0:T(8,128)S(1)} %dynamic-slice_bitcast_fusion.2, pred[512,2048]{1,0:T(8,128)(4,1)S(1)} %broadcast_compare_fusion.5), kind=kLoop, calls=%fused_computation.21.clone.1 | loop fusion | flops 37748736 | bytes 63987712 | tf_op jit(solution)/shard_map/while/body/eval_jaxpr/convert_element_type | solution.py:61
  835.8 18.1 %multiply_reduce_fusion.3 = (f32[6,512]{1,0:T(8,128)S(1)}, f32[6,512,2048]{2,1,0:T(8,128)}) fusion(f32[6,512,2048]{2,1,0:T(8,128)} %fusion.143, f32[6,512]{1,0:T(8,128)S(1)} %dynamic-slice_bitcast_fusion.2, pred[512,2048]{1,0:T(8,128)(4,1)S(1)} %broadcast_compare_fusion.5, bf16[2048,6,64]{0,2,1:T(8,128)(2,1)} %get-tuple-element.473, ...), kind=kOutput, calls=%fused_computation.22.clone.1 | convolution fusion | flops 836760576 | bytes 53370884 | tf_op jit(solution)/shard_map/while/body/eval_jaxpr/qhd,khd->hqk/dot_general | solution.py:57
  853.8 21.3 %multiply_convert_fusion.3 = bf16[6,512,2048]{2,1,0:T(8,128)(2,1)} fusion(f32[6,512,2048]{2,1,0:T(8,128)} %get-tuple-element.408, f32[6,512,2048]{2,1,0:T(8,128)} %fusion.143, f32[6,512]{1,0:T(8,128)S(1)} %get-tuple-element.409, f32[6,512]{1,0:T(8,128)S(1)} %dynamic-slice_bitcast_fusion.2, pred[512,2048]{1,0:T(8,128)(4,1)S(1)} %broadcast_compare_fusion.5), kind=kLoop, calls=%fused_computation.21.clone.1 | loop fusion | flops 37748736 | bytes 63987712 | tf_op jit(solution)/shard_map/while/body/eval_jaxpr/convert_element_type | solution.py:61
  919.7 18.1 %multiply_reduce_fusion.3 = (f32[6,512]{1,0:T(8,128)S(1)}, f32[6,512,2048]{2,1,0:T(8,128)}) fusion(f32[6,512,2048]{2,1,0:T(8,128)} %fusion.143, f32[6,512]{1,0:T(8,128)S(1)} %dynamic-slice_bitcast_fusion.2, pred[512,2048]{1,0:T(8,128)(4,1)S(1)} %broadcast_compare_fusion.5, bf16[2048,6,64]{0,2,1:T(8,128)(2,1)} %get-tuple-element.473, ...), kind=kOutput, calls=%fused_computation.22.clone.1 | convolution fusion | flops 836760576 | bytes 53370884 | tf_op jit(solution)/shard_map/while/body/eval_jaxpr/qhd,khd->hqk/dot_general | solution.py:57
  937.8 21.3 %multiply_convert_fusion.3 = bf16[6,512,2048]{2,1,0:T(8,128)(2,1)} fusion(f32[6,512,2048]{2,1,0:T(8,128)} %get-tuple-element.408, f32[6,512,2048]{2,1,0:T(8,128)} %fusion.143, f32[6,512]{1,0:T(8,128)S(1)} %get-tuple-element.409, f32[6,512]{1,0:T(8,128)S(1)} %dynamic-slice_bitcast_fusion.2, pred[512,2048]{1,0:T(8,128)(4,1)S(1)} %broadcast_compare_fusion.5), kind=kLoop, calls=%fused_computation.21.clone.1 | loop fusion | flops 37748736 | bytes 63987712 | tf_op jit(solution)/shard_map/while/body/eval_jaxpr/convert_element_type | solution.py:61
  1003.6 18.1 %multiply_reduce_fusion.3 = (f32[6,512]{1,0:T(8,128)S(1)}, f32[6,512,2048]{2,1,0:T(8,128)}) fusion(f32[6,512,2048]{2,1,0:T(8,128)} %fusion.143, f32[6,512]{1,0:T(8,128)S(1)} %dynamic-slice_bitcast_fusion.2, pred[512,2048]{1,0:T(8,128)(4,1)S(1)} %broadcast_compare_fusion.5, bf16[2048,6,64]{0,2,1:T(8,128)(2,1)} %get-tuple-element.473, ...), kind=kOutput, calls=%fused_computation.22.clone.1 | convolution fusion | flops 836760576 | bytes 53370884 | tf_op jit(solution)/shard_map/while/body/eval_jaxpr/qhd,khd->hqk/dot_general | solution.py:57
  1021.7 21.3 %multiply_convert_fusion.3 = bf16[6,512,2048]{2,1,0:T(8,128)(2,1)} fusion(f32[6,512,2048]{2,1,0:T(8,128)} %get-tuple-element.408, f32[6,512,2048]{2,1,0:T(8,128)} %fusion.143, f32[6,512]{1,0:T(8,128)S(1)} %get-tuple-element.409, f32[6,512]{1,0:T(8,128)S(1)} %dynamic-slice_bitcast_fusion.2, pred[512,2048]{1,0:T(8,128)(4,1)S(1)} %broadcast_compare_fusion.5), kind=kLoop, calls=%fused_computation.21.clone.1 | loop fusion | flops 37748736 | bytes 63987712 | tf_op jit(solution)/shard_map/while/body/eval_jaxpr/convert_element_type | solution.py:61
  1167.2 66.7 %all-reduce = (f32[6,768]{1,0:T(8,128)S(1)}, f32[2,768]{1,0:T(2,128)S(1)}, f32[3072]{0:T(1024)S(1)}) all-reduce(f32[6,768]{1,0:T(8,128)S(1)} %stack.76, f32[2,768]{1,0:T(2,128)S(1)} %maximum_dynamic-update-slice_fusion, f32[3072]{0:T(1024)S(1)} %dynamic_update_slice.18), channel_id=1, replica_groups=mesh['dp'=16,'tensor'=2] {'dp','tensor'}, use_global_device_ids=true, to_apply=%region_27.29 | all-reduce | flops 9216 | bytes 73728 | tf_op jit(solution)/shard_map/psum | solution.py:249
  1242.8 66.0 %reduce-scatter.23.cloned.1.call-done = f32[1536,48]{0,1:T(8,128)} async-done(((f32[1536,768]{0,1:T(8,128)}), f32[1536,48]{0,1:T(8,128)}) %reduce-scatter.23.cloned.1.call-update) | async-done | bytes 294928 | tf_op jit(solution)/shard_map/reduce_scatter | solution.py:77
  1308.9 61.5 %reduce-scatter.19.cloned.1.call-done = f32[384,48]{0,1:T(8,128)} async-done(((f32[384,768]{0,1:T(8,128)}), f32[384,48]{0,1:T(8,128)}) %reduce-scatter.19.cloned.1.call-update) | async-done | bytes 73744 | tf_op jit(solution)/shard_map/reduce_scatter | solution.py:77
  1370.3 71.4 %reduce-scatter.17.cloned.1.call-done = f32[48,3,384]{2,0,1:T(8,128)} async-done(((f32[768,3,384]{2,0,1:T(8,128)}), f32[48,3,384]{2,0,1:T(8,128)}) %reduce-scatter.17.cloned.1.call-update) | async-done | bytes 221200 | tf_op jit(solution)/shard_map/reduce_scatter | solution.py:76
  (301 shorter events, 596.1 us)
Async XLA Ops:
  22.6 54.0 %all-to-all-start = ((bf16[16,64,768]{2,1,0:T(8,128)(2,1)}), bf16[16,64,768]{2,1,0:T(8,128)(2,1)S(1)}, u32[]{:S(2)}, u32[]{:S(2)}) async-start(bf16[16,64,768]{2,1,0:T(8,128)(2,1)} %bitcast.8), calls=%async_computation | async-start | bytes 3145728 | tf_op jit(solution)/shard_map/all_to_all | solution.py:101
  30.1 79.2 %all-gather.11.cloned.1.call-start = ((), (), s32[]{:S(2)}) async-start(), calls=%async_computation.13 | async-start | bytes 1880064 | tf_op jit(solution)/shard_map/all_gather | solution.py:116
  30.9 100.0 %all-gather.9.cloned.1.call-start = ((), (), s32[]{:S(2)}) async-start(), calls=%async_computation.12 | async-start | bytes 4718592 | tf_op jit(solution)/shard_map/all_gather | solution.py:126
  77.6 53.3 %copy-start.25 = (f32[1024]{0:T(1024)}, f32[1024]{0:T(1024)S(1)}, u32[]{:S(2)}) copy-start(f32[1024]{0:T(1024)S(1)} %rsqrt.20) | copy-start | bytes 12292
  79.4 274.3 %reduce-scatter.9.cloned.1.call-start = ((), (), s32[]{:S(2)}) async-start(), calls=%async_computation.14 | async-start | bytes 4718592 | tf_op jit(solution)/shard_map/reduce_scatter | solution.py:137
  310.1 43.6 %copy-start.22 = (f32[768]{0:T(1024)S(1)}, f32[768]{0:T(1024)}, u32[]{:S(2)}) copy-start(f32[768]{0:T(1024)} %get-tuple-element.213) | copy-start | bytes 9220
  310.2 104.4 %all-gather.15.cloned.1.call-start = ((), (), s32[]{:S(2)}) async-start(), calls=%async_computation.16 | async-start | bytes 2506752 | tf_op jit(solution)/shard_map/all_gather | solution.py:118
  310.7 145.2 %all-gather.13.cloned.1.call-start = ((), (), s32[]{:S(2)}) async-start(), calls=%async_computation.15 | async-start | bytes 4718592 | tf_op jit(solution)/shard_map/all_gather | solution.py:145
  358.9 97.0 %copy-start.46 = (f32[1536]{0:T(1024)S(1)}, f32[1536]{0:T(1024)}, u32[]{:S(2)}) copy-start(f32[1536]{0:T(1024)} %param.35) | copy-start | bytes 18436
  358.9 141.5 %all-gather.17.cloned.1.call-start = ((), (), s32[]{:S(2)}) async-start(), calls=%async_computation.17 | async-start | bytes 2506752 | tf_op jit(solution)/shard_map/all_gather | solution.py:119
  359.5 186.1 %all-gather.19.cloned.1.call-start = ((), (), s32[]{:S(2)}) async-start(), calls=%async_computation.19 | async-start | bytes 4718592 | tf_op jit(solution)/shard_map/all_gather | solution.py:160
  414.5 201.0 %reduce-scatter.13.cloned.1.call-start = ((), (), s32[]{:S(2)}) async-start(), calls=%async_computation.20 | async-start | bytes 4718592 | tf_op jit(solution)/shard_map/reduce_scatter | solution.py:168
  572.0 89.3 %reduce-scatter.11.cloned.1.call-start = ((), (), s32[]{:S(2)}) async-start(), calls=%async_computation.18 | async-start | bytes 4718592 | tf_op jit(solution)/shard_map/reduce_scatter | solution.py:151
  581.5 79.8 %copy-start.35 = (f32[768]{0:T(1024)S(1)}, f32[768]{0:T(1024)}, u32[]{:S(2)}) copy-start(f32[768]{0:T(1024)} %get-tuple-element.210) | copy-start | bytes 9220
  581.5 133.3 %all-gather.21.cloned.1.call-start = ((), (), s32[]{:S(2)}) async-start(), calls=%async_computation.21 | async-start | bytes 4718592 | tf_op jit(solution)/shard_map/all_gather | solution.py:179
  668.4 46.4 %copy-start.21 = (bf16[384,768]{0,1:T(8,128)(2,1)S(1)}, bf16[384,768]{0,1:T(8,128)(2,1)}, u32[]{:S(2)}) copy-start(bf16[384,768]{0,1:T(8,128)(2,1)} %all_gather.30) | copy-start | bytes 1769476
  669.7 457.7 %reduce-scatter.15.cloned.1.call-start = ((), (), s32[]{:S(2)}) async-start(), calls=%async_computation.22 | async-start | bytes 4718592 | tf_op jit(solution)/shard_map/reduce_scatter | solution.py:212
  1083.9 159.0 %reduce-scatter.21.cloned.1.call-start = ((), (), s32[]{:S(2)}) async-start(), calls=%async_computation.25 | async-start | bytes 5013504 | tf_op jit(solution)/shard_map/reduce_scatter | solution.py:76
  1093.6 215.3 %reduce-scatter.23.cloned.1.call-start = ((), (), s32[]{:S(2)}) async-start(), calls=%async_computation.26 | async-start | bytes 5013504 | tf_op jit(solution)/shard_map/reduce_scatter | solution.py:77
  1104.0 266.4 %reduce-scatter.19.cloned.1.call-start = ((), (), s32[]{:S(2)}) async-start(), calls=%async_computation.24 | async-start | bytes 1253376 | tf_op jit(solution)/shard_map/reduce_scatter | solution.py:77
  1110.1 37.7 %all-to-all-start.1 = ((bf16[16,64,768]{2,1,0:T(8,128)(2,1)}), bf16[16,64,768]{2,1,0:T(8,128)(2,1)}, u32[]{:S(2)}, u32[]{:S(2)}) async-start(bf16[16,64,768]{2,1,0:T(8,128)(2,1)} %bitcast.22), calls=%async_computation.3 | async-start | bytes 3145728 | tf_op jit(solution)/shard_map/all_to_all | solution.py:259
  1115.9 325.9 %reduce-scatter.17.cloned.1.call-start = ((), (), s32[]{:S(2)}) async-start(), calls=%async_computation.23 | async-start | bytes 3760128 | tf_op jit(solution)/shard_map/reduce_scatter | solution.py:76
  1147.8 88.0 %all-to-all-start.3 = ((bf16[16,64,768]{2,1,0:T(8,128)(2,1)}), bf16[16,64,768]{2,1,0:T(8,128)(2,1)}, u32[]{:S(2)}, u32[]{:S(2)}) async-start(bf16[16,64,768]{2,1,0:T(8,128)(2,1)} %bitcast.217), calls=%async_computation.7 | async-start | bytes 3145728 | tf_op jit(solution)/shard_map/all_to_all | solution.py:260
  1158.0 283.8 %copy-start.1 = (bf16[1024,768]{1,0:T(8,128)(2,1)S(1)}, bf16[1024,768]{1,0:T(8,128)(2,1)}, u32[]{:S(2)}) copy-start(bf16[1024,768]{1,0:T(8,128)(2,1)} %param.23) | copy-start | bytes 4718596
  (51 other events, 431.7 us)
Sparse Core Ops, SparseCore 0:
  33.3 50.2 all-gather.10
  85.7 45.1 all-gather.8
  310.3 43.4 reduce-scatter.8
  355.9 54.1 all-gather.14
  412.1 43.7 all-gather.12
  458.0 42.2 all-gather.16
  501.9 43.6 all-gather.18
  572.1 43.4 reduce-scatter.12
  617.8 43.4 reduce-scatter.10
  669.8 44.8 all-gather.20
  1084.0 43.4 reduce-scatter.14
  1131.7 97.9 reduce-scatter.20
  1234.1 74.6 reduce-scatter.22
  1312.9 57.3 reduce-scatter.18
  1374.6 67.1 reduce-scatter.16
where the time goes:
time: 1460 us; the launch traced here: 1450 us
  waiting for transfers between devices  520 us (36%)
  matrix products  444 us (30%)
  blocking collectives  196 us (13%)
  other arithmetic  181 us (12%)
  local copies, waits for them, and re-layouts  69.5 us (5%)
  starting transfers between devices  23.4 us (2%)
  between operations  15 us (1%)
    reduce_scatter x2, waiting for transfers between devices, reduce_pair(): lax.psum_scatter(by_cols, 'dp', scatter_dimension=1, tiled=True)  128 us
    dot_general x8, matrix products, masked_scores(): jnp.einsum('qhd,khd->hqk', queries, key_rows, preferred_element_type=jnp....  91.4 us
    convert_element_type x4, other arithmetic, attend_backward(): grad_scores = (weights * (grad_weights - inner)).astype(jnp.bfloat16)  85.1 us
    dot_general x4, matrix products, attend_backward(): jnp.einsum('qhd,khd->hqk', grad_mixed, value_rows, preferred_element_type...  72.3 us
    reduce_scatter x2, waiting for transfers between devices, reduce_pair(): lax.psum_scatter(by_rows, 'dp', scatter_dimension=0, tiled=True)  71.4 us
    psum x1, blocking collectives, per_device(): lax.psum((small_grads, qv_spread, up_spread), ('dp', 'tensor'))  66.7 us
    all_to_all x1, blocking collectives, per_device(): lax.all_to_all(jnp.take(grad_tokens, row_order, axis=0), 'dp', split_axis...  55 us
    dot_general x4, matrix products, attend_backward(): jnp.einsum('hqk,qhd->khd', weights.astype(jnp.bfloat16), grad_mixed, pref...  54.5 us
  transfers between devices with their start and end apart: 18, of which 13 were waited for; matrix products, arithmetic and copies ran while one was open for 7% of the time, Pallas kernels for 0%

commit v1 on v0

v1 whole, which is shorter than its diff:
```python
import functools

import jax
import jax.numpy as jnp
from jax import lax
from jax.experimental import pallas as pl
from jax.experimental.pallas import tpu as pltpu
from jax.sharding import PartitionSpec as P

HD = 64
LANES = 128
EPS = 1e-06
LN2 = 0.6931471805599453
LOG2E = 1.4426950408889634
F32 = jnp.float32
BF16 = jnp.bfloat16


def normalize(values, gain_row, bias_row):
    centred = values - jnp.mean(values, axis=-1, keepdims=True)
    factor = lax.rsqrt(jnp.mean(centred * centred, axis=-1, keepdims=True) + EPS)
    normed = centred * factor
    return (normed * gain_row + bias_row, normed, factor)


def norm_back(grad_rows, normed, factor, gain_row):
    scaled = grad_rows * gain_row
    centred = scaled - jnp.mean(scaled, axis=-1, keepdims=True)
    return factor * (centred - normed * jnp.mean(scaled * normed, axis=-1, keepdims=True))


def mm(left, right, left_dim=1, right_dim=0):
    return lax.dot_general(
        left, right, (((left_dim,), (right_dim,)), ((), ())), preferred_element_type=F32
    )


def head_lanes(head):
    return (lax.broadcasted_iota(jnp.int32, (1, LANES), 1) // HD) == head


def attend_rows(q, keys, values):
    outs, lses = [], []
    one = jnp.ones((), BF16)
    for head in range(2):
        mine = head_lanes(head)
        scores = mm(jnp.where(mine, q, jnp.zeros_like(q)), keys, 1, 1)
        row_max = jnp.max(scores, axis=1, keepdims=True)
        weights = jnp.exp2(scores - row_max).astype(BF16)
        mixed = mm(weights, jnp.where(mine, values, one))
        total = jnp.sum(jnp.where(mine, 0.0, mixed), axis=1, keepdims=True) * (1.0 / HD)
        outs.append(mixed / total)
        lses.append(row_max + jnp.log2(total))
    first = head_lanes(0)
    return (jnp.where(first, outs[0], outs[1]), jnp.where(first, lses[0], lses[1]))


def own_forward(q_ref, kv_ref, mixed_ref, lse_ref, *, qblock):
    for block in range(q_ref.shape[0] // qblock):
        rows = pl.ds(block * qblock, qblock)
        mixed, lse = attend_rows(q_ref[rows, :], kv_ref[:, :LANES], kv_ref[:, LANES:])
        mixed_ref[rows, :] = mixed
        lse_ref[rows, :] = lse


def pair_forward(joined_ref, q_ref, kv_ref, own_ref, own_lse_ref, mixed_ref, lse_ref, *, qblock):
    joined = joined_ref[0] > 0

    @pl.when(joined)
    def _():
        for block in range(q_ref.shape[0] // qblock):
            rows = pl.ds(block * qblock, qblock)
            mixed, lse = attend_rows(q_ref[rows, :], kv_ref[:, :LANES], kv_ref[:, LANES:])
            own_lse = own_lse_ref[rows, :]
            top = jnp.maximum(own_lse, lse)
            own_share = jnp.exp2(own_lse - top)
            pair_share = jnp.exp2(lse - top)
            total = own_share + pair_share
            mixed_ref[rows, :] = (
                (own_ref[rows, :] * own_share + mixed * pair_share) / total
            ).astype(BF16)
            lse_ref[rows, :] = top + jnp.log2(total)

    @pl.when(jnp.logical_not(joined))
    def _():
        mixed_ref[...] = own_ref[...].astype(BF16)
        lse_ref[...] = own_lse_ref[...]


def split_three(values):
    high = values.astype(BF16)
    rest = values - high.astype(F32)
    middle = rest.astype(BF16)
    return high, middle, (rest - middle.astype(F32)).astype(BF16)


def attend_back(q_ref, grad_ref, mixed_ref, lse_ref, kv_ref, dkv_ref, dq_sum, kblock):
    lane = lax.broadcasted_iota(jnp.int32, (1, LANES), 1)
    q = q_ref[...]
    grad = grad_ref[...]
    products = grad.astype(F32) * mixed_ref[...].astype(F32)
    wide_q, wide_grad = [], []
    for head in range(2):
        mine = head_lanes(head)
        spare = (1 - head) * HD
        inner = jnp.sum(jnp.where(mine, products, 0.0), axis=1, keepdims=True)
        lse_parts = split_three(-lse_ref[:, head * HD : head * HD + 1])
        inner_parts = split_three(-inner)
        q_head = jnp.where(mine, q, jnp.zeros_like(q))
        grad_head = jnp.where(mine, grad, jnp.zeros_like(grad))
        for part in range(3):
            q_head = jnp.where(lane == spare + part, lse_parts[part], q_head)
            grad_head = jnp.where(lane == spare + part, inner_parts[part], grad_head)
        wide_q.append(q_head)
        wide_grad.append(grad_head)
    one = jnp.ones((), BF16)
    first = head_lanes(0)
    for block in range(kv_ref.shape[0] // kblock):
        rows = pl.ds(block * kblock, kblock)
        keys = kv_ref[rows, :LANES]
        values = kv_ref[rows, LANES:]
        key_grads, value_grads = [], []
        for head in range(2):
            mine = head_lanes(head)
            weights = jnp.exp2(mm(jnp.where(mine, keys, one), wide_q[head], 1, 1))
            grad_weights = mm(jnp.where(mine, values, one), wide_grad[head], 1, 1)
            grad_scores = (weights * grad_weights).astype(BF16)
            value_grads.append(mm(weights.astype(BF16), grad))
            key_grads.append(mm(grad_scores, q))
            dq_sum[head] += mm(keys, grad_scores, 0, 0)
        dkv_ref[rows, :LANES] = (jnp.where(first, key_grads[0], key_grads[1]) * LN2).astype(BF16)
        dkv_ref[rows, LANES:] = jnp.where(first, value_grads[0], value_grads[1]).astype(BF16)


def query_grad(dq_sum):
    return jnp.concatenate([dq_sum[0, :HD, :], dq_sum[1, HD:, :]], axis=0)


def pair_backward(
    joined_ref, q_ref, grad_ref, mixed_ref, lse_ref, kv_ref, dq_ref, dkv_ref, dq_sum, *, kblock
):
    joined = joined_ref[0] > 0
    dq_sum[...] = jnp.zeros_like(dq_sum)

    @pl.when(joined)
    def _():
        attend_back(q_ref, grad_ref, mixed_ref, lse_ref, kv_ref, dkv_ref, dq_sum, kblock)

    @pl.when(jnp.logical_not(joined))
    def _():
        dkv_ref[...] = jnp.zeros_like(dkv_ref)

    dq_ref[...] = query_grad(dq_sum)


def own_backward(
    q_ref, grad_ref, mixed_ref, lse_ref, kv_ref, pair_dq_ref, dq_ref, dkv_ref, dq_sum, *, kblock
):
    dq_sum[...] = jnp.zeros_like(dq_sum)
    attend_back(q_ref, grad_ref, mixed_ref, lse_ref, kv_ref, dkv_ref, dq_sum, kblock)
    total = query_grad(dq_sum) + pair_dq_ref[...]
    dq_ref[...] = (total.T * HD**-0.5).astype(BF16)


def params(**extra):
    return pltpu.CompilerParams(vmem_limit_bytes=56 << 20, **extra)


def cost(rows, keys, width, products):
    return pl.CostEstimate(
        flops=2 * rows * keys * width * products * 4,
        bytes_accessed=2 * width * (rows + 2 * keys),
        transcendentals=rows * keys * width // HD,
    )


def attention(joined, qkv, kv_of_pair):
    rows = qkv.shape[0]
    width = qkv.shape[1] // 3
    pairs = width // LANES
    column = pl.BlockSpec((rows, LANES), lambda p: (0, p))
    own_kv = pl.BlockSpec((rows, 2 * LANES), lambda p: (0, pairs // 2 + p))
    pair_kv = pl.BlockSpec((rows, 2 * LANES), lambda p: (0, p))
    flag = pl.BlockSpec(memory_space=pltpu.SMEM)
    qblock = min(512, rows)
    shape = jax.ShapeDtypeStruct((rows, width), F32)
    own, own_lse = pl.pallas_call(
        functools.partial(own_forward, qblock=qblock),
        grid=(pairs,),
        in_specs=[column, own_kv],
        out_specs=[column, column],
        out_shape=[shape, shape],
        compiler_params=params(),
        cost_estimate=cost(rows, rows, width, 2),
        name="attend_own",
    )(qkv, qkv)
    return pl.pallas_call(
        functools.partial(pair_forward, qblock=qblock),
        grid=(pairs,),
        in_specs=[flag, column, pair_kv, column, column],
        out_specs=[column, column],
        out_shape=[jax.ShapeDtypeStruct((rows, width), BF16), shape],
        compiler_params=params(),
        cost_estimate=cost(rows, rows, width, 2),
        name="attend_pair",
    )(joined, qkv, kv_of_pair, own, own_lse)


def attention_back_pair(joined, qkv, kv_of_pair, grad, mixed, lse):
    rows, width = grad.shape
    pairs = width // LANES
    column = pl.BlockSpec((rows, LANES), lambda p: (0, p))
    pair_kv = pl.BlockSpec((rows, 2 * LANES), lambda p: (0, p))
    across = pl.BlockSpec((LANES, rows), lambda p: (p, 0))
    return pl.pallas_call(
        functools.partial(pair_backward, kblock=min(512, rows)),
        grid=(pairs,),
        in_specs=[pl.BlockSpec(memory_space=pltpu.SMEM)] + [column] * 4 + [pair_kv],
        out_specs=[across, pair_kv],
        out_shape=[
            jax.ShapeDtypeStruct((width, rows), F32),
            jax.ShapeDtypeStruct((rows, 2 * width), BF16),
        ],
        scratch_shapes=[pltpu.VMEM((2, LANES, rows), F32)],
        compiler_params=params(),
        cost_estimate=cost(rows, rows, width, 5),
        name="attend_back_pair",
    )(joined, qkv, grad, mixed, lse, kv_of_pair)


def attention_back_own(qkv, grad, mixed, lse, pair_dq):
    rows, width = grad.shape
    pairs = width // LANES
    column = pl.BlockSpec((rows, LANES), lambda p: (0, p))
    own_kv = pl.BlockSpec((rows, 2 * LANES), lambda p: (0, pairs // 2 + p))
    kv_out = pl.BlockSpec((rows, 2 * LANES), lambda p: (0, p))
    across = pl.BlockSpec((LANES, rows), lambda p: (p, 0))
    return pl.pallas_call(
        functools.partial(own_backward, kblock=min(512, rows)),
        grid=(pairs,),
        in_specs=[column] * 4 + [own_kv, across],
        out_specs=[column, kv_out],
        out_shape=[
            jax.ShapeDtypeStruct((rows, width), BF16),
            jax.ShapeDtypeStruct((rows, 2 * width), BF16),
        ],
        scratch_shapes=[pltpu.VMEM((2, LANES, rows), F32)],
        compiler_params=params(),
        cost_estimate=cost(rows, rows, width, 5),
        name="attend_back_own",
    )(qkv, grad, mixed, lse, qkv, pair_dq)


def small_kernel(n_dp, slice_ref, bias_ref, all_ref, partner_ref, send_sem, recv_sem):
    me = lax.axis_index("dp")
    t = lax.axis_index("tensor")

    barrier = pltpu.get_barrier_semaphore()

    def greet(step, carry):
        peer = lax.rem(me + step, n_dp)
        pl.semaphore_signal(
            barrier, inc=1, device_id=(peer, t), device_id_type=pl.DeviceIdType.MESH
        )
        return carry

    lax.fori_loop(1, n_dp, greet, 0)
    pl.semaphore_signal(
        barrier, inc=1, device_id=(me, 1 - t), device_id_type=pl.DeviceIdType.MESH
    )
    pl.semaphore_wait(barrier, n_dp)

    def to_peer(step):
        return pltpu.make_async_remote_copy(
            src_ref=slice_ref,
            dst_ref=all_ref.at[me],
            send_sem=send_sem.at[step],
            recv_sem=recv_sem.at[step],
            device_id=(lax.rem(me + step, n_dp), t),
            device_id_type=pl.DeviceIdType.MESH,
        )

    to_partner = pltpu.make_async_remote_copy(
        src_ref=bias_ref,
        dst_ref=partner_ref,
        send_sem=send_sem.at[0],
        recv_sem=recv_sem.at[0],
        device_id=(me, 1 - t),
        device_id_type=pl.DeviceIdType.MESH,
    )
    to_partner.start()

    def start(step, carry):
        to_peer(step).start()
        return carry

    def finish(step, carry):
        to_peer(step).wait()
        return carry

    lax.fori_loop(1, n_dp, start, 0)
    all_ref[me] = slice_ref[...]
    lax.fori_loop(1, n_dp, finish, 0)
    to_partner.wait()


def share_small(n_dp, slices, biases):
    vmem = pl.BlockSpec(memory_space=pltpu.VMEM)
    return pl.pallas_call(
        functools.partial(small_kernel, n_dp),
        in_specs=[vmem, vmem],
        out_specs=[vmem, vmem],
        out_shape=[
            jax.ShapeDtypeStruct((n_dp,) + slices.shape, F32),
            jax.ShapeDtypeStruct(biases.shape, F32),
        ],
        scratch_shapes=[
            pltpu.SemaphoreType.DMA((n_dp,)),
            pltpu.SemaphoreType.DMA((n_dp,)),
        ],
        compiler_params=pltpu.CompilerParams(collective_id=0, has_side_effects=True),
        name="share_small",
    )(slices, biases)


def swap(values):
    return lax.ppermute(values, "tensor", [(0, 1), (1, 0)])


def per_device(
    tokens,
    grad_tokens,
    dealing,
    segment_ids,
    ln1_gain,
    ln1_bias,
    w_qkv,
    b_qv,
    w_out,
    b_out,
    ln2_gain,
    ln2_bias,
    w_up,
    b_up,
    w_down,
    b_down,
):
    n_dp = lax.axis_size("dp")
    t = lax.axis_index("tensor")
    rows, width = tokens.shape
    piece = ln1_gain.shape[0]
    half = b_qv.shape[1]
    hidden_half = b_up.shape[0]
    pairs = width // LANES

    def join(own, other, axis):
        return jnp.where(
            t == 0,
            jnp.concatenate([own, other], axis=axis),
            jnp.concatenate([other, own], axis=axis),
        )

    def mine_of(values, axis):
        size = values.shape[axis] // 2
        low, high = (
            lax.slice_in_dim(values, 0, size, axis=axis),
            lax.slice_in_dim(values, size, 2 * size, axis=axis),
        )
        return jnp.where(t == 0, low, high), jnp.where(t == 0, high, low)

    qkv_local = join(w_qkv, swap(w_qkv), 2)
    kv_local = (
        qkv_local[:, 1:].reshape(piece, 2, pairs, LANES).transpose(0, 2, 1, 3).reshape(piece, -1)
    )
    qkv_local = jnp.concatenate([qkv_local[:, 0], kv_local], axis=1)
    rest_local = jnp.concatenate([w_out.T, w_up, w_down.T], axis=1)
    other_rest = swap(rest_local)
    up_at, down_at = half, half + hidden_half
    rest_local = jnp.concatenate(
        [
            join(rest_local[:, :up_at], other_rest[:, :up_at], 1),
            join(rest_local[:, up_at:down_at], other_rest[:, up_at:down_at], 1),
            join(rest_local[:, down_at:], other_rest[:, down_at:], 1),
        ],
        axis=1,
    )
    wqkv = lax.all_gather(qkv_local, "dp", axis=0, tiled=True)
    rest = lax.all_gather(rest_local, "dp", axis=0, tiled=True)
    wout_t = rest[:, :width]
    wup = rest[:, width : width + 2 * hidden_half]
    wdown_t = rest[:, width + 2 * hidden_half :]
    wkv = wqkv[:, width:]
    wq = wqkv[:, :width]

    small = jnp.stack([ln1_gain, ln1_bias, b_out, ln2_gain, ln2_bias, b_down])
    small = jnp.pad(small, ((0, 2), (0, LANES - piece)))
    biases = jnp.concatenate([b_qv.reshape(-1), b_up])
    bias_rows = -(-biases.shape[0] // (8 * LANES)) * 8
    biases = jnp.pad(biases, (0, bias_rows * LANES - biases.shape[0]))
    biases = biases.reshape(bias_rows, LANES)
    small_all, other_biases = share_small(n_dp, small, biases)
    small_full = small_all[:, :6, :piece].transpose(1, 0, 2).reshape(6, width)
    flat, other_flat = biases.reshape(-1), other_biases.reshape(-1)
    bqv_full = join(flat[: 2 * half].reshape(2, half), other_flat[: 2 * half].reshape(2, half), 1)
    bup_full = join(
        flat[2 * half : 2 * half + hidden_half],
        other_flat[2 * half : 2 * half + hidden_half],
        0,
    )

    row_order = dealing[0]
    picks = (row_order[:, None] == jnp.arange(rows, dtype=jnp.int32)[None, :]).astype(BF16)
    sent_rows = mm(picks, tokens).astype(BF16)
    sent_grads = mm(picks, grad_tokens).astype(BF16)
    dealt = lax.all_to_all(sent_rows, "dp", split_axis=0, concat_axis=0, tiled=True)
    grad_out = lax.all_to_all(sent_grads, "dp", split_axis=0, concat_axis=0, tiled=True)
    dealt_of_pair = swap(dealt)
    joined = (segment_ids[:1] == segment_ids[-1:]).astype(jnp.int32)

    resid = dealt.astype(F32)
    ln_one, normed_one, factor_one = normalize(resid, small_full[0], small_full[1])
    ln_one = ln_one.astype(BF16)
    ln_of_pair = normalize(dealt_of_pair.astype(F32), small_full[0], small_full[1])[0].astype(BF16)
    kv_bias = jnp.stack(
        [jnp.zeros((pairs, LANES), F32), bqv_full[1].reshape(pairs, LANES)], axis=1
    ).reshape(-1)
    score_scale = HD**-0.5 * LOG2E
    shift = jnp.concatenate([bqv_full[0] * score_scale, kv_bias])
    scale = jnp.concatenate([jnp.full((width,), score_scale, F32), jnp.ones((2 * width,), F32)])
    qkv = (mm(ln_one, wqkv) * scale + shift).astype(BF16)
    kv_of_pair = (mm(ln_of_pair, wkv) + kv_bias).astype(BF16)
    attended, lse = attention(joined, qkv, kv_of_pair)
    hidden = resid + mm(attended, wout_t, 1, 1) + small_full[2]

    ln_two, normed_two, factor_two = normalize(hidden, small_full[3], small_full[4])
    ln_two = ln_two.astype(BF16)
    pre_act = mm(ln_two, wup) + bup_full
    activated, gelu_pull = jax.vjp(lambda values: jax.nn.gelu(values, approximate=True), pre_act)
    slope = gelu_pull(jnp.ones_like(pre_act))[0].astype(BF16)
    act = activated.astype(BF16)
    output = (hidden + mm(act, wdown_t, 1, 1) + small_full[5]).astype(BF16)

    grad_down_t = mm(grad_out, act, 0, 0).astype(BF16)
    grad_pre = (mm(grad_out, wdown_t) * slope.astype(F32)).astype(BF16)
    bias_up_grad = jnp.sum(grad_pre, axis=0, dtype=F32)
    grad_up = mm(ln_two, grad_pre, 0, 0).astype(BF16)
    grad_ln_two = mm(grad_pre, wup, 1, 1)
    grad_hidden = grad_out.astype(F32) + norm_back(
        grad_ln_two, normed_two, factor_two, small_full[3]
    )
    grad_branch = grad_hidden.astype(BF16)
    grad_wout_t = mm(grad_branch, attended, 0, 0).astype(BF16)
    grad_att = mm(grad_branch, wout_t).astype(BF16)

    pair_dq, pair_dkv = attention_back_pair(joined, qkv, kv_of_pair, grad_att, attended, lse)
    for_pair = swap(mm(pair_dkv, wkv, 1, 1).astype(BF16))
    dq, dkv = attention_back_own(qkv, grad_att, attended, lse, pair_dq)
    grad_wq = mm(ln_one, dq, 0, 0).astype(BF16)
    grad_wkv = (mm(ln_one, dkv, 0, 0) + mm(ln_of_pair, pair_dkv, 0, 0)).astype(BF16)
    bias_q_grad = jnp.sum(dq, axis=0, dtype=F32)
    kv_sum = jnp.sum(dkv, axis=0, dtype=F32) + jnp.sum(pair_dkv, axis=0, dtype=F32)
    bias_v_grad = kv_sum.reshape(pairs, 2, LANES)[:, 1].reshape(-1)
    grad_ln_one = mm(dq, wq, 1, 1) + mm(dkv, wkv, 1, 1) + for_pair.astype(F32)
    grad_input = (
        grad_hidden + norm_back(grad_ln_one, normed_one, factor_one, small_full[0])
    ).astype(BF16)

    def reduced(values):
        total = lax.psum_scatter(values, "dp", scatter_dimension=0, tiled=True)
        return total

    down_sum = reduced(grad_down_t)
    up_out_sum = reduced(jnp.concatenate([grad_up, grad_wout_t], axis=1))
    qkv_sum = reduced(jnp.concatenate([grad_wq, grad_wkv], axis=1))

    def paired(values):
        mine, other = mine_of(values, 1)
        return mine.astype(F32) + swap(other).astype(F32)

    down_part = paired(down_sum).T
    up_part = paired(up_out_sum[:, : 2 * hidden_half])
    wout_part = paired(up_out_sum[:, 2 * hidden_half :]).T
    q_part = paired(qkv_sum[:, :width])
    kv_part = paired(qkv_sum[:, width:])
    kv_part = kv_part.reshape(piece, pairs // 2, 2, LANES).transpose(0, 2, 1, 3)
    qkv_part = jnp.concatenate(
        [q_part.reshape(piece, 1, half), kv_part.reshape(piece, 2, half)], axis=1
    )

    small_grads = jnp.stack(
        [
            jnp.sum(grad_ln_one * normed_one, axis=0),
            jnp.sum(grad_ln_one, axis=0),
            jnp.sum(grad_hidden, axis=0),
            jnp.sum(grad_ln_two * normed_two, axis=0),
            jnp.sum(grad_ln_two, axis=0),
            jnp.sum(grad_out, axis=0, dtype=F32),
            bias_q_grad,
            bias_v_grad,
        ]
    )
    small_total, up_total = lax.psum((small_grads, bias_up_grad), ("dp", "tensor"))
    small_part = lax.dynamic_slice_in_dim(
        small_total[:6], lax.axis_index("dp") * piece, piece, 1
    )
    qv_part = mine_of(small_total[6:], 1)[0]
    bias_up_part = mine_of(up_total, 0)[0]

    sent_out = lax.all_to_all(output, "dp", split_axis=0, concat_axis=0, tiled=True)
    sent_grad = lax.all_to_all(grad_input, "dp", split_axis=0, concat_axis=0, tiled=True)
    restored_out = mm(picks, sent_out, 0, 0).astype(BF16)
    restored_grad = mm(picks, sent_grad, 0, 0).astype(BF16)
    return (
        restored_out,
        restored_grad,
        small_part[0],
        small_part[1],
        qkv_part,
        qv_part,
        wout_part,
        small_part[2],
        small_part[3],
        small_part[4],
        up_part,
        bias_up_part,
        down_part,
        small_part[5],
    )


def solution(mesh):
    placed = (
        P(("dp", "tensor"), None),
        P(("dp", "tensor"), None),
        P(("dp", "tensor"), None),
        P("dp"),
        P("dp"),
        P("dp"),
        P("dp", None, "tensor"),
        P(None, "tensor"),
        P("tensor", "dp"),
        P("dp"),
        P("dp"),
        P("dp"),
        P("dp", "tensor"),
        P("tensor"),
        P("tensor", "dp"),
        P("dp"),
    )
    return jax.shard_map(
        per_device,
        mesh=mesh,
        in_specs=placed,
        out_specs=(
            P(("dp", "tensor"), None),
            P(("dp", "tensor"), None),
            P("dp"),
            P("dp"),
            P("dp", None, "tensor"),
            P(None, "tensor"),
            P("tensor", "dp"),
            P("dp"),
            P("dp"),
            P("dp"),
            P("dp", "tensor"),
            P("tensor"),
            P("tensor", "dp"),
            P("dp"),
        ),
        check_vma=False,
    )
```

time: 1460 us -> 625 us (0.43)
  waiting for transfers between devices: 520 us -> 148 us
  matrix products: 444 us -> 139 us
  other arithmetic: 181 us -> 34.7 us
  blocking collectives: 196 us -> 72.9 us
  Pallas kernels: 0 us -> 123 us
  local copies, waits for them, and re-layouts: 69.5 us -> 12.6 us
  starting transfers between devices: 23.4 us -> 68.7 us
    dot_general x40 -> x21, matrix products: 444 us -> 139 us  [mm(): lax.dot_general(left, right, (((left_dim,), (right_dim,)), ((), ())), pre...]
    reduce_scatter x8 -> x3, waiting for transfers between devices: 320 us -> 59.2 us  [reduced(): total = lax.psum_scatter(values, 'dp', scatter_dimension=0, tiled=True)]
    all_gather x7 -> x2, waiting for transfers between devices: 184 us -> 13.4 us  [the longest x1 13.3 us: per_device(): rest = lax.all_gather(rest_local, 'dp', axis=0, tiled=True)]
    pallas_call x0 -> x5, Pallas kernels: none -> 123 us  [the longest x1 51.1 us: share_small(): pl.pallas_call(functools.partial(small_kernel, n_dp), in_specs=[vmem, vme...]
    convert_element_type x11 -> x2, other arithmetic: 99.2 us -> 4.05 us  [the longest x1 2.26 us: per_device(): grad_input = (grad_hidden + norm_back(grad_ln_one, normed_one, factor_one...]
    all_gather x2 -> x0, blocking collectives: 74.5 us -> none  [the longest x1 44.8 us: per_device(): lax.all_gather(small_params.astype(jnp.bfloat16), 'dp', axis=1, tiled=True)]
    reduce_sum x9 -> x4, other arithmetic: 57.7 us -> 1.56 us  [the longest x1 0.49 us: per_device(): jnp.sum(dkv, axis=0, dtype=F32) + jnp.sum(pair_dkv, axis=0, dtype=F32)]
    all_to_all x1 -> x0, blocking collectives: 55 us -> none  [per_device(): lax.all_to_all(jnp.take(grad_tokens, row_order, axis=0), 'dp', split_axis...]
  transfers between devices with their start and end apart: 18 -> 18, of which waited for: 13 -> 11; matrix products, arithmetic and copies ran while one was open for 7% -> 21% of each run, Pallas kernels for 0% -> 13%
where the time goes in v1:
time: 625 us; the launch traced here: 616 us
  waiting for transfers between devices  148 us (24%)
  matrix products  139 us (22%)
  Pallas kernels  123 us (20%)
  blocking collectives  72.9 us (12%)
  starting transfers between devices  68.7 us (11%)
  other arithmetic  34.7 us (6%)
  between operations  16.5 us (3%)
  local copies, waits for them, and re-layouts  12.6 us (2%)
    dot_general x21, matrix products, mm(): lax.dot_general(left, right, (((left_dim,), (right_dim,)), ((), ())), pre...  139 us
    psum x1, blocking collectives, per_device(): lax.psum((small_grads, bias_up_grad), ('dp', 'tensor'))  72.9 us
    reduce_scatter x3, waiting for transfers between devices, reduced(): total = lax.psum_scatter(values, 'dp', scatter_dimension=0, tiled=True)  59.2 us
    pallas_call x1, Pallas kernels, share_small(): pl.pallas_call(functools.partial(small_kernel, n_dp), in_specs=[vmem, vme...  51.1 us
    ppermute x9, waiting for transfers between devices, swap(): return lax.ppermute(values, 'tensor', [(0, 1), (1, 0)])  48.2 us
    pallas_call x1, Pallas kernels, attention_back_own(): pl.pallas_call(functools.partial(own_backward, kblock=min(512, rows)), gr...  35 us
    all_to_all x1, starting transfers between devices, per_device(): lax.all_to_all(output, 'dp', split_axis=0, concat_axis=0, tiled=True)  34.8 us
    all_to_all x1, waiting for transfers between devices, per_device(): lax.all_to_all(output, 'dp', split_axis=0, concat_axis=0, tiled=True)  27.1 us
  transfers between devices with their start and end apart: 18, of which 11 were waited for; matrix products, arithmetic and copies ran while one was open for 21% of the time, Pallas kernels for 13%

profile of v1, /device:TPU:0, one launch (start us, length us, event | category | flops | bytes accessed | tf_op | source)
XLA Modules:
  0.0 615.9 jit_solution(14597851489603701783)
XLA Ops:
  18.7 7.2 %collective-permute-done.2 = bf16[48,3456]{1,0:T(8,128)(2,1)S(1)} collective-permute-done((bf16[48,3456]{1,0:T(8,128)(2,1)S(1)}, bf16[48,3456]{1,0:T(8,128)(2,1)S(1)}, u32[]{:S(2)}, u32[]{:S(2)}) %collective-permute-start.2) | collective-permute-done | bytes 331808 | tf_op jit(solution)/shard_map/ppermute | solution.py:327
  30.3 6.0 all-to-all-start
  40.2 51.1 %share_small.1 = (f32[16,8,128]{2,1,0:T(8,128)}, f32[24,128]{1,0:T(8,128)}) custom-call(f32[8,128]{1,0:T(8,128)} %pad.9.slice_ref, f32[24,128]{1,0:T(8,128)} %fusion.63.bias_ref), custom_call_target="tpu_custom_call" | custom-call | tf_op jit(solution)/shard_map/share_small/pallas_call | solution.py:309
  106.9 32.4 %collective-permute-done.1 = bf16[1024,768]{1,0:T(8,128)(2,1)} collective-permute-done((bf16[1024,768]{1,0:T(8,128)(2,1)S(1)}, bf16[1024,768]{1,0:T(8,128)(2,1)}, u32[]{:S(2)}, u32[]{:S(2)}) %collective-permute-start.1) | collective-permute-done | bytes 1572896 | tf_op jit(solution)/shard_map/ppermute | solution.py:327
  143.2 6.8 %add_convert_fusion.1.kv_ref = bf16[1024,1536]{1,0:T(8,128)(2,1)} fusion(f32[1536]{0:T(1024)S(1)} %reshape.201, bf16[768,2304]{1,0:T(8,128)(2,1)} %all-gather.3.cloned.1.call-done, bf16[1024,768]{1,0:T(8,128)(2,1)} %collective-permute-done.1, f32[1024]{0:T(1024)S(1)} %add_rsqrt_fusion.2, f32[1024]{0:T(1024)S(1)} %broadcast_multiply_fusion.6, ...), kind=kOutput, calls=%fused_computation.15 | convolution fusion | flops 2423783424 | bytes 7098368 | tf_op jit(solution)/shard_map/dot_general | solution.py:33
  150.0 5.6 add_convert_fusion.q_ref.kv_ref
  155.6 21.2 %attend_own.1 = (f32[1024,768]{1,0:T(8,128)}, f32[1024,768]{1,0:T(8,128)}) custom-call(bf16[1024,2304]{1,0:T(8,128)(2,1)} %add_convert_fusion.q_ref.kv_ref, bf16[1024,2304]{1,0:T(8,128)(2,1)} %add_convert_fusion.q_ref.kv_ref), custom_call_target="tpu_custom_call" | custom-call | flops 12884901888 | bytes 4718592 | tf_op jit(solution)/shard_map/attend_own/pallas_call | solution.py:187
  176.8 7.5 %attend_pair.1 = (bf16[1024,768]{1,0:T(8,128)(2,1)}, f32[1024,768]{1,0:T(8,128)}) custom-call(s32[1]{0:T(128)S(6)} %convert_element_type.141.joined_ref, bf16[1024,2304]{1,0:T(8,128)(2,1)} %add_convert_fusion.q_ref.kv_ref, bf16[1024,1536]{1,0:T(8,128)(2,1)} %add_convert_fusion.1.kv_ref, f32[1024,768]{1,0:T(8,128)} %get-tuple-element.26.own_ref, ...), custom_call_target="tpu_custom_call" | custom-call | flops 12884901888 | bytes 4718592 | tf_op jit(solution)/shard_map/attend_pair/pallas_call | solution.py:197
  184.3 13.3 %all-gather.5.cloned.1.call-done = bf16[768,6912]{1,0:T(8,128)(2,1)} async-done(((bf16[48,6912]{1,0:T(8,128)(2,1)}), bf16[768,6912]{1,0:T(8,128)(2,1)}) %all-gather.5.cloned.1.call-update) | async-done | bytes 10616848 | tf_op jit(solution)/shard_map/all_gather | solution.py:388
  202.6 10.6 %fusion.16 = f32[1024,3072]{1,0:T(8,128)} fusion(bf16[768,6912]{1,0:T(8,128)(2,1)} %all-gather.5.cloned.1.call-done, f32[1024,768]{1,0:T(8,128)S(1)} %get-tuple-element.65, f32[768]{0:T(1024)S(1)} %add.179, f32[768]{0:T(1024)S(1)} %mul.191, f32[1024]{0:T(1024)S(1)} %add_rsqrt_fusion.1, f32[1024]{0:T(1024)S(1)} %broadcast_multiply_fusion.5), kind=kOutput, calls=%fused_computation.30 | convolution fusion | flops 4835770368 | bytes 20461568 | tf_op jit(solution)/shard_map/dot_general | solution.py:33
  213.2 16.2 %convert_reduce_fusion = (f32[3072]{0:T(1024)}, bf16[1024,3072]{1,0:T(8,128)(2,1)S(1)}) fusion(f32[1024,3072]{1,0:T(8,128)} %fusion.16, f32[3072]{0:T(1024)S(1)} %maximum_select_fusion.4, bf16[1024,768]{1,0:T(8,128)(2,1)S(1)} %bitcast.85, bf16[768,6912]{1,0:T(8,128)(2,1)} %all-gather.5.cloned.1.call-done), kind=kOutput, calls=%fused_computation.9 | convolution fusion | flops 4907332608 | bytes 25190400 | tf_op jit(solution)/shard_map/dot_general | solution.py:33
  229.3 10.4 %multiply_reduce_fusion = (f32[768]{0:T(1024)S(1)}, f32[1024]{0:T(1024)S(1)}, f32[1024]{0:T(1024)S(1)}, f32[768]{0:T(1024)S(1)}, f32[1024,768]{1,0:T(8,128)S(1)}) fusion(f32[1024,768]{1,0:T(8,128)S(1)} %copy-done.6, f32[1024]{0:T(1024)S(1)} %add_rsqrt_fusion.1, f32[1024]{0:T(1024)S(1)} %broadcast_multiply_fusion.5, f32[768]{0:T(1024)S(1)} %mul.191, ...), kind=kOutput, calls=%fused_computation.63 | convolution fusion | flops 4838912000 | bytes 17327104 | tf_op jit(solution)/shard_map/dot_general | solution.py:33
  246.1 8.5 %attend_back_pair.1 = (f32[768,1024]{1,0:T(8,128)}, bf16[1024,1536]{1,0:T(8,128)(2,1)}) custom-call(s32[1]{0:T(128)S(6)} %convert_element_type.141.joined_ref, bf16[1024,2304]{1,0:T(8,128)(2,1)} %add_convert_fusion.q_ref.kv_ref, bf16[1024,768]{1,0:T(8,128)(2,1)} %convolution_convert_fusion.2.grad_ref, bf16[1024,768]{1,0:T(8,128)(2,1)} %get-tuple-element.28.mixed_ref, ...), custom_call_target="tpu_custom_call" | custom-call | flops 32212254720 | bytes 4718592 | tf_op jit(solution)/shard_map/attend_back_pair/pallas_call | solution.py:215
  254.5 35.0 %attend_back_own.1 = (bf16[1024,768]{1,0:T(8,128)(2,1)}, bf16[1024,1536]{1,0:T(8,128)(2,1)}) custom-call(bf16[1024,2304]{1,0:T(8,128)(2,1)} %add_convert_fusion.q_ref.kv_ref, bf16[1024,768]{1,0:T(8,128)(2,1)} %convolution_convert_fusion.2.grad_ref, bf16[1024,768]{1,0:T(8,128)(2,1)} %get-tuple-element.28.mixed_ref, f32[1024,768]{1,0:T(8,128)} %get-tuple-element.29.lse_ref, ...), custom_call_target="tpu_custom_call" | custom-call | flops 32212254720 | bytes 4718592 | tf_op jit(solution)/shard_map/attend_back_own/pallas_call | solution.py:238
  307.6 10.1 %convolution_convert_fusion = bf16[768,3072]{1,0:T(8,128)(2,1)} fusion(bf16[1024,768]{1,0:T(8,128)(2,1)S(1)} %bitcast.86, f32[1024,3072]{1,0:T(8,128)} %fusion.16, f32[3072]{0:T(1024)S(1)} %maximum_select_fusion.4), kind=kOutput, calls=%fused_computation.17 | convolution fusion | flops 4865654784 | bytes 18886656 | tf_op jit(solution)/shard_map/dot_general | solution.py:33
  318.5 6.6 %fusion.51 = bf16[1024,768]{1,0:T(8,128)(2,1)} fusion(bf16[1024,1536]{1,0:T(8,128)(2,1)} %get-tuple-element.33, bf16[768,2304]{1,0:T(8,128)(2,1)} %all-gather.3.cloned.1.call-done), kind=kOutput, calls=%fused_computation.82 | convolution fusion | flops 2416705536 | bytes 7077888 | tf_op jit(solution)/shard_map/dot_general | solution.py:33
  328.1 8.7 %convolution_convert_fusion.1 = bf16[768,3072]{1,0:T(8,128)(2,1)S(1)} fusion(bf16[1024,3072]{1,0:T(8,128)(2,1)} %copy-done.47, f32[1024,768]{1,0:T(8,128)S(1)} %copy-done.7, f32[768]{0:T(1024)S(1)} %add.179, f32[768]{0:T(1024)S(1)} %mul.191, f32[1024]{0:T(1024)S(1)} %add_rsqrt_fusion.1, f32[1024]{0:T(1024)S(1)} %broadcast_multiply_fusion.5), kind=kOutput, calls=%fused_computation.18 | convolution fusion | flops 4838129664 | bytes 14170112 | tf_op jit(solution)/shard_map/dot_general | solution.py:33
  339.8 13.8 %add_convert_fusion.3 = bf16[1024,768]{1,0:T(8,128)(2,1)} fusion(f32[1024,768]{1,0:T(8,128)} %copy-done.5, bf16[768,6912]{1,0:T(8,128)(2,1)} %all-gather.5.cloned.1.call-done, f32[768]{0:T(1024)S(1)} %add.187, f32[1024,3072]{1,0:T(8,128)} %fusion.16, f32[3072]{0:T(1024)S(1)} %maximum_select_fusion.4), kind=kOutput, calls=%fused_computation.67 | convolution fusion | flops 4865654784 | bytes 22035456 | tf_op jit(solution)/shard_map/dot_general | solution.py:33
  353.5 34.8 %all-to-all-start.1 = ((bf16[16,64,768]{2,1,0:T(8,128)(2,1)}), bf16[16,64,768]{2,1,0:T(8,128)(2,1)}, u32[]{:S(2)}, u32[]{:S(2)}) async-start(bf16[16,64,768]{2,1,0:T(8,128)(2,1)} %bitcast.16), calls=%async_computation.1 | async-start | bytes 3145728 | tf_op jit(solution)/shard_map/all_to_all | solution.py:509
  388.4 5.4 fusion.46
  400.4 27.1 %all-to-all-done.1 = bf16[16,64,768]{2,1,0:T(8,128)(2,1)} async-done(((bf16[16,64,768]{2,1,0:T(8,128)(2,1)}), bf16[16,64,768]{2,1,0:T(8,128)(2,1)}, u32[]{:S(2)}, u32[]{:S(2)}) %all-to-all-start.1) | async-done | bytes 1572896 | tf_op jit(solution)/shard_map/all_to_all | solution.py:509
  427.5 9.4 %all-to-all-start.3 = ((bf16[16,64,768]{2,1,0:T(8,128)(2,1)}), bf16[16,64,768]{2,1,0:T(8,128)(2,1)}, u32[]{:S(2)}, u32[]{:S(2)}) async-start(bf16[16,64,768]{2,1,0:T(8,128)(2,1)} %bitcast.20), calls=%async_computation.3 | async-start | bytes 3145728 | tf_op jit(solution)/shard_map/all_to_all | solution.py:510
  440.7 72.9 %all-reduce.3 = (f32[8,768]{1,0:T(8,128)S(1)}, f32[3072]{0:T(1024)S(1)}) all-reduce(f32[8,768]{1,0:T(8,128)S(1)} %stack.63, f32[3072]{0:T(1024)S(1)} %copy-done.34), channel_id=1, replica_groups=mesh['dp'=16,'tensor'=2] {'dp','tensor'}, use_global_device_ids=true, to_apply=%region_19.20 | all-reduce | flops 9216 | bytes 73728 | tf_op jit(solution)/shard_map/psum | solution.py:502
  539.5 59.2 %reduce-scatter.6.cloned.1.call-done = bf16[48,3840]{1,0:T(8,128)(2,1)} async-done(((bf16[768,3840]{1,0:T(8,128)(2,1)}), bf16[48,3840]{1,0:T(8,128)(2,1)}) %reduce-scatter.6.cloned.1.call-update) | async-done | bytes 368656 | tf_op jit(solution)/shard_map/reduce_scatter | solution.py:469
  (234 shorter events, 119.7 us)
Async XLA Ops:
  7.2 135.9 %all-gather.3.cloned.1.call-start = ((), (), s32[]{:S(2)}) async-start(), calls=%async_computation.7 | async-start | bytes 3760128 | tf_op jit(solution)/shard_map/all_gather | solution.py:387
  7.3 6.3 %collective-permute-start = (bf16[48,3,384]{2,0,1:T(8,128)(2,1)}, bf16[48,3,384]{2,0,1:T(8,128)(2,1)S(1)}, u32[]{:S(2)}, u32[]{:S(2)}) collective-permute-start(bf16[48,3,384]{2,0,1:T(8,128)(2,1)} %param.22), channel_id=1, source_target_pairs={{0,1},{1,0},{2,3},{3,2},{4,5},{5,4},{6,7},{7,6},{8,9},{9,8},{10,11... | collective-permute-start | bytes 331784 | tf_op jit(solution)/shard_map/ppermute | solution.py:327
  15.8 181.8 %all-gather.5.cloned.1.call-start = ((), (), s32[]{:S(2)}) async-start(), calls=%async_computation.8 | async-start | bytes 11280384 | tf_op jit(solution)/shard_map/all_gather | solution.py:388
  16.9 9.0 %collective-permute-start.2 = (bf16[48,3456]{1,0:T(8,128)(2,1)S(1)}, bf16[48,3456]{1,0:T(8,128)(2,1)S(1)}, u32[]{:S(2)}, u32[]{:S(2)}) collective-permute-start(bf16[48,3456]{1,0:T(8,128)(2,1)S(1)} %pad_maximum_fusion.3), channel_id=1, source_target_pairs={{0,1},{1,0},{2,3},{3,2},{4,5},{5,4},{6,7},{7,6},{8,9},{9,8},{10,11... | collective-permute-start | bytes 995336 | tf_op jit(solution)/shard_map/ppermute | solution.py:327
  30.3 68.4 %all-to-all-start = ((bf16[16,64,768]{2,1,0:T(8,128)(2,1)}), bf16[16,64,768]{2,1,0:T(8,128)(2,1)S(1)}, u32[]{:S(2)}, u32[]{:S(2)}) async-start(bf16[16,64,768]{2,1,0:T(8,128)(2,1)} %bitcast.88), calls=%async_computation | async-start | bytes 3145728 | tf_op jit(solution)/shard_map/all_to_all | solution.py:415
  92.9 50.2 %copy-start.20 = (f32[768]{0:T(1024)}, f32[768]{0:T(1024)S(1)}, u32[]{:S(2)}) copy-start(f32[768]{0:T(1024)S(1)} %mul.176) | copy-start | bytes 9220
  93.0 50.2 %copy-start.28 = (f32[768]{0:T(1024)}, f32[768]{0:T(1024)S(1)}, u32[]{:S(2)}) copy-start(f32[768]{0:T(1024)S(1)} %add.165) | copy-start | bytes 9220
  98.7 99.0 %copy-start.2 = (bf16[16,64,768]{2,1,0:T(8,128)(2,1)}, bf16[16,64,768]{2,1,0:T(8,128)(2,1)S(1)}, u32[]{:S(2)}) copy-start(bf16[16,64,768]{2,1,0:T(8,128)(2,1)S(1)} %all-to-all-done) | copy-start | bytes 4718596
  98.7 114.5 %all-to-all-start.2 = ((bf16[16,64,768]{2,1,0:T(8,128)(2,1)}), bf16[16,64,768]{2,1,0:T(8,128)(2,1)S(1)}, u32[]{:S(2)}, u32[]{:S(2)}) async-start(bf16[16,64,768]{2,1,0:T(8,128)(2,1)} %bitcast.87), calls=%async_computation.2 | async-start | bytes 3145728 | tf_op jit(solution)/shard_map/all_to_all | solution.py:416
  102.5 423.0 %reduce-scatter.4.cloned.1.call-start = ((), (), s32[]{:S(2)}) async-start(), calls=%async_computation.9 | async-start | bytes 3760128 | tf_op jit(solution)/shard_map/reduce_scatter | solution.py:469
  102.6 36.8 %collective-permute-start.1 = (bf16[1024,768]{1,0:T(8,128)(2,1)S(1)}, bf16[1024,768]{1,0:T(8,128)(2,1)}, u32[]{:S(2)}, u32[]{:S(2)}) collective-permute-start(bf16[1024,768]{1,0:T(8,128)(2,1)S(1)} %bitcast.83), channel_id=1, source_target_pairs={{0,1},{1,0},{2,3},{3,2},{4,5},{5,4},{6,7},{7,6},{8,9},{9,8},{10,11... | collective-permute-start | bytes 4718600 | tf_op jit(solution)/shard_map/ppermute | solution.py:327
  105.1 38.0 %copy-start.24 = (f32[1024]{0:T(1024)}, f32[1024]{0:T(1024)S(1)}, u32[]{:S(2)}) copy-start(f32[1024]{0:T(1024)S(1)} %rsqrt.28) | copy-start | bytes 12292
  307.6 223.9 %reduce-scatter.8.cloned.1.call-start = ((), (), s32[]{:S(2)}) async-start(), calls=%async_computation.11 | async-start | bytes 5013504 | tf_op jit(solution)/shard_map/reduce_scatter | solution.py:469
  317.8 280.9 %reduce-scatter.6.cloned.1.call-start = ((), (), s32[]{:S(2)}) async-start(), calls=%async_computation.10 | async-start | bytes 6266880 | tf_op jit(solution)/shard_map/reduce_scatter | solution.py:469
  325.1 68.7 %collective-permute-start.3 = (bf16[1024,768]{1,0:T(8,128)(2,1)}, bf16[1024,768]{1,0:T(8,128)(2,1)}, u32[]{:S(2)}, u32[]{:S(2)}) collective-permute-start(bf16[1024,768]{1,0:T(8,128)(2,1)} %fusion.51), channel_id=1, source_target_pairs={{0,1},{1,0},{2,3},{3,2},{4,5},{5,4},{6,7},{7,6},{8,9},{9,8},{10,11... | collective-permute-start | bytes 4718600 | tf_op jit(solution)/shard_map/ppermute | solution.py:327
  353.5 74.0 %all-to-all-start.1 = ((bf16[16,64,768]{2,1,0:T(8,128)(2,1)}), bf16[16,64,768]{2,1,0:T(8,128)(2,1)}, u32[]{:S(2)}, u32[]{:S(2)}) async-start(bf16[16,64,768]{2,1,0:T(8,128)(2,1)} %bitcast.16), calls=%async_computation.1 | async-start | bytes 3145728 | tf_op jit(solution)/shard_map/all_to_all | solution.py:509
  427.5 92.8 %all-to-all-start.3 = ((bf16[16,64,768]{2,1,0:T(8,128)(2,1)}), bf16[16,64,768]{2,1,0:T(8,128)(2,1)}, u32[]{:S(2)}, u32[]{:S(2)}) async-start(bf16[16,64,768]{2,1,0:T(8,128)(2,1)} %bitcast.20), calls=%async_computation.3 | async-start | bytes 3145728 | tf_op jit(solution)/shard_map/all_to_all | solution.py:510
  439.0 76.5 %copy-start.45 = (s32[1,1024]{1,0:T(1,128)S(1)}, s32[1,1024]{1,0:T(1,128)}, u32[]{:S(2)}) copy-start(s32[1,1024]{1,0:T(1,128)} %param.18) | copy-start | bytes 12292
  520.4 88.6 %copy-start.1 = (bf16[1024,768]{1,0:T(8,128)(2,1)S(1)}, bf16[1024,768]{1,0:T(8,128)(2,1)}, u32[]{:S(2)}) copy-start(bf16[1024,768]{1,0:T(8,128)(2,1)} %param.16) | copy-start | bytes 4718596
  526.4 4.3 collective-permute-start.4
  529.6 5.2 collective-permute-start.5
  532.5 5.2 collective-permute-start.8
  599.5 4.0 collective-permute-start.6
  602.0 5.2 collective-permute-start.7
  (43 other events, 386.7 us)
Sparse Core Ops, SparseCore 0:
  15.9 65.1 all-gather.2
  83.4 114.1 all-gather.4
  307.7 108.9 reduce-scatter.3
  420.4 92.8 reduce-scatter.7
  517.1 81.4 reduce-scatter.5

commit v2 on v1

--- a/solution.py
+++ b/solution.py
@@ -6,6 +6,7 @@
 from jax.experimental import pallas as pl
 from jax.experimental.pallas import tpu as pltpu
 from jax.sharding import PartitionSpec as P
+
 
 HD = 64
 LANES = 128
@@ -174,18 +175,15 @@
     )
 
 
-def attention(joined, qkv, kv_of_pair):
+def attention_own(qkv):
     rows = qkv.shape[0]
     width = qkv.shape[1] // 3
     pairs = width // LANES
     column = pl.BlockSpec((rows, LANES), lambda p: (0, p))
     own_kv = pl.BlockSpec((rows, 2 * LANES), lambda p: (0, pairs // 2 + p))
-    pair_kv = pl.BlockSpec((rows, 2 * LANES), lambda p: (0, p))
-    flag = pl.BlockSpec(memory_space=pltpu.SMEM)
-    qblock = min(512, rows)
     shape = jax.ShapeDtypeStruct((rows, width), F32)
-    own, own_lse = pl.pallas_call(
-        functools.partial(own_forward, qblock=qblock),
+    return pl.pallas_call(
+        functools.partial(own_forward, qblock=min(512, rows)),
         grid=(pairs,),
         in_specs=[column, own_kv],
         out_specs=[column, column],
@@ -194,12 +192,22 @@
         cost_estimate=cost(rows, rows, width, 2),
         name="attend_own",
     )(qkv, qkv)
+
+
+def attention_pair(joined, qkv, kv_of_pair, own, own_lse):
+    rows, width = own.shape
+    pairs = width // LANES
+    column = pl.BlockSpec((rows, LANES), lambda p: (0, p))
+    pair_kv = pl.BlockSpec((rows, 2 * LANES), lambda p: (0, p))
     return pl.pallas_call(
-        functools.partial(pair_forward, qblock=qblock),
+        functools.partial(pair_forward, qblock=min(512, rows)),
         grid=(pairs,),
-        in_specs=[flag, column, pair_kv, column, column],
+        in_specs=[pl.BlockSpec(memory_space=pltpu.SMEM), column, pair_kv, column, column],
         out_specs=[column, column],
-        out_shape=[jax.ShapeDtypeStruct((rows, width), BF16), shape],
+        out_shape=[
+            jax.ShapeDtypeStruct((rows, width), BF16),
+            jax.ShapeDtypeStruct((rows, width), F32),
+        ],
         compiler_params=params(),
         cost_estimate=cost(rows, rows, width, 2),
         name="attend_pair",
@@ -321,6 +329,111 @@
         compiler_params=pltpu.CompilerParams(collective_id=0, has_side_effects=True),
         name="share_small",
     )(slices, biases)
+
+
+def sum_small_kernel(
+    n_dp, parts_ref, total_ref, bias_ref, landed, pair_sum, pair_in, own_bias, send_sem, recv_sem
+):
+    me = lax.axis_index("dp")
+    t = lax.axis_index("tensor")
+    mesh_id = pl.DeviceIdType.MESH
+
+    barrier = pltpu.get_barrier_semaphore()
+
+    def greet(step, carry):
+        pl.semaphore_signal(
+            barrier, inc=1, device_id=(lax.rem(me + step, n_dp), t), device_id_type=mesh_id
+        )
+        return carry
+
+    lax.fori_loop(1, n_dp, greet, 0)
+    pl.semaphore_signal(barrier, inc=1, device_id=(me, 1 - t), device_id_type=mesh_id)
+    pl.semaphore_wait(barrier, n_dp)
+
+    def part_to(step):
+        peer = lax.rem(me + step, n_dp)
+        return pltpu.make_async_remote_copy(
+            src_ref=parts_ref.at[peer],
+            dst_ref=landed.at[step],
+            send_sem=send_sem.at[0, step],
+            recv_sem=recv_sem.at[0, step],
+            device_id=(peer, t),
+            device_id_type=mesh_id,
+        )
+
+    def bias_to(step):
+        return pltpu.make_async_remote_copy(
+            src_ref=own_bias,
+            dst_ref=bias_ref.at[me],
+            send_sem=send_sem.at[1, step],
+            recv_sem=recv_sem.at[1, step],
+            device_id=(lax.rem(me + step, n_dp), t),
+            device_id_type=mesh_id,
+        )
+
+    def start_part(step, carry):
+        part_to(step).start()
+        return carry
+
+    def add_part(step, carry):
+        part_to(step).wait()
+        return carry + landed[step]
+
+    lax.fori_loop(1, n_dp, start_part, 0)
+    pair_sum[...] = lax.fori_loop(1, n_dp, add_part, parts_ref[me])
+    to_partner = pltpu.make_async_remote_copy(
+        src_ref=pair_sum,
+        dst_ref=pair_in,
+        send_sem=send_sem.at[1, 0],
+        recv_sem=recv_sem.at[1, 0],
+        device_id=(me, 1 - t),
+        device_id_type=mesh_id,
+    )
+    to_partner.start()
+    to_partner.wait()
+    total = pair_sum[...] + pair_in[...]
+    total_ref[...] = total
+    own_bias[...] = total[:8]
+    bias_ref[me] = total[:8]
+
+    def start_bias(step, carry):
+        bias_to(step).start()
+        return carry
+
+    def finish_bias(step, carry):
+        bias_to(step).wait()
+        return carry
+
+    lax.fori_loop(1, n_dp, start_bias, 0)
+    lax.fori_loop(1, n_dp, finish_bias, 0)
+
+
+def sum_small(n_dp, parts):
+    vmem = pl.BlockSpec(memory_space=pltpu.VMEM)
+    block = parts.shape[1:]
+    return pl.pallas_call(
+        functools.partial(sum_small_kernel, n_dp),
+        in_specs=[vmem],
+        out_specs=[vmem, vmem],
+        out_shape=[
+            jax.ShapeDtypeStruct(block, F32),
+            jax.ShapeDtypeStruct((n_dp, 8, LANES), F32),
+        ],
+        scratch_shapes=[
+            pltpu.VMEM(parts.shape, F32),
+            pltpu.VMEM(block, F32),
+            pltpu.VMEM(block, F32),
+            pltpu.VMEM((8, LANES), F32),
+            pltpu.SemaphoreType.DMA((2, n_dp)),
+            pltpu.SemaphoreType.DMA((2, n_dp)),
+        ],
+        compiler_params=pltpu.CompilerParams(collective_id=1, has_side_effects=True),
+        name="sum_small",
+    )(parts)
+
+
+def after(*values):
+    return lax.optimization_barrier(values)
 
 
 def swap(values):
@@ -360,6 +473,9 @@
             jnp.concatenate([other, own], axis=axis),
         )
 
+    def reduced(values):
+        return lax.psum_scatter(values, "dp", scatter_dimension=0, tiled=True)
+
     def mine_of(values, axis):
         size = values.shape[axis] // 2
         low, high = (
@@ -399,6 +515,17 @@
     biases = jnp.pad(biases, (0, bias_rows * LANES - biases.shape[0]))
     biases = biases.reshape(bias_rows, LANES)
     small_all, other_biases = share_small(n_dp, small, biases)
+    row_order = dealing[0]
+    picks = (row_order[:, None] == jnp.arange(rows, dtype=jnp.int32)[None, :]).astype(BF16)
+    sent_rows = mm(picks, tokens).astype(BF16)
+    sent_rows, small_all = after(sent_rows, small_all)
+    dealt = lax.all_to_all(sent_rows, "dp", split_axis=0, concat_axis=0, tiled=True)
+    grad_tokens, dealt = after(grad_tokens, dealt)
+    sent_grads = mm(picks, grad_tokens).astype(BF16)
+    grad_out = lax.all_to_all(sent_grads, "dp", split_axis=0, concat_axis=0, tiled=True)
+    dealt_of_pair = swap(dealt)
+    joined = (segment_ids[:1] == segment_ids[-1:]).astype(jnp.int32)
+
     small_full = small_all[:, :6, :piece].transpose(1, 0, 2).reshape(6, width)
     flat, other_flat = biases.reshape(-1), other_biases.reshape(-1)
     bqv_full = join(flat[: 2 * half].reshape(2, half), other_flat[: 2 * half].reshape(2, half), 1)
@@ -408,19 +535,9 @@
         0,
     )
 
-    row_order = dealing[0]
-    picks = (row_order[:, None] == jnp.arange(rows, dtype=jnp.int32)[None, :]).astype(BF16)
-    sent_rows = mm(picks, tokens).astype(BF16)
-    sent_grads = mm(picks, grad_tokens).astype(BF16)
-    dealt = lax.all_to_all(sent_rows, "dp", split_axis=0, concat_axis=0, tiled=True)
-    grad_out = lax.all_to_all(sent_grads, "dp", split_axis=0, concat_axis=0, tiled=True)
-    dealt_of_pair = swap(dealt)
-    joined = (segment_ids[:1] == segment_ids[-1:]).astype(jnp.int32)
-
     resid = dealt.astype(F32)
     ln_one, normed_one, factor_one = normalize(resid, small_full[0], small_full[1])
     ln_one = ln_one.astype(BF16)
-    ln_of_pair = normalize(dealt_of_pair.astype(F32), small_full[0], small_full[1])[0].astype(BF16)
     kv_bias = jnp.stack(
         [jnp.zeros((pairs, LANES), F32), bqv_full[1].reshape(pairs, LANES)], axis=1
     ).reshape(-1)
@@ -428,8 +545,11 @@
     shift = jnp.concatenate([bqv_full[0] * score_scale, kv_bias])
     scale = jnp.concatenate([jnp.full((width,), score_scale, F32), jnp.ones((2 * width,), F32)])
     qkv = (mm(ln_one, wqkv) * scale + shift).astype(BF16)
+    own, own_lse = attention_own(qkv)
+    dealt_of_pair, own = after(dealt_of_pair, own)
+    ln_of_pair = normalize(dealt_of_pair.astype(F32), small_full[0], small_full[1])[0].astype(BF16)
     kv_of_pair = (mm(ln_of_pair, wkv) + kv_bias).astype(BF16)
-    attended, lse = attention(joined, qkv, kv_of_pair)
+    attended, lse = attention_pair(joined, qkv, kv_of_pair, own, own_lse)
     hidden = resid + mm(attended, wout_t, 1, 1) + small_full[2]
 
     ln_two, normed_two, factor_two = normalize(hidden, small_full[3], small_full[4])
@@ -437,23 +557,30 @@
     pre_act = mm(ln_two, wup) + bup_full
     activated, gelu_pull = jax.vjp(lambda values: jax.nn.gelu(values, approximate=True), pre_act)
     slope = gelu_pull(jnp.ones_like(pre_act))[0].astype(BF16)
-    act = activated.astype(BF16)
+    act, slope = after(activated.astype(BF16), slope)
     output = (hidden + mm(act, wdown_t, 1, 1) + small_full[5]).astype(BF16)
 
     grad_down_t = mm(grad_out, act, 0, 0).astype(BF16)
     grad_pre = (mm(grad_out, wdown_t) * slope.astype(F32)).astype(BF16)
     bias_up_grad = jnp.sum(grad_pre, axis=0, dtype=F32)
     grad_up = mm(ln_two, grad_pre, 0, 0).astype(BF16)
+    grad_down_t, grad_up, grad_pre = after(grad_down_t, grad_up, grad_pre)
     grad_ln_two = mm(grad_pre, wup, 1, 1)
     grad_hidden = grad_out.astype(F32) + norm_back(
         grad_ln_two, normed_two, factor_two, small_full[3]
     )
     grad_branch = grad_hidden.astype(BF16)
     grad_wout_t = mm(grad_branch, attended, 0, 0).astype(BF16)
+    mlp_grads = jnp.concatenate([grad_down_t, grad_up, grad_wout_t], axis=1)
     grad_att = mm(grad_branch, wout_t).astype(BF16)
-
-    pair_dq, pair_dkv = attention_back_pair(joined, qkv, kv_of_pair, grad_att, attended, lse)
-    for_pair = swap(mm(pair_dkv, wkv, 1, 1).astype(BF16))
+    grad_att, mlp_grads, output = after(grad_att, mlp_grads, output)
+    mlp_sum = reduced(mlp_grads)
+
+    pair_dq, pair_dkv = attention_back_pair(
+        joined, qkv, kv_of_pair, grad_att, attended, lse
+    )
+    for_pair = mm(pair_dkv, wkv, 1, 1).astype(BF16)
+    for_pair = swap(for_pair)
     dq, dkv = attention_back_own(qkv, grad_att, attended, lse, pair_dq)
     grad_wq = mm(ln_one, dq, 0, 0).astype(BF16)
     grad_wkv = (mm(ln_one, dkv, 0, 0) + mm(ln_of_pair, pair_dkv, 0, 0)).astype(BF16)
@@ -465,46 +592,52 @@
         grad_hidden + norm_back(grad_ln_one, normed_one, factor_one, small_full[0])
     ).astype(BF16)
 
-    def reduced(values):
-        total = lax.psum_scatter(values, "dp", scatter_dimension=0, tiled=True)
-        return total
-
-    down_sum = reduced(grad_down_t)
-    up_out_sum = reduced(jnp.concatenate([grad_up, grad_wout_t], axis=1))
     qkv_sum = reduced(jnp.concatenate([grad_wq, grad_wkv], axis=1))
 
-    def paired(values):
-        mine, other = mine_of(values, 1)
-        return mine.astype(F32) + swap(other).astype(F32)
-
-    down_part = paired(down_sum).T
-    up_part = paired(up_out_sum[:, : 2 * hidden_half])
-    wout_part = paired(up_out_sum[:, 2 * hidden_half :]).T
-    q_part = paired(qkv_sum[:, :width])
-    kv_part = paired(qkv_sum[:, width:])
+    def paired(values, sizes):
+        columns, start = [], 0
+        for size in sizes:
+            columns.append(mine_of(values[:, start : start + size], 1))
+            start += size
+        mine = jnp.concatenate([c[0] for c in columns], axis=1)
+        other = jnp.concatenate([c[1] for c in columns], axis=1)
+        total = mine.astype(F32) + swap(other).astype(F32)
+        cuts = [sum(sizes[:i]) // 2 for i in range(1, len(sizes))]
+        return jnp.split(total, cuts, axis=1)
+
+    down_part, up_part, wout_part = paired(mlp_sum, (2 * hidden_half, 2 * hidden_half, width))
+    down_part, wout_part = down_part.T, wout_part.T
+    q_part, kv_part = paired(qkv_sum, (width, 2 * width))
     kv_part = kv_part.reshape(piece, pairs // 2, 2, LANES).transpose(0, 2, 1, 3)
     qkv_part = jnp.concatenate(
         [q_part.reshape(piece, 1, half), kv_part.reshape(piece, 2, half)], axis=1
     )
 
-    small_grads = jnp.stack(
+    row_sums = jnp.concatenate(
         [
-            jnp.sum(grad_ln_one * normed_one, axis=0),
-            jnp.sum(grad_ln_one, axis=0),
-            jnp.sum(grad_hidden, axis=0),
-            jnp.sum(grad_ln_two * normed_two, axis=0),
-            jnp.sum(grad_ln_two, axis=0),
-            jnp.sum(grad_out, axis=0, dtype=F32),
-            bias_q_grad,
-            bias_v_grad,
+            jnp.stack([bias_q_grad, bias_v_grad]),
+            bias_up_grad.reshape(-1, width),
+            jnp.zeros((2, width), F32),
+            jnp.stack(
+                [
+                    jnp.sum(grad_ln_one * normed_one, axis=0),
+                    jnp.sum(grad_ln_one, axis=0),
+                    jnp.sum(grad_hidden, axis=0),
+                    jnp.sum(grad_ln_two * normed_two, axis=0),
+                    jnp.sum(grad_ln_two, axis=0),
+                    jnp.sum(grad_out, axis=0, dtype=F32),
+                ]
+            ),
+            jnp.zeros((2, width), F32),
         ]
     )
-    small_total, up_total = lax.psum((small_grads, bias_up_grad), ("dp", "tensor"))
-    small_part = lax.dynamic_slice_in_dim(
-        small_total[:6], lax.axis_index("dp") * piece, piece, 1
-    )
-    qv_part = mine_of(small_total[6:], 1)[0]
-    bias_up_part = mine_of(up_total, 0)[0]
+    row_sums = row_sums.reshape(16, n_dp, piece).transpose(1, 0, 2)
+    row_sums = jnp.pad(row_sums, ((0, 0), (0, 0), (0, LANES - piece)))
+    slice_total, bias_total = sum_small(n_dp, row_sums)
+    small_part = slice_total[8:14, :piece]
+    bias_total = bias_total[:, :6, :piece].transpose(1, 0, 2).reshape(6, width)
+    qv_part = mine_of(bias_total[:2], 1)[0]
+    bias_up_part = mine_of(bias_total[2:].reshape(-1), 0)[0]
 
     sent_out = lax.all_to_all(output, "dp", split_axis=0, concat_axis=0, tiled=True)
     sent_grad = lax.all_to_all(grad_input, "dp", split_axis=0, concat_axis=0, tiled=True)
@@ -547,6 +680,7 @@
         P("tensor", "dp"),
         P("dp"),
     )
+
     return jax.shard_map(
         per_device,
         mesh=mesh,

time: 625 us -> 605 us (0.968)
  blocking collectives: 72.9 us -> 0 us
  waiting for transfers between devices: 148 us -> 208 us
  matrix products: 139 us -> 127 us
    psum x1 -> x0, blocking collectives: 72.9 us -> none  [per_device(): lax.psum((small_grads, bias_up_grad), ('dp', 'tensor'))]
    pallas_call x2 -> x3, Pallas kernels: 28.7 us -> 74.7 us  [the longest x1 45.6 us: sum_small(): pl.pallas_call(functools.partial(sum_small_kernel, n_dp), in_specs=[vmem]...]
    pallas_call x1, Pallas kernels: 51.1 us -> 9.3 us  [share_small(): pl.pallas_call(functools.partial(small_kernel, n_dp), in_specs=[vmem, vme...]
    all_to_all x1, waiting for transfers between devices: 0.01 us -> 40 us  [per_device(): lax.all_to_all(sent_rows, 'dp', split_axis=0, concat_axis=0, tiled=True)]
    ppermute x9 -> x6, waiting for transfers between devices: 48.2 us -> 21.9 us  [swap(): return lax.ppermute(values, 'tensor', [(0, 1), (1, 0)])]
    all_gather x1, waiting for transfers between devices: 13.3 us -> 39.1 us  [per_device(): rest = lax.all_gather(rest_local, 'dp', axis=0, tiled=True)]
    reduce_scatter x3 -> x2, waiting for transfers between devices: 59.2 us -> 77 us  [reduced(): return lax.psum_scatter(values, 'dp', scatter_dimension=0, tiled=True)]
    dot_general x21, matrix products: 139 us -> 127 us  [mm(): lax.dot_general(left, right, (((left_dim,), (right_dim,)), ((), ())), pre...]
  transfers between devices with their start and end apart: 18 -> 14, of which waited for: 11 -> 8; matrix products, arithmetic and copies ran while one was open for 21% -> 16% of each run, Pallas kernels for 13% -> 14%
where the time goes in v2:
time: 605 us; the launch traced here: 598 us
  waiting for transfers between devices  208 us (34%)
  Pallas kernels  128 us (21%)
  matrix products  127 us (21%)
  starting transfers between devices  70.8 us (12%)
  other arithmetic  33.4 us (6%)
  between operations  16.3 us (3%)
  local copies, waits for them, and re-layouts  14.2 us (2%)
    dot_general x21, matrix products, mm(): lax.dot_general(left, right, (((left_dim,), (right_dim,)), ((), ())), pre...  127 us
    reduce_scatter x2, waiting for transfers between devices, reduced(): return lax.psum_scatter(values, 'dp', scatter_dimension=0, tiled=True)  77 us
    pallas_call x1, Pallas kernels, sum_small(): pl.pallas_call(functools.partial(sum_small_kernel, n_dp), in_specs=[vmem]...  45.6 us
    all_to_all x1, waiting for transfers between devices, per_device(): lax.all_to_all(sent_rows, 'dp', split_axis=0, concat_axis=0, tiled=True)  40 us
    all_gather x1, waiting for transfers between devices, per_device(): rest = lax.all_gather(rest_local, 'dp', axis=0, tiled=True)  39.1 us
    pallas_call x1, Pallas kernels, attention_back_own(): pl.pallas_call(functools.partial(own_backward, kblock=min(512, rows)), gr...  35 us
    all_to_all x1, starting transfers between devices, per_device(): lax.all_to_all(output, 'dp', split_axis=0, concat_axis=0, tiled=True)  30.8 us
    all_to_all x1, waiting for transfers between devices, per_device(): lax.all_to_all(output, 'dp', split_axis=0, concat_axis=0, tiled=True)  29.8 us
  transfers between devices with their start and end apart: 14, of which 8 were waited for; matrix products, arithmetic and copies ran while one was open for 16% of the time, Pallas kernels for 14%

profile of v2, /device:TPU:0, one launch (start us, length us, event | category | flops | bytes accessed | tf_op | source)
XLA Modules:
  0.0 597.8 jit_solution(1334894559751872075)
XLA Ops:
  18.8 7.2 %collective-permute-done.2 = bf16[48,3456]{1,0:T(8,128)(2,1)S(1)} collective-permute-done((bf16[48,3456]{1,0:T(8,128)(2,1)S(1)}, bf16[48,3456]{1,0:T(8,128)(2,1)S(1)}, u32[]{:S(2)}, u32[]{:S(2)}) %collective-permute-start.2) | collective-permute-done | bytes 331808 | tf_op jit(solution)/shard_map/ppermute | solution.py:440
  28.5 9.3 %share_small.1 = (f32[16,8,128]{2,1,0:T(8,128)}, f32[24,128]{1,0:T(8,128)}) custom-call(f32[8,128]{1,0:T(8,128)} %pad.13.slice_ref, f32[24,128]{1,0:T(8,128)} %fusion.63.bias_ref), custom_call_target="tpu_custom_call" | custom-call | tf_op jit(solution)/shard_map/share_small/pallas_call | solution.py:317
  50.4 40.0 %all-to-all-done = bf16[16,64,768]{2,1,0:T(8,128)(2,1)S(1)} async-done(((bf16[16,64,768]{2,1,0:T(8,128)(2,1)}), bf16[16,64,768]{2,1,0:T(8,128)(2,1)S(1)}, u32[]{:S(2)}, u32[]{:S(2)}) %all-to-all-start) | async-done | bytes 1572896 | tf_op jit(solution)/shard_map/all_to_all | solution.py:522
  94.9 9.1 %all-to-all-start.1 = ((bf16[16,64,768]{2,1,0:T(8,128)(2,1)}), bf16[16,64,768]{2,1,0:T(8,128)(2,1)S(1)}, u32[]{:S(2)}, u32[]{:S(2)}) async-start(bf16[16,64,768]{2,1,0:T(8,128)(2,1)} %bitcast.93), calls=%async_computation.1 | async-start | bytes 3145728 | tf_op jit(solution)/shard_map/all_to_all | solution.py:525
  106.8 8.4 %add_convert_fusion.q_ref.kv_ref = bf16[1024,2304]{1,0:T(8,128)(2,1)} fusion(bf16[768,2304]{1,0:T(8,128)(2,1)} %all-gather.3.cloned.1.call-done, f32[2304]{0:T(1024)S(1)} %pad_maximum_fusion.8, f32[2304]{0:T(1024)S(1)} %copy-done.39, bf16[1024,768]{1,0:T(8,128)(2,1)S(1)} %bitcast.82, f32[768]{0:T(1024)S(1)} %add.148, f32[768]{0:T(1024)S(1)} %mul.172, ...), kind=kOutput, calls=%fused_computation.13 | convolution fusion | flops 3635675136 | bytes 9863168 | tf_op jit(solution)/shard_map/dot_general | solution.py:34
  115.1 21.4 %attend_own.1 = (f32[1024,768]{1,0:T(8,128)}, f32[1024,768]{1,0:T(8,128)}) custom-call(bf16[1024,2304]{1,0:T(8,128)(2,1)} %add_convert_fusion.q_ref.kv_ref, bf16[1024,2304]{1,0:T(8,128)(2,1)} %add_convert_fusion.q_ref.kv_ref), custom_call_target="tpu_custom_call" | custom-call | flops 12884901888 | bytes 4718592 | tf_op jit(solution)/shard_map/attend_own/pallas_call | solution.py:185
  150.9 7.7 %attend_pair.1 = (bf16[1024,768]{1,0:T(8,128)(2,1)}, f32[1024,768]{1,0:T(8,128)}) custom-call(s32[1]{0:T(128)S(6)} %convert_element_type.123.joined_ref, bf16[1024,2304]{1,0:T(8,128)(2,1)} %add_convert_fusion.q_ref.kv_ref, bf16[1024,1536]{1,0:T(8,128)(2,1)} %add_convert_fusion.1.kv_ref, f32[1024,768]{1,0:T(8,128)} %get-tuple-element.48.own_ref, ...), custom_call_target="tpu_custom_call" | custom-call | flops 12884901888 | bytes 4718592 | tf_op jit(solution)/shard_map/attend_pair/pallas_call | solution.py:202
  158.6 39.1 %all-gather.5.cloned.1.call-done = bf16[768,6912]{1,0:T(8,128)(2,1)} async-done(((bf16[48,6912]{1,0:T(8,128)(2,1)}), bf16[768,6912]{1,0:T(8,128)(2,1)}) %all-gather.5.cloned.1.call-update) | async-done | bytes 10616848 | tf_op jit(solution)/shard_map/all_gather | solution.py:504
  201.6 17.3 %fusion.6 = (bf16[1024,3072]{1,0:T(8,128)(2,1)}, bf16[1024,3072]{1,0:T(8,128)(2,1)}) fusion(f32[3072]{0:T(1024)S(1)} %maximum_select_fusion.4, bf16[768,6912]{1,0:T(8,128)(2,1)} %all-gather.5.cloned.1.call-done, f32[1024,768]{1,0:T(8,128)S(1)} %get-tuple-element.111, f32[768]{0:T(1024)S(1)} %add.162, f32[768]{0:T(1024)S(1)} %mul.187, ...), kind=kOutput, calls=%fused_computation.8 | convolution fusion | flops 4901830656 | bytes 20473856 | tf_op jit(solution)/shard_map/dot_general | solution.py:34
  218.8 8.2 %convolution_convert_fusion.1 = bf16[768,3072]{1,0:T(8,128)(2,1)S(1)} fusion(bf16[1024,768]{1,0:T(8,128)(2,1)S(1)} %bitcast.88, bf16[1024,3072]{1,0:T(8,128)(2,1)} %get-tuple-element.51), kind=kOutput, calls=%fused_computation.18 | convolution fusion | flops 4834197504 | bytes 12582912 | tf_op jit(solution)/shard_map/dot_general | solution.py:34
  227.0 8.7 %convert_reduce_fusion = (f32[3072]{0:T(1024)S(1)}, bf16[1024,3072]{1,0:T(8,128)(2,1)S(1)}) fusion(bf16[1024,3072]{1,0:T(8,128)(2,1)} %get-tuple-element.52, bf16[1024,768]{1,0:T(8,128)(2,1)S(1)} %bitcast.89, bf16[768,6912]{1,0:T(8,128)(2,1)} %all-gather.5.cloned.1.call-done), kind=kOutput, calls=%fused_computation.9 | convolution fusion | flops 4847563776 | bytes 18886656 | tf_op jit(solution)/shard_map/dot_general | solution.py:34
  238.4 6.5 %convolution_convert_fusion = bf16[768,3072]{1,0:T(8,128)(2,1)S(1)} fusion(bf16[1024,3072]{1,0:T(8,128)(2,1)S(1)} %get-tuple-element.53, f32[1024,768]{1,0:T(8,128)S(1)} %copy-done.3, f32[768]{0:T(1024)S(1)} %add.162, f32[768]{0:T(1024)S(1)} %mul.187, f32[1024]{0:T(1024)S(1)} %add_rsqrt_fusion, f32[1024]{0:T(1024)S(1)} %broadcast_multiply_fusion.4), kind=kOutput, calls=%fused_computation.17 | convolution fusion | flops 4838129664 | bytes 14170112 | tf_op jit(solution)/shard_map/dot_general | solution.py:34
  244.9 9.3 %multiply_reduce_fusion = (f32[768]{0:T(1024)S(1)}, f32[1024]{0:T(1024)S(1)}, f32[1024]{0:T(1024)S(1)}, f32[768]{0:T(1024)S(1)}, f32[1024,768]{1,0:T(8,128)S(1)}) fusion(f32[1024,768]{1,0:T(8,128)S(1)} %copy-done.3, f32[1024]{0:T(1024)S(1)} %add_rsqrt_fusion, f32[1024]{0:T(1024)S(1)} %broadcast_multiply_fusion.4, f32[768]{0:T(1024)S(1)} %mul.187, ...), kind=kOutput, calls=%fused_computation.61 | convolution fusion | flops 4838912000 | bytes 17327104 | tf_op jit(solution)/shard_map/dot_general | solution.py:34
  258.8 8.0 %pad_maximum_fusion = bf16[768,6912]{1,0:T(8,128)(2,1)} fusion(bf16[768,768]{1,0:T(8,128)(2,1)S(1)} %convolution_convert_fusion.4, bf16[768,3072]{1,0:T(8,128)(2,1)S(1)} %convolution_convert_fusion, bf16[768,3072]{1,0:T(8,128)(2,1)S(1)} %convolution_convert_fusion.1), kind=kLoop, calls=%fused_computation.12 | loop fusion | flops 31850496 | bytes 21233664 | tf_op jit(solution)/shard_map/concatenate | solution.py:574
  271.7 9.5 %add_convert_fusion.3 = bf16[1024,768]{1,0:T(8,128)(2,1)} fusion(f32[1024,768]{1,0:T(8,128)S(1)} %copy-done.4, bf16[1024,3072]{1,0:T(8,128)(2,1)} %get-tuple-element.51, bf16[768,6912]{1,0:T(8,128)(2,1)} %all-gather.5.cloned.1.call-done, f32[768]{0:T(1024)S(1)} %add.171), kind=kOutput, calls=%fused_computation.64 | convolution fusion | flops 4834197504 | bytes 15731712 | tf_op jit(solution)/shard_map/dot_general | solution.py:34
  281.2 8.6 %attend_back_pair.1 = (f32[768,1024]{1,0:T(8,128)}, bf16[1024,1536]{1,0:T(8,128)(2,1)}) custom-call(s32[1]{0:T(128)S(6)} %convert_element_type.123.joined_ref, bf16[1024,2304]{1,0:T(8,128)(2,1)} %add_convert_fusion.q_ref.kv_ref, bf16[1024,768]{1,0:T(8,128)(2,1)} %convolution_convert_fusion.2.grad_ref, bf16[1024,768]{1,0:T(8,128)(2,1)} %get-tuple-element.50.mixed_ref, ...), custom_call_target="tpu_custom_call" | custom-call | flops 32212254720 | bytes 4718592 | tf_op jit(solution)/shard_map/attend_back_pair/pallas_call | solution.py:223
  289.8 35.0 %attend_back_own.1 = (bf16[1024,768]{1,0:T(8,128)(2,1)}, bf16[1024,1536]{1,0:T(8,128)(2,1)}) custom-call(bf16[1024,2304]{1,0:T(8,128)(2,1)} %add_convert_fusion.q_ref.kv_ref, bf16[1024,768]{1,0:T(8,128)(2,1)} %convolution_convert_fusion.2.grad_ref, bf16[1024,768]{1,0:T(8,128)(2,1)} %get-tuple-element.50.mixed_ref, f32[1024,768]{1,0:T(8,128)} %get-tuple-element.58.lse_ref, ...), custom_call_target="tpu_custom_call" | custom-call | flops 32212254720 | bytes 4718592 | tf_op jit(solution)/shard_map/attend_back_own/pallas_call | solution.py:246
  338.8 6.4 %fusion.51 = bf16[1024,768]{1,0:T(8,128)(2,1)} fusion(bf16[1024,1536]{1,0:T(8,128)(2,1)} %get-tuple-element.62, bf16[768,2304]{1,0:T(8,128)(2,1)} %all-gather.3.cloned.1.call-done), kind=kOutput, calls=%fused_computation.81 | convolution fusion | flops 2416705536 | bytes 7077888 | tf_op jit(solution)/shard_map/dot_general | solution.py:34
  346.7 30.8 %all-to-all-start.2 = ((bf16[16,64,768]{2,1,0:T(8,128)(2,1)}), bf16[16,64,768]{2,1,0:T(8,128)(2,1)}, u32[]{:S(2)}, u32[]{:S(2)}) async-start(bf16[16,64,768]{2,1,0:T(8,128)(2,1)} %bitcast.92), calls=%async_computation.2 | async-start | bytes 3145728 | tf_op jit(solution)/shard_map/all_to_all | solution.py:642
  389.7 29.8 %all-to-all-done.2 = bf16[16,64,768]{2,1,0:T(8,128)(2,1)} async-done(((bf16[16,64,768]{2,1,0:T(8,128)(2,1)}), bf16[16,64,768]{2,1,0:T(8,128)(2,1)}, u32[]{:S(2)}, u32[]{:S(2)}) %all-to-all-start.2) | async-done | bytes 1572896 | tf_op jit(solution)/shard_map/all_to_all | solution.py:642
  419.4 13.3 %all-to-all-start.3 = ((bf16[16,64,768]{2,1,0:T(8,128)(2,1)}), bf16[16,64,768]{2,1,0:T(8,128)(2,1)S(1)}, u32[]{:S(2)}, u32[]{:S(2)}) async-start(bf16[16,64,768]{2,1,0:T(8,128)(2,1)} %bitcast.90), calls=%async_computation.3 | async-start | bytes 3145728 | tf_op jit(solution)/shard_map/all_to_all | solution.py:643
  439.7 45.6 %sum_small.1 = (f32[16,128]{1,0:T(8,128)}, f32[16,8,128]{2,1,0:T(8,128)}) custom-call(f32[16,16,128]{2,1,0:T(8,128)} %pad.15.parts_ref), custom_call_target="tpu_custom_call" | custom-call | tf_op jit(solution)/shard_map/sum_small/pallas_call | solution.py:414
  501.2 77.0 %reduce-scatter.5.cloned.1.call-done = bf16[48,6912]{1,0:T(8,128)(2,1)} async-done(((bf16[768,6912]{1,0:T(8,128)(2,1)}), bf16[48,6912]{1,0:T(8,128)(2,1)}) %reduce-scatter.5.cloned.1.call-update) | async-done | bytes 663568 | tf_op jit(solution)/shard_map/reduce_scatter | solution.py:477
  582.4 7.0 %collective-permute-done.5 = bf16[48,3456]{1,0:T(8,128)(2,1)S(1)} collective-permute-done((bf16[48,3456]{1,0:T(8,128)(2,1)S(1)}, bf16[48,3456]{1,0:T(8,128)(2,1)S(1)}, u32[]{:S(2)}, u32[]{:S(2)}) %collective-permute-start.5) | collective-permute-done | bytes 331808 | tf_op jit(solution)/shard_map/ppermute | solution.py:440
  (218 shorter events, 118.4 us)
Async XLA Ops:
  7.2 30.6 %copy-start = (bf16[1024,768]{1,0:T(8,128)(2,1)S(1)}, bf16[1024,768]{1,0:T(8,128)(2,1)}, u32[]{:S(2)}) copy-start(bf16[1024,768]{1,0:T(8,128)(2,1)} %param.16) | copy-start | bytes 4718596
  7.2 99.5 %all-gather.3.cloned.1.call-start = ((), (), s32[]{:S(2)}) async-start(), calls=%async_computation.6 | async-start | bytes 3760128 | tf_op jit(solution)/shard_map/all_gather | solution.py:503
  7.3 6.3 %collective-permute-start = (bf16[48,3,384]{2,0,1:T(8,128)(2,1)}, bf16[48,3,384]{2,0,1:T(8,128)(2,1)S(1)}, u32[]{:S(2)}, u32[]{:S(2)}) collective-permute-start(bf16[48,3,384]{2,0,1:T(8,128)(2,1)} %param.22), channel_id=1, source_target_pairs={{0,1},{1,0},{2,3},{3,2},{4,5},{5,4},{6,7},{7,6},{8,9},{9,8},{10,11... | collective-permute-start | bytes 331784 | tf_op jit(solution)/shard_map/ppermute | solution.py:440
  15.9 181.8 %all-gather.5.cloned.1.call-start = ((), (), s32[]{:S(2)}) async-start(), calls=%async_computation.7 | async-start | bytes 11280384 | tf_op jit(solution)/shard_map/all_gather | solution.py:504
  17.0 9.0 %collective-permute-start.2 = (bf16[48,3456]{1,0:T(8,128)(2,1)S(1)}, bf16[48,3456]{1,0:T(8,128)(2,1)S(1)}, u32[]{:S(2)}, u32[]{:S(2)}) collective-permute-start(bf16[48,3456]{1,0:T(8,128)(2,1)S(1)} %pad_maximum_fusion.3), channel_id=1, source_target_pairs={{0,1},{1,0},{2,3},{3,2},{4,5},{5,4},{6,7},{7,6},{8,9},{9,8},{10,11... | collective-permute-start | bytes 995336 | tf_op jit(solution)/shard_map/ppermute | solution.py:440
  40.9 49.5 %all-to-all-start = ((bf16[16,64,768]{2,1,0:T(8,128)(2,1)}), bf16[16,64,768]{2,1,0:T(8,128)(2,1)S(1)}, u32[]{:S(2)}, u32[]{:S(2)}) async-start(bf16[16,64,768]{2,1,0:T(8,128)(2,1)} %bitcast.8), calls=%async_computation | async-start | bytes 3145728 | tf_op jit(solution)/shard_map/all_to_all | solution.py:522
  50.1 94.6 %copy-start.18 = (f32[768]{0:T(1024)}, f32[768]{0:T(1024)S(1)}, u32[]{:S(2)}) copy-start(f32[768]{0:T(1024)S(1)} %mul.172) | copy-start | bytes 9220
  50.1 94.6 %copy-start.26 = (f32[768]{0:T(1024)}, f32[768]{0:T(1024)S(1)}, u32[]{:S(2)}) copy-start(f32[768]{0:T(1024)S(1)} %add.148) | copy-start | bytes 9220
  94.9 123.9 %all-to-all-start.1 = ((bf16[16,64,768]{2,1,0:T(8,128)(2,1)}), bf16[16,64,768]{2,1,0:T(8,128)(2,1)S(1)}, u32[]{:S(2)}, u32[]{:S(2)}) async-start(bf16[16,64,768]{2,1,0:T(8,128)(2,1)} %bitcast.93), calls=%async_computation.1 | async-start | bytes 3145728 | tf_op jit(solution)/shard_map/all_to_all | solution.py:525
  104.0 389.9 %reduce-scatter.3.cloned.1.call-start = ((), (), s32[]{:S(2)}) async-start(), calls=%async_computation.8 | async-start | bytes 3760128 | tf_op jit(solution)/shard_map/reduce_scatter | solution.py:477
  104.1 36.9 %collective-permute-start.1 = (bf16[1024,768]{1,0:T(8,128)(2,1)S(1)}, bf16[1024,768]{1,0:T(8,128)(2,1)}, u32[]{:S(2)}, u32[]{:S(2)}) collective-permute-start(bf16[1024,768]{1,0:T(8,128)(2,1)S(1)} %bitcast.79), channel_id=1, source_target_pairs={{0,1},{1,0},{2,3},{3,2},{4,5},{5,4},{6,7},{7,6},{8,9},{9,8},{10,11... | collective-permute-start | bytes 4718600 | tf_op jit(solution)/shard_map/ppermute | solution.py:440
  115.1 29.6 %copy-start.36 = (bf16[768,2304]{1,0:T(8,128)(2,1)S(1)}, bf16[768,2304]{1,0:T(8,128)(2,1)}, u32[]{:S(2)}) copy-start(bf16[768,2304]{1,0:T(8,128)(2,1)} %all-gather.3.cloned.1.call-done) | copy-start | bytes 10616836
  289.8 35.1 %copy-start.16 = (f32[1024]{0:T(1024)S(1)}, f32[1024]{0:T(1024)}, u32[]{:S(2)}) copy-start(f32[1024]{0:T(1024)} %copy-done.15) | copy-start | bytes 12292
  289.8 35.1 %copy-start.19 = (f32[768]{0:T(1024)S(1)}, f32[768]{0:T(1024)}, u32[]{:S(2)}) copy-start(f32[768]{0:T(1024)} %copy-done.18) | copy-start | bytes 9220
  289.8 35.1 %copy-start.21 = (f32[1024]{0:T(1024)S(1)}, f32[1024]{0:T(1024)}, u32[]{:S(2)}) copy-start(f32[1024]{0:T(1024)} %copy-done.20) | copy-start | bytes 12292
  289.8 35.1 %copy-start.27 = (f32[768]{0:T(1024)S(1)}, f32[768]{0:T(1024)}, u32[]{:S(2)}) copy-start(f32[768]{0:T(1024)} %copy-done.26) | copy-start | bytes 9220
  338.2 239.9 %reduce-scatter.5.cloned.1.call-start = ((), (), s32[]{:S(2)}) async-start(), calls=%async_computation.9 | async-start | bytes 11280384 | tf_op jit(solution)/shard_map/reduce_scatter | solution.py:477
  345.2 37.9 %collective-permute-start.3 = (bf16[1024,768]{1,0:T(8,128)(2,1)}, bf16[1024,768]{1,0:T(8,128)(2,1)}, u32[]{:S(2)}, u32[]{:S(2)}) collective-permute-start(bf16[1024,768]{1,0:T(8,128)(2,1)} %fusion.51), channel_id=1, source_target_pairs={{0,1},{1,0},{2,3},{3,2},{4,5},{5,4},{6,7},{7,6},{8,9},{9,8},{10,11... | collective-permute-start | bytes 4718600 | tf_op jit(solution)/shard_map/ppermute | solution.py:440
  346.7 72.8 %all-to-all-start.2 = ((bf16[16,64,768]{2,1,0:T(8,128)(2,1)}), bf16[16,64,768]{2,1,0:T(8,128)(2,1)}, u32[]{:S(2)}, u32[]{:S(2)}) async-start(bf16[16,64,768]{2,1,0:T(8,128)(2,1)} %bitcast.92), calls=%async_computation.2 | async-start | bytes 3145728 | tf_op jit(solution)/shard_map/all_to_all | solution.py:642
  419.4 78.0 %all-to-all-start.3 = ((bf16[16,64,768]{2,1,0:T(8,128)(2,1)}), bf16[16,64,768]{2,1,0:T(8,128)(2,1)S(1)}, u32[]{:S(2)}, u32[]{:S(2)}) async-start(bf16[16,64,768]{2,1,0:T(8,128)(2,1)} %bitcast.90), calls=%async_computation.3 | async-start | bytes 3145728 | tf_op jit(solution)/shard_map/all_to_all | solution.py:643
  435.3 53.8 %copy-start.38 = (s32[1,1024]{1,0:T(1,128)S(1)}, s32[1,1024]{1,0:T(1,128)}, u32[]{:S(2)}) copy-start(s32[1,1024]{1,0:T(1,128)} %param.18) | copy-start | bytes 12292
  495.7 5.2 collective-permute-start.4
  500.9 90.1 %copy-start.1 = (bf16[1024,768]{1,0:T(8,128)(2,1)S(1)}, bf16[1024,768]{1,0:T(8,128)(2,1)}, u32[]{:S(2)}) copy-start(bf16[1024,768]{1,0:T(8,128)(2,1)} %param.16) | copy-start | bytes 4718596
  580.2 9.2 %collective-permute-start.5 = (bf16[48,3456]{1,0:T(8,128)(2,1)S(1)}, bf16[48,3456]{1,0:T(8,128)(2,1)S(1)}, u32[]{:S(2)}, u32[]{:S(2)}) collective-permute-start(bf16[48,3456]{1,0:T(8,128)(2,1)S(1)} %pad_maximum_fusion.4), channel_id=1, source_target_pairs={{0,1},{1,0},{2,3},{3,2},{4,5},{5,4},{6,7},{7,6},{8,9},{9,8},{10,11... | collective-permute-start | bytes 995336 | tf_op jit(solution)/shard_map/ppermute | solution.py:440
  (32 other events, 308.8 us)
Sparse Core Ops, SparseCore 0:
  16.0 70.0 all-gather.2
  88.4 109.2 all-gather.4
  338.4 115.5 reduce-scatter.2
  457.8 120.3 reduce-scatter.4

commit v3 on v2

--- a/solution.py
+++ b/solution.py
@@ -13,6 +13,8 @@
 EPS = 1e-06
 LN2 = 0.6931471805599453
 LOG2E = 1.4426950408889634
+GELU_ONE = 0.7978845608028654
+GELU_THREE = 0.7978845608028654 * 0.044715
 F32 = jnp.float32
 BF16 = jnp.bfloat16
 
@@ -440,6 +442,34 @@
     return lax.ppermute(values, "tensor", [(0, 1), (1, 0)])
 
 
+def tree_sum(n_dp, piece, t, values):
+    me = lax.axis_index("dp")
+    columns = values.shape[1]
+
+    def add(first, second, upper, exchange):
+        mine = jnp.where(upper, second, first)
+        arrived = exchange(jnp.where(upper, first, second))
+        return mine.astype(F32) + arrived.astype(F32)
+
+    def along_dp(total, step):
+        blocks = total.reshape(-1, 2, piece, total.shape[-1])
+        partners = [(i, i ^ step) for i in range(n_dp)]
+        return add(
+            blocks[:, 0],
+            blocks[:, 1],
+            (me // step) % 2 == 1,
+            lambda v: lax.ppermute(v, "dp", partners),
+        ).astype(BF16)
+
+    total = along_dp(values, 1)
+    total = add(total[..., : columns // 2], total[..., columns // 2 :], t == 1, swap).astype(BF16)
+    step = 2
+    while step < n_dp:
+        total = along_dp(total, step)
+        step *= 2
+    return total.reshape(piece, columns // 2).astype(F32)
+
+
 def per_device(
     tokens,
     grad_tokens,
@@ -484,7 +514,8 @@
         )
         return jnp.where(t == 0, low, high), jnp.where(t == 0, high, low)
 
-    qkv_local = join(w_qkv, swap(w_qkv), 2)
+    other_qkv = swap(w_qkv)
+    qkv_local = join(w_qkv, other_qkv, 2)
     kv_local = (
         qkv_local[:, 1:].reshape(piece, 2, pairs, LANES).transpose(0, 2, 1, 3).reshape(piece, -1)
     )
@@ -518,7 +549,6 @@
     row_order = dealing[0]
     picks = (row_order[:, None] == jnp.arange(rows, dtype=jnp.int32)[None, :]).astype(BF16)
     sent_rows = mm(picks, tokens).astype(BF16)
-    sent_rows, small_all = after(sent_rows, small_all)
     dealt = lax.all_to_all(sent_rows, "dp", split_axis=0, concat_axis=0, tiled=True)
     grad_tokens, dealt = after(grad_tokens, dealt)
     sent_grads = mm(picks, grad_tokens).astype(BF16)
@@ -555,26 +585,31 @@
     ln_two, normed_two, factor_two = normalize(hidden, small_full[3], small_full[4])
     ln_two = ln_two.astype(BF16)
     pre_act = mm(ln_two, wup) + bup_full
-    activated, gelu_pull = jax.vjp(lambda values: jax.nn.gelu(values, approximate=True), pre_act)
-    slope = gelu_pull(jnp.ones_like(pre_act))[0].astype(BF16)
-    act, slope = after(activated.astype(BF16), slope)
+    square = pre_act * pre_act
+    bend = jnp.tanh(pre_act * (GELU_ONE + GELU_THREE * square))
+    gate = 0.5 + 0.5 * bend
+    slope = gate + (0.5 * pre_act) * (1.0 - bend * bend) * (GELU_ONE + 3.0 * GELU_THREE * square)
+    act, slope = after((pre_act * gate).astype(BF16), slope.astype(BF16))
     output = (hidden + mm(act, wdown_t, 1, 1) + small_full[5]).astype(BF16)
 
     grad_down_t = mm(grad_out, act, 0, 0).astype(BF16)
     grad_pre = (mm(grad_out, wdown_t) * slope.astype(F32)).astype(BF16)
     bias_up_grad = jnp.sum(grad_pre, axis=0, dtype=F32)
     grad_up = mm(ln_two, grad_pre, 0, 0).astype(BF16)
-    grad_down_t, grad_up, grad_pre = after(grad_down_t, grad_up, grad_pre)
+    mlp_grads = jnp.concatenate([grad_down_t, grad_up], axis=1)
+    mlp_grads, grad_pre = after(mlp_grads, grad_pre)
+    mlp_sum = reduced(mlp_grads)
     grad_ln_two = mm(grad_pre, wup, 1, 1)
+    gain_two_grad = jnp.sum(grad_ln_two * normed_two, axis=0)
+    bias_two_grad = jnp.sum(grad_ln_two, axis=0)
     grad_hidden = grad_out.astype(F32) + norm_back(
         grad_ln_two, normed_two, factor_two, small_full[3]
     )
     grad_branch = grad_hidden.astype(BF16)
     grad_wout_t = mm(grad_branch, attended, 0, 0).astype(BF16)
-    mlp_grads = jnp.concatenate([grad_down_t, grad_up, grad_wout_t], axis=1)
+    wout_sum = reduced(grad_wout_t)
     grad_att = mm(grad_branch, wout_t).astype(BF16)
-    grad_att, mlp_grads, output = after(grad_att, mlp_grads, output)
-    mlp_sum = reduced(mlp_grads)
+    grad_att, output = after(grad_att, output)
 
     pair_dq, pair_dkv = attention_back_pair(
         joined, qkv, kv_of_pair, grad_att, attended, lse
@@ -592,7 +627,11 @@
         grad_hidden + norm_back(grad_ln_one, normed_one, factor_one, small_full[0])
     ).astype(BF16)
 
-    qkv_sum = reduced(jnp.concatenate([grad_wq, grad_wkv], axis=1))
+    grad_wqkv = jnp.concatenate(
+        [grad_wq[:, :half], grad_wkv[:, : 2 * half], grad_wq[:, half:], grad_wkv[:, 2 * half :]],
+        axis=1,
+    )
+    qkv_part = tree_sum(n_dp, piece, t, grad_wqkv)
 
     def paired(values, sizes):
         columns, start = [], 0
@@ -605,9 +644,10 @@
         cuts = [sum(sizes[:i]) // 2 for i in range(1, len(sizes))]
         return jnp.split(total, cuts, axis=1)
 
-    down_part, up_part, wout_part = paired(mlp_sum, (2 * hidden_half, 2 * hidden_half, width))
-    down_part, wout_part = down_part.T, wout_part.T
-    q_part, kv_part = paired(qkv_sum, (width, 2 * width))
+    down_part, up_part = paired(mlp_sum, (2 * hidden_half, 2 * hidden_half))
+    wout_part = paired(wout_sum, (width,))[0].T
+    down_part = down_part.T
+    q_part, kv_part = qkv_part[:, :half], qkv_part[:, half:]
     kv_part = kv_part.reshape(piece, pairs // 2, 2, LANES).transpose(0, 2, 1, 3)
     qkv_part = jnp.concatenate(
         [q_part.reshape(piece, 1, half), kv_part.reshape(piece, 2, half)], axis=1
@@ -623,8 +663,8 @@
                     jnp.sum(grad_ln_one * normed_one, axis=0),
                     jnp.sum(grad_ln_one, axis=0),
                     jnp.sum(grad_hidden, axis=0),
-                    jnp.sum(grad_ln_two * normed_two, axis=0),
-                    jnp.sum(grad_ln_two, axis=0),
+                    gain_two_grad,
+                    bias_two_grad,
                     jnp.sum(grad_out, axis=0, dtype=F32),
                 ]
             ),
@@ -634,6 +674,7 @@
     row_sums = row_sums.reshape(16, n_dp, piece).transpose(1, 0, 2)
     row_sums = jnp.pad(row_sums, ((0, 0), (0, 0), (0, LANES - piece)))
     slice_total, bias_total = sum_small(n_dp, row_sums)
+    grad_input, slice_total = after(grad_input, slice_total)
     small_part = slice_total[8:14, :piece]
     bias_total = bias_total[:, :6, :piece].transpose(1, 0, 2).reshape(6, width)
     qv_part = mine_of(bias_total[:2], 1)[0]

time: 605 us -> 599 us (0.990)
  waiting for transfers between devices: 208 us -> 74.8 us
  blocking collectives: 0 us -> 56.3 us
  Pallas kernels: 128 us -> 162 us
  local copies, waits for them, and re-layouts: 14.2 us -> 43.2 us
  other arithmetic: 33.4 us -> 43.4 us
    reduce_scatter x2, waiting for transfers between devices: 77 us -> 0.01 us  [reduced(): return lax.psum_scatter(values, 'dp', scatter_dimension=0, tiled=True)]
    all_to_all x0 -> x1, blocking collectives: none -> 56.3 us  [per_device(): lax.all_to_all(sent_rows, 'dp', split_axis=0, concat_axis=0, tiled=True)]
    pallas_call x1, Pallas kernels: 9.3 us -> 57.5 us  [share_small(): pl.pallas_call(functools.partial(small_kernel, n_dp), in_specs=[vmem, vme...]
    ppermute x0 -> x4, waiting for transfers between devices: none -> 42.6 us  [along_dp(): lax.ppermute(v, 'dp', partners)]
    all_to_all x1 -> x0, waiting for transfers between devices: 40 us -> none  [per_device(): lax.all_to_all(sent_rows, 'dp', split_axis=0, concat_axis=0, tiled=True)]
    all_gather x1, waiting for transfers between devices: 39.1 us -> 0.01 us  [per_device(): rest = lax.all_gather(rest_local, 'dp', axis=0, tiled=True)]
    ppermute x0 -> x4, starting transfers between devices: none -> 32.1 us  [along_dp(): lax.ppermute(v, 'dp', partners)]
    all_to_all x1, waiting for transfers between devices: 29.8 us -> 0.01 us  [per_device(): lax.all_to_all(output, 'dp', split_axis=0, concat_axis=0, tiled=True)]
  transfers between devices with their start and end apart: 14 -> 18, of which waited for: 8 -> 7; matrix products, arithmetic and copies ran while one was open for 16% -> 19% of each run, Pallas kernels for 14% -> 27%
where the time goes in v3:
time: 599 us; the launch traced here: 593 us
  Pallas kernels  162 us (27%)
  matrix products  123 us (21%)
  waiting for transfers between devices  74.8 us (12%)
  starting transfers between devices  74.1 us (12%)
  blocking collectives  56.3 us (9%)
  other arithmetic  43.4 us (7%)
  local copies, waits for them, and re-layouts  43.2 us (7%)
  between operations  16.6 us (3%)
    dot_general x21, matrix products, mm(): lax.dot_general(left, right, (((left_dim,), (right_dim,)), ((), ())), pre...  123 us
    pallas_call x1, Pallas kernels, share_small(): pl.pallas_call(functools.partial(small_kernel, n_dp), in_specs=[vmem, vme...  57.5 us
    all_to_all x1, blocking collectives, per_device(): lax.all_to_all(sent_rows, 'dp', split_axis=0, concat_axis=0, tiled=True)  56.3 us
    ppermute x4, waiting for transfers between devices, along_dp(): lax.ppermute(v, 'dp', partners)  42.6 us
    pallas_call x1, Pallas kernels, attention_back_own(): pl.pallas_call(functools.partial(own_backward, kblock=min(512, rows)), gr...  35.2 us
    ppermute x4, starting transfers between devices, along_dp(): lax.ppermute(v, 'dp', partners)  32.1 us
    pallas_call x1, Pallas kernels, sum_small(): pl.pallas_call(functools.partial(sum_small_kernel, n_dp), in_specs=[vmem]...  31.6 us
    ppermute x7, waiting for transfers between devices, swap(): return lax.ppermute(values, 'tensor', [(0, 1), (1, 0)])  31.4 us
  transfers between devices with their start and end apart: 18, of which 7 were waited for; matrix products, arithmetic and copies ran while one was open for 19% of the time, Pallas kernels for 27%

profile of v3, /device:TPU:0, one launch (start us, length us, event | category | flops | bytes accessed | tf_op | source)
XLA Modules:
  0.0 592.7 jit_solution(5279198247146374578)
XLA Ops:
  18.7 7.2 %collective-permute-done.2 = bf16[48,3456]{1,0:T(8,128)(2,1)S(1)} collective-permute-done((bf16[48,3456]{1,0:T(8,128)(2,1)S(1)}, bf16[48,3456]{1,0:T(8,128)(2,1)S(1)}, u32[]{:S(2)}, u32[]{:S(2)}) %collective-permute-start.2) | collective-permute-done | bytes 331808 | tf_op jit(solution)/shard_map/ppermute | solution.py:442
  29.1 56.3 %all_to_all.48 = bf16[16,64,768]{2,1,0:T(8,128)(2,1)} all-to-all(bf16[16,64,768]{2,1,0:T(8,128)(2,1)S(1)} %bitcast.163), channel_id=1, replica_groups=mesh['dp'=16,'tensor'=2] {'dp'}, dimensions={0} | all-to-all | bytes 3145728 | tf_op jit(solution)/shard_map/all_to_all | solution.py:552
  88.6 6.2 %all-to-all-start.1 = ((bf16[16,64,768]{2,1,0:T(8,128)(2,1)}), bf16[16,64,768]{2,1,0:T(8,128)(2,1)S(1)}, u32[]{:S(2)}, u32[]{:S(2)}) async-start(bf16[16,64,768]{2,1,0:T(8,128)(2,1)} %bitcast.3), calls=%async_computation.1 | async-start | bytes 3145728 | tf_op jit(solution)/shard_map/all_to_all | solution.py:555
  98.8 57.5 %share_small.1 = (f32[16,8,128]{2,1,0:T(8,128)}, f32[24,128]{1,0:T(8,128)}) custom-call(f32[8,128]{1,0:T(8,128)} %pad.13.slice_ref, f32[24,128]{1,0:T(8,128)} %fusion.67.bias_ref), custom_call_target="tpu_custom_call" | custom-call | tf_op jit(solution)/shard_map/share_small/pallas_call | solution.py:319
  166.1 7.8 %add_convert_fusion.1.q_ref.kv_ref = bf16[1024,2304]{1,0:T(8,128)(2,1)} fusion(bf16[768,2304]{1,0:T(8,128)(2,1)} %all-gather.3.cloned.1.call-done, f32[2304]{0:T(1024)S(1)} %pad_maximum_fusion.7, f32[2304]{0:T(1024)S(1)} %copy-done.50, bf16[1024,768]{0,1:T(8,128)(2,1)S(1)} %copy.78, f32[768]{0:T(1024)S(1)} %add.185, f32[768]{0:T(1024)S(1)} %mul.170, ...), kind=kOutput, calls=%fused_computation.8 | convolution fusion | flops 3635675136 | bytes 9863168 | tf_op jit(solution)/shard_map/dot_general | solution.py:36
  174.0 21.4 %attend_own.1 = (f32[1024,768]{1,0:T(8,128)}, f32[1024,768]{1,0:T(8,128)}) custom-call(bf16[1024,2304]{1,0:T(8,128)(2,1)} %add_convert_fusion.1.q_ref.kv_ref, bf16[1024,2304]{1,0:T(8,128)(2,1)} %add_convert_fusion.1.q_ref.kv_ref), custom_call_target="tpu_custom_call" | custom-call | flops 12884901888 | bytes 4718592 | tf_op jit(solution)/shard_map/attend_own/pallas_call | solution.py:187
  201.8 6.1 %add_convert_fusion.2.kv_ref = bf16[1024,1536]{1,0:T(8,128)(2,1)} fusion(f32[1536]{0:T(1024)S(1)} %reshape.295, bf16[768,2304]{1,0:T(8,128)(2,1)S(1)} %copy-done.46, bf16[1024,768]{0,1:T(8,128)(2,1)} %collective-permute-done.1, f32[1024]{0:T(1024)S(1)} %add_rsqrt_fusion.1, f32[1024]{0:T(1024)S(1)} %broadcast_multiply_fusion.5, f32[768]{0:T(1024)S(1)} %add.185, ...), kind=kOutput, calls=%fused_computation.11 | convolution fusion | flops 2423783424 | bytes 7102464 | tf_op jit(solution)/shard_map/dot_general | solution.py:36
  207.8 7.6 %attend_pair.1 = (bf16[1024,768]{1,0:T(8,128)(2,1)}, f32[1024,768]{1,0:T(8,128)}) custom-call(s32[1]{0:T(128)S(6)} %convert_element_type.194.joined_ref, bf16[1024,2304]{1,0:T(8,128)(2,1)} %add_convert_fusion.1.q_ref.kv_ref, bf16[1024,1536]{1,0:T(8,128)(2,1)} %add_convert_fusion.2.kv_ref, f32[1024,768]{1,0:T(8,128)} %get-tuple-element.44.own_ref, ...), custom_call_target="tpu_custom_call" | custom-call | flops 12884901888 | bytes 4718592 | tf_op jit(solution)/shard_map/attend_pair/pallas_call | solution.py:204
  220.8 13.8 %add_convert_fusion = (bf16[1024,3072]{1,0:T(8,128)(2,1)S(1)}, bf16[1024,3072]{1,0:T(8,128)(2,1)}) fusion(f32[3072]{0:T(1024)S(1)} %maximum_select_fusion.4, bf16[768,6912]{1,0:T(8,128)(2,1)S(1)} %copy-done.45, f32[1024,768]{0,1:T(8,128)S(1)} %get-tuple-element.104, f32[768]{0:T(1024)S(1)} %add.199, f32[768]{0:T(1024)S(1)} %mul.185, ...), kind=kOutput, calls=%fused_computation.2 | convolution fusion | flops 4892393472 | bytes 20475904 | tf_op jit(solution)/shard_map/dot_general | solution.py:36
  234.6 7.3 %convert_reduce_fusion = (f32[3072]{0:T(1024)S(1)}, bf16[1024,3072]{1,0:T(8,128)(2,1)}) fusion(bf16[1024,3072]{1,0:T(8,128)(2,1)S(1)} %get-tuple-element.48, bf16[1024,768]{1,0:T(8,128)(2,1)S(1)} %bitcast.155, bf16[768,6912]{1,0:T(8,128)(2,1)S(1)} %copy-done.45), kind=kOutput, calls=%fused_computation | convolution fusion | flops 4847563776 | bytes 18886656 | tf_op jit(solution)/shard_map/dot_general | solution.py:36
  242.6 7.8 %convolution_convert_fusion.1 = bf16[768,3072]{1,0:T(8,128)(2,1)S(1)} fusion(bf16[1024,768]{1,0:T(8,128)(2,1)} %bitcast.154, bf16[1024,3072]{1,0:T(8,128)(2,1)} %get-tuple-element.47), kind=kOutput, calls=%fused_computation.13 | convolution fusion | flops 4834197504 | bytes 12582912 | tf_op jit(solution)/shard_map/dot_general | solution.py:36
  250.4 5.6 convolution_convert_fusion
  260.1 9.7 %fusion.81 = (f32[768]{0:T(1024)S(1)}, f32[1024,768]{1,0:T(8,128)}) fusion(bf16[1024,3072]{1,0:T(8,128)(2,1)} %get-tuple-element.49, bf16[768,6912]{1,0:T(8,128)(2,1)} %all-gather.5.cloned.1.call-done), kind=kOutput, calls=%fused_computation.178 | convolution fusion | flops 4832623616 | bytes 14158848 | tf_op jit(solution)/shard_map/dot_general | solution.py:36
  292.5 9.5 %add_convert_fusion.4 = bf16[1024,768]{0,1:T(8,128)(2,1)} fusion(f32[1024,768]{0,1:T(8,128)S(1)} %get-tuple-element.104, bf16[1024,3072]{1,0:T(8,128)(2,1)} %get-tuple-element.47, bf16[768,6912]{1,0:T(8,128)(2,1)} %all-gather.5.cloned.1.call-done, f32[768]{0:T(1024)S(1)} %add.210), kind=kOutput, calls=%fused_computation.61 | convolution fusion | flops 4834197504 | bytes 15731712 | tf_op jit(solution)/shard_map/dot_general | solution.py:36
  305.3 20.4 %all-to-all-start.2 = ((bf16[16,64,768]{2,1,0:T(8,128)(2,1)}), bf16[16,64,768]{2,1,0:T(8,128)(2,1)}, u32[]{:S(2)}, u32[]{:S(2)}) async-start(bf16[16,64,768]{2,1,0:T(8,128)(2,1)} %bitcast.18), calls=%async_computation.2 | async-start | bytes 3145728 | tf_op jit(solution)/shard_map/all_to_all | solution.py:683
  326.5 8.3 %attend_back_pair.1 = (f32[768,1024]{1,0:T(8,128)}, bf16[1024,1536]{1,0:T(8,128)(2,1)}) custom-call(s32[1]{0:T(128)S(6)} %convert_element_type.194.joined_ref, bf16[1024,2304]{1,0:T(8,128)(2,1)} %add_convert_fusion.1.q_ref.kv_ref, bf16[1024,768]{1,0:T(8,128)(2,1)} %convolution_convert_fusion.2.grad_ref, bf16[1024,768]{1,0:T(8,128)(2,1)} %get-tuple-element.46.mixed_ref, ...), custom_call_target="tpu_custom_call" | custom-call | flops 32212254720 | bytes 4718592 | tf_op jit(solution)/shard_map/attend_back_pair/pallas_call | solution.py:225
  334.9 35.2 %attend_back_own.1 = (bf16[1024,768]{1,0:T(8,128)(2,1)}, bf16[1024,1536]{1,0:T(8,128)(2,1)}) custom-call(bf16[1024,2304]{1,0:T(8,128)(2,1)} %add_convert_fusion.1.q_ref.kv_ref, bf16[1024,768]{1,0:T(8,128)(2,1)} %convolution_convert_fusion.2.grad_ref, bf16[1024,768]{1,0:T(8,128)(2,1)} %get-tuple-element.46.mixed_ref, f32[1024,768]{1,0:T(8,128)} %get-tuple-element.52.lse_ref, ...), custom_call_target="tpu_custom_call" | custom-call | flops 32212254720 | bytes 4718592 | tf_op jit(solution)/shard_map/attend_back_own/pallas_call | solution.py:248
  377.8 6.6 %fusion.43 = bf16[1024,768]{0,1:T(8,128)(2,1)} fusion(bf16[1024,1536]{1,0:T(8,128)(2,1)} %get-tuple-element.56, bf16[768,2304]{1,0:T(8,128)(2,1)} %all-gather.3.cloned.1.call-done), kind=kOutput, calls=%fused_computation.82 | convolution fusion | flops 2416705536 | bytes 7077888 | tf_op jit(solution)/shard_map/dot_general | solution.py:36
  405.2 27.8 %collective-permute-start.4 = (bf16[8,48,2304]{2,1,0:T(8,128)(2,1)}, bf16[8,48,2304]{2,1,0:T(8,128)(2,1)}, u32[]{:S(2)}, u32[]{:S(2)}) collective-permute-start(bf16[8,48,2304]{2,1,0:T(8,128)(2,1)} %select_bitcast_fusion), channel_id=1, source_target_pairs={{0,2},{2,0},{4,6},{6,4},{8,10},{10,8},{12,14},{14,12},{16,18},{18,... | collective-permute-start | bytes 5308424 | tf_op jit(solution)/shard_map/ppermute | solution.py:461
  437.5 6.0 %fusion.27 = (f32[768]{0:T(1024)}, f32[1024]{0:T(1024)}, f32[1024]{0:T(1024)}, f32[768]{0:T(1024)S(1)}, f32[1024,768]{0,1:T(8,128)}) fusion(bf16[1024,768]{0,1:T(8,128)(2,1)S(1)} %copy-done.4, f32[1024]{0:T(1024)S(1)} %copy-done.30, f32[1024]{0:T(1024)S(1)} %copy-done.22, f32[768]{0:T(1024)S(1)} %copy-done.26, ...), kind=kOutput, calls=%fused_computation.50 | convolution fusion | flops 1218179584 | bytes 12215296 | tf_op jit(solution)/shard_map/dot_general | solution.py:36
  450.1 31.6 %sum_small.1 = (f32[16,128]{1,0:T(8,128)}, f32[16,8,128]{2,1,0:T(8,128)}) custom-call(f32[16,16,128]{2,1,0:T(8,128)} %pad.15.parts_ref), custom_call_target="tpu_custom_call" | custom-call | tf_op jit(solution)/shard_map/sum_small/pallas_call | solution.py:416
  496.2 14.2 %collective-permute-done.5 = bf16[8,48,1152]{2,1,0:T(8,128)(2,1)} collective-permute-done((bf16[8,48,1152]{2,1,0:T(8,128)(2,1)}, bf16[8,48,1152]{2,1,0:T(8,128)(2,1)}, u32[]{:S(2)}, u32[]{:S(2)}) %collective-permute-start.5) | collective-permute-done | bytes 884768 | tf_op jit(solution)/shard_map/ppermute | solution.py:442
  515.1 8.1 %collective-permute-done.6 = bf16[4,48,1152]{2,1,0:T(8,128)(2,1)S(1)} collective-permute-done((bf16[4,48,1152]{2,1,0:T(8,128)(2,1)S(1)}, bf16[4,48,1152]{2,1,0:T(8,128)(2,1)S(1)}, u32[]{:S(2)}, u32[]{:S(2)}) %collective-permute-start.6) | collective-permute-done | bytes 442400 | tf_op jit(solution)/shard_map/ppermute | solution.py:461
  537.6 34.5 %collective-permute-done.8 = bf16[1,48,1152]{2,1,0:T(8,128)(2,1)S(1)} collective-permute-done((bf16[1,48,1152]{2,1,0:T(8,128)(2,1)S(1)}, bf16[1,48,1152]{2,1,0:T(8,128)(2,1)S(1)}, u32[]{:S(2)}, u32[]{:S(2)}) %collective-permute-start.8) | collective-permute-done | bytes 110624 | tf_op jit(solution)/shard_map/ppermute | solution.py:461
  (265 shorter events, 159.6 us)
Async XLA Ops:
  7.2 158.9 %all-gather.3.cloned.1.call-start = ((), (), s32[]{:S(2)}) async-start(), calls=%async_computation.6 | async-start | bytes 3760128 | tf_op jit(solution)/shard_map/all_gather | solution.py:534
  7.3 6.3 %collective-permute-start = (bf16[48,3,384]{2,0,1:T(8,128)(2,1)}, bf16[48,3,384]{2,0,1:T(8,128)(2,1)S(1)}, u32[]{:S(2)}, u32[]{:S(2)}) collective-permute-start(bf16[48,3,384]{2,0,1:T(8,128)(2,1)} %param.22), channel_id=1, source_target_pairs={{0,1},{1,0},{2,3},{3,2},{4,5},{5,4},{6,7},{7,6},{8,9},{9,8},{10,11... | collective-permute-start | bytes 331784 | tf_op jit(solution)/shard_map/ppermute | solution.py:442
  15.8 199.6 %all-gather.5.cloned.1.call-start = ((), (), s32[]{:S(2)}) async-start(), calls=%async_computation.7 | async-start | bytes 11280384 | tf_op jit(solution)/shard_map/all_gather | solution.py:535
  16.9 9.0 %collective-permute-start.2 = (bf16[48,3456]{1,0:T(8,128)(2,1)S(1)}, bf16[48,3456]{1,0:T(8,128)(2,1)S(1)}, u32[]{:S(2)}, u32[]{:S(2)}) collective-permute-start(bf16[48,3456]{1,0:T(8,128)(2,1)S(1)} %pad_maximum_fusion.3), channel_id=1, source_target_pairs={{0,1},{1,0},{2,3},{3,2},{4,5},{5,4},{6,7},{7,6},{8,9},{9,8},{10,11... | collective-permute-start | bytes 995336 | tf_op jit(solution)/shard_map/ppermute | solution.py:442
  29.1 56.3 %copy-start.47 = (bf16[1024,768]{1,0:T(8,128)(2,1)S(1)}, bf16[1024,768]{1,0:T(8,128)(2,1)}, u32[]{:S(2)}) copy-start(bf16[1024,768]{1,0:T(8,128)(2,1)} %param.17) | copy-start | bytes 4718596
  88.6 74.7 %all-to-all-start.1 = ((bf16[16,64,768]{2,1,0:T(8,128)(2,1)}), bf16[16,64,768]{2,1,0:T(8,128)(2,1)S(1)}, u32[]{:S(2)}, u32[]{:S(2)}) async-start(bf16[16,64,768]{2,1,0:T(8,128)(2,1)} %bitcast.3), calls=%async_computation.1 | async-start | bytes 3145728 | tf_op jit(solution)/shard_map/all_to_all | solution.py:555
  157.5 44.3 %copy-start.25 = (f32[768]{0:T(1024)}, f32[768]{0:T(1024)S(1)}, u32[]{:S(2)}) copy-start(f32[768]{0:T(1024)S(1)} %mul.170) | copy-start | bytes 9220
  157.5 44.2 %copy-start.35 = (f32[768]{0:T(1024)}, f32[768]{0:T(1024)S(1)}, u32[]{:S(2)}) copy-start(f32[768]{0:T(1024)S(1)} %add.185) | copy-start | bytes 9220
  161.0 37.1 %collective-permute-start.1 = (bf16[1024,768]{0,1:T(8,128)(2,1)S(1)}, bf16[1024,768]{0,1:T(8,128)(2,1)}, u32[]{:S(2)}, u32[]{:S(2)}) collective-permute-start(bf16[1024,768]{0,1:T(8,128)(2,1)S(1)} %copy.78), channel_id=1, source_target_pairs={{0,1},{1,0},{2,3},{3,2},{4,5},{5,4},{6,7},{7,6},{8,9},{9,8},{10,11... | collective-permute-start | bytes 4718600 | tf_op jit(solution)/shard_map/ppermute | solution.py:442
  305.3 220.3 %all-to-all-start.2 = ((bf16[16,64,768]{2,1,0:T(8,128)(2,1)}), bf16[16,64,768]{2,1,0:T(8,128)(2,1)}, u32[]{:S(2)}, u32[]{:S(2)}) async-start(bf16[16,64,768]{2,1,0:T(8,128)(2,1)} %bitcast.18), calls=%async_computation.2 | async-start | bytes 3145728 | tf_op jit(solution)/shard_map/all_to_all | solution.py:683
  325.7 187.4 %reduce-scatter.3.cloned.1.call-start = ((), (), s32[]{:S(2)}) async-start(), calls=%async_computation.8 | async-start | bytes 1253376 | tf_op jit(solution)/shard_map/reduce_scatter | solution.py:507
  326.5 246.6 %reduce-scatter.5.cloned.1.call-start = ((), (), s32[]{:S(2)}) async-start(), calls=%async_computation.9 | async-start | bytes 10027008 | tf_op jit(solution)/shard_map/reduce_scatter | solution.py:507
  334.9 35.2 %copy-start.26 = (f32[768]{0:T(1024)S(1)}, f32[768]{0:T(1024)}, u32[]{:S(2)}) copy-start(f32[768]{0:T(1024)} %copy-done.25) | copy-start | bytes 9220
  334.9 35.2 %copy-start.29 = (f32[1024]{0:T(1024)S(1)}, f32[1024]{0:T(1024)}, u32[]{:S(2)}) copy-start(f32[1024]{0:T(1024)} %copy-done.28) | copy-start | bytes 12292
  334.9 35.2 %copy-start.36 = (f32[768]{0:T(1024)S(1)}, f32[768]{0:T(1024)}, u32[]{:S(2)}) copy-start(f32[768]{0:T(1024)} %copy-done.35) | copy-start | bytes 9220
  384.4 53.0 %collective-permute-start.3 = (bf16[1024,768]{0,1:T(8,128)(2,1)}, bf16[1024,768]{0,1:T(8,128)(2,1)}, u32[]{:S(2)}, u32[]{:S(2)}) collective-permute-start(bf16[1024,768]{0,1:T(8,128)(2,1)} %fusion.43), channel_id=1, source_target_pairs={{0,1},{1,0},{2,3},{3,2},{4,5},{5,4},{6,7},{7,6},{8,9},{9,8},{10,11... | collective-permute-start | bytes 4718600 | tf_op jit(solution)/shard_map/ppermute | solution.py:442
  405.2 78.7 %collective-permute-start.4 = (bf16[8,48,2304]{2,1,0:T(8,128)(2,1)}, bf16[8,48,2304]{2,1,0:T(8,128)(2,1)}, u32[]{:S(2)}, u32[]{:S(2)}) collective-permute-start(bf16[8,48,2304]{2,1,0:T(8,128)(2,1)} %select_bitcast_fusion), channel_id=1, source_target_pairs={{0,2},{2,0},{4,6},{6,4},{8,10},{10,8},{12,14},{14,12},{16,18},{18,... | collective-permute-start | bytes 5308424 | tf_op jit(solution)/shard_map/ppermute | solution.py:461
  488.5 21.9 %collective-permute-start.5 = (bf16[8,48,1152]{2,1,0:T(8,128)(2,1)}, bf16[8,48,1152]{2,1,0:T(8,128)(2,1)}, u32[]{:S(2)}, u32[]{:S(2)}) collective-permute-start(bf16[8,48,1152]{2,1,0:T(8,128)(2,1)} %broadcast_select_fusion), channel_id=1, source_target_pairs={{0,1},{1,0},{2,3},{3,2},{4,5},{5,4},{6,7},{7,6},{8,9},{9,8},{10,11... | collective-permute-start | bytes 2654216 | tf_op jit(solution)/shard_map/ppermute | solution.py:442
  511.9 11.3 %collective-permute-start.6 = (bf16[4,48,1152]{2,1,0:T(8,128)(2,1)S(1)}, bf16[4,48,1152]{2,1,0:T(8,128)(2,1)S(1)}, u32[]{:S(2)}, u32[]{:S(2)}) collective-permute-start(bf16[4,48,1152]{2,1,0:T(8,128)(2,1)S(1)} %fusion.58), channel_id=1, source_target_pairs={{0,4},{2,6},{4,0},{6,2},{8,12},{10,14},{12,8},{14,10},{16,20},{18,... | collective-permute-start | bytes 1327112 | tf_op jit(solution)/shard_map/ppermute | solution.py:461
  514.0 10.2 %collective-permute-start.9 = (bf16[48,384]{1,0:T(8,128)(2,1)S(1)}, bf16[48,384]{1,0:T(8,128)(2,1)S(1)}, u32[]{:S(2)}, u32[]{:S(2)}) collective-permute-start(bf16[48,384]{1,0:T(8,128)(2,1)S(1)} %broadcast_select_fusion.5), channel_id=1, source_target_pairs={{0,1},{1,0},{2,3},{3,2},{4,5},{5,4},{6,7},{7,6},{8,9},{9,8},{10,11... | collective-permute-start | bytes 110600 | tf_op jit(solution)/shard_map/ppermute | solution.py:442
  523.4 6.2 %collective-permute-start.7 = (bf16[2,48,1152]{2,1,0:T(8,128)(2,1)S(1)}, bf16[2,48,1152]{2,1,0:T(8,128)(2,1)S(1)}, u32[]{:S(2)}, u32[]{:S(2)}) collective-permute-start(bf16[2,48,1152]{2,1,0:T(8,128)(2,1)S(1)} %fusion.61), channel_id=1, source_target_pairs={{0,8},{2,10},{4,12},{6,14},{8,0},{10,2},{12,4},{14,6},{16,24},{18,... | collective-permute-start | bytes 663560 | tf_op jit(solution)/shard_map/ppermute | solution.py:461
  525.6 50.7 %all-to-all-start.3 = ((bf16[16,64,768]{2,1,0:T(8,128)(2,1)}), bf16[16,64,768]{2,1,0:T(8,128)(2,1)S(1)}, u32[]{:S(2)}, u32[]{:S(2)}) async-start(bf16[16,64,768]{2,1,0:T(8,128)(2,1)} %bitcast.159), calls=%async_computation.3 | async-start | bytes 3145728 | tf_op jit(solution)/shard_map/all_to_all | solution.py:684
  529.7 42.3 %collective-permute-start.8 = (bf16[1,48,1152]{2,1,0:T(8,128)(2,1)S(1)}, bf16[1,48,1152]{2,1,0:T(8,128)(2,1)S(1)}, u32[]{:S(2)}, u32[]{:S(2)}) collective-permute-start(bf16[1,48,1152]{2,1,0:T(8,128)(2,1)S(1)} %select_bitcast_fusion.1), channel_id=1, source_target_pairs={{0,16},{2,18},{4,20},{6,22},{8,24},{10,26},{12,28},{14,30},{16,0},... | collective-permute-start | bytes 331784 | tf_op jit(solution)/shard_map/ppermute | solution.py:461
  575.0 8.8 %collective-permute-start.10 = (bf16[48,3072]{1,0:T(8,128)(2,1)}, bf16[48,3072]{1,0:T(8,128)(2,1)}, u32[]{:S(2)}, u32[]{:S(2)}) collective-permute-start(bf16[48,3072]{1,0:T(8,128)(2,1)} %pad_maximum_fusion.4), channel_id=1, source_target_pairs={{0,1},{1,0},{2,3},{3,2},{4,5},{5,4},{6,7},{7,6},{8,9},{9,8},{10,11... | collective-permute-start | bytes 884744 | tf_op jit(solution)/shard_map/ppermute | solution.py:442
  (47 other events, 566.0 us)
Sparse Core Ops, SparseCore 0:
  15.9 65.4 all-gather.2
  83.7 114.1 all-gather.4
  330.2 61.0 reduce-scatter.2
  395.2 123.0 reduce-scatter.4

commit v4 on v3

--- a/solution.py
+++ b/solution.py
@@ -4,6 +4,7 @@
 import jax.numpy as jnp
 from jax import lax
 from jax.experimental import pallas as pl
+from jax.experimental.layout import Layout, with_layout_constraint
 from jax.experimental.pallas import tpu as pltpu
 from jax.sharding import PartitionSpec as P
 
@@ -434,12 +435,44 @@
     )(parts)
 
 
+def by_rows(values):
+    return with_layout_constraint(values, Layout((0, 1)))
+
+
 def after(*values):
     return lax.optimization_barrier(values)
 
 
 def swap(values):
     return lax.ppermute(values, "tensor", [(0, 1), (1, 0)])
+
+
+def tree_gather(n_dp, t, values, split):
+    me = lax.axis_index("dp")
+
+    def joined(own, other, upper, axis):
+        return jnp.where(
+            upper, jnp.concatenate([other, own], axis=axis), jnp.concatenate([own, other], axis=axis)
+        )
+
+    blocks = values[None]
+    steps = [1 << bit for bit in range(n_dp.bit_length() - 1)]
+    for step in reversed(steps[1:]):
+        other = lax.ppermute(blocks, "dp", [(i, i ^ step) for i in range(n_dp)])
+        upper = (me // step) % 2 == 1
+        blocks = joined(blocks[:, None], other[:, None], upper, 1).reshape((-1,) + values.shape)
+    other = swap(blocks)
+    blocks = jnp.concatenate(
+        [
+            joined(blocks[..., :split], other[..., :split], t == 1, 2),
+            joined(blocks[..., split:], other[..., split:], t == 1, 2),
+        ],
+        axis=2,
+    )
+    other = lax.ppermute(blocks, "dp", [(i, i ^ 1) for i in range(n_dp)])
+    full = joined(blocks[:, None], other[:, None], me % 2 == 1, 1)
+    full = full.reshape(n_dp * values.shape[0], 2 * values.shape[1])
+    return full
 
 
 def tree_sum(n_dp, piece, t, values):
@@ -514,12 +547,14 @@
         )
         return jnp.where(t == 0, low, high), jnp.where(t == 0, high, low)
 
-    other_qkv = swap(w_qkv)
-    qkv_local = join(w_qkv, other_qkv, 2)
     kv_local = (
-        qkv_local[:, 1:].reshape(piece, 2, pairs, LANES).transpose(0, 2, 1, 3).reshape(piece, -1)
-    )
-    qkv_local = jnp.concatenate([qkv_local[:, 0], kv_local], axis=1)
+        w_qkv[:, 1:]
+        .reshape(piece, 2, pairs // 2, LANES)
+        .transpose(0, 2, 1, 3)
+        .reshape(piece, 2 * half)
+    )
+    wqkv = tree_gather(n_dp, t, jnp.concatenate([w_qkv[:, 0], kv_local], axis=1), half)
+    wq, wkv = wqkv[:, :width], wqkv[:, width:]
     rest_local = jnp.concatenate([w_out.T, w_up, w_down.T], axis=1)
     other_rest = swap(rest_local)
     up_at, down_at = half, half + hidden_half
@@ -531,13 +566,10 @@
         ],
         axis=1,
     )
-    wqkv = lax.all_gather(qkv_local, "dp", axis=0, tiled=True)
     rest = lax.all_gather(rest_local, "dp", axis=0, tiled=True)
     wout_t = rest[:, :width]
     wup = rest[:, width : width + 2 * hidden_half]
     wdown_t = rest[:, width + 2 * hidden_half :]
-    wkv = wqkv[:, width:]
-    wq = wqkv[:, :width]
 
     small = jnp.stack([ln1_gain, ln1_bias, b_out, ln2_gain, ln2_bias, b_down])
     small = jnp.pad(small, ((0, 2), (0, LANES - piece)))
@@ -553,7 +585,7 @@
     grad_tokens, dealt = after(grad_tokens, dealt)
     sent_grads = mm(picks, grad_tokens).astype(BF16)
     grad_out = lax.all_to_all(sent_grads, "dp", split_axis=0, concat_axis=0, tiled=True)
-    dealt_of_pair = swap(dealt)
+    dealt_of_pair = by_rows(swap(dealt))
     joined = (segment_ids[:1] == segment_ids[-1:]).astype(jnp.int32)
 
     small_full = small_all[:, :6, :piece].transpose(1, 0, 2).reshape(6, width)
@@ -565,7 +597,7 @@
         0,
     )
 
-    resid = dealt.astype(F32)
+    resid = by_rows(dealt.astype(F32))
     ln_one, normed_one, factor_one = normalize(resid, small_full[0], small_full[1])
     ln_one = ln_one.astype(BF16)
     kv_bias = jnp.stack(
@@ -580,7 +612,7 @@
     ln_of_pair = normalize(dealt_of_pair.astype(F32), small_full[0], small_full[1])[0].astype(BF16)
     kv_of_pair = (mm(ln_of_pair, wkv) + kv_bias).astype(BF16)
     attended, lse = attention_pair(joined, qkv, kv_of_pair, own, own_lse)
-    hidden = resid + mm(attended, wout_t, 1, 1) + small_full[2]
+    hidden = by_rows(resid + mm(attended, wout_t, 1, 1) + small_full[2])
 
     ln_two, normed_two, factor_two = normalize(hidden, small_full[3], small_full[4])
     ln_two = ln_two.astype(BF16)
@@ -590,7 +622,7 @@
     gate = 0.5 + 0.5 * bend
     slope = gate + (0.5 * pre_act) * (1.0 - bend * bend) * (GELU_ONE + 3.0 * GELU_THREE * square)
     act, slope = after((pre_act * gate).astype(BF16), slope.astype(BF16))
-    output = (hidden + mm(act, wdown_t, 1, 1) + small_full[5]).astype(BF16)
+    output = by_rows((hidden + mm(act, wdown_t, 1, 1) + small_full[5]).astype(BF16))
 
     grad_down_t = mm(grad_out, act, 0, 0).astype(BF16)
     grad_pre = (mm(grad_out, wdown_t) * slope.astype(F32)).astype(BF16)
@@ -599,7 +631,7 @@
     mlp_grads = jnp.concatenate([grad_down_t, grad_up], axis=1)
     mlp_grads, grad_pre = after(mlp_grads, grad_pre)
     mlp_sum = reduced(mlp_grads)
-    grad_ln_two = mm(grad_pre, wup, 1, 1)
+    grad_ln_two = by_rows(mm(grad_pre, wup, 1, 1))
     gain_two_grad = jnp.sum(grad_ln_two * normed_two, axis=0)
     bias_two_grad = jnp.sum(grad_ln_two, axis=0)
     grad_hidden = grad_out.astype(F32) + norm_back(
@@ -617,16 +649,16 @@
     for_pair = mm(pair_dkv, wkv, 1, 1).astype(BF16)
     for_pair = swap(for_pair)
     dq, dkv = attention_back_own(qkv, grad_att, attended, lse, pair_dq)
+    grad_ln_one = by_rows(mm(dq, wq, 1, 1) + mm(dkv, wkv, 1, 1) + for_pair.astype(F32))
+    grad_input = (
+        grad_hidden + norm_back(grad_ln_one, normed_one, factor_one, small_full[0])
+    ).astype(BF16)
+    dq, dkv, grad_input = after(dq, dkv, grad_input)
     grad_wq = mm(ln_one, dq, 0, 0).astype(BF16)
     grad_wkv = (mm(ln_one, dkv, 0, 0) + mm(ln_of_pair, pair_dkv, 0, 0)).astype(BF16)
     bias_q_grad = jnp.sum(dq, axis=0, dtype=F32)
     kv_sum = jnp.sum(dkv, axis=0, dtype=F32) + jnp.sum(pair_dkv, axis=0, dtype=F32)
     bias_v_grad = kv_sum.reshape(pairs, 2, LANES)[:, 1].reshape(-1)
-    grad_ln_one = mm(dq, wq, 1, 1) + mm(dkv, wkv, 1, 1) + for_pair.astype(F32)
-    grad_input = (
-        grad_hidden + norm_back(grad_ln_one, normed_one, factor_one, small_full[0])
-    ).astype(BF16)
-
     grad_wqkv = jnp.concatenate(
         [grad_wq[:, :half], grad_wkv[:, : 2 * half], grad_wq[:, half:], grad_wkv[:, 2 * half :]],
         axis=1,
@@ -674,7 +706,6 @@
     row_sums = row_sums.reshape(16, n_dp, piece).transpose(1, 0, 2)
     row_sums = jnp.pad(row_sums, ((0, 0), (0, 0), (0, LANES - piece)))
     slice_total, bias_total = sum_small(n_dp, row_sums)
-    grad_input, slice_total = after(grad_input, slice_total)
     small_part = slice_total[8:14, :piece]
     bias_total = bias_total[:, :6, :piece].transpose(1, 0, 2).reshape(6, width)
     qv_part = mine_of(bias_total[:2], 1)[0]

time: 599 us -> 593 us (0.990)
  blocking collectives: 56.3 us -> 0 us
  waiting for transfers between devices: 74.8 us -> 126 us
  starting transfers between devices: 74.1 us -> 93.5 us
  local copies, waits for them, and re-layouts: 43.2 us -> 29.5 us
  Pallas kernels: 162 us -> 149 us
    ppermute x0 -> x4, waiting for transfers between devices: none -> 66.4 us  [the longest x3 66.4 us: tree_gather(): other = lax.ppermute(blocks, 'dp', [(i, i ^ step) for i in range(n_dp)])]
    all_to_all x1 -> x0, blocking collectives: 56.3 us -> none  [per_device(): lax.all_to_all(sent_rows, 'dp', split_axis=0, concat_axis=0, tiled=True)]
    pallas_call x1, Pallas kernels: 57.5 us -> 17.2 us  [share_small(): pl.pallas_call(functools.partial(small_kernel, n_dp), in_specs=[vmem, vme...]
    pallas_call x1, Pallas kernels: 31.6 us -> 59.5 us  [sum_small(): pl.pallas_call(functools.partial(sum_small_kernel, n_dp), in_specs=[vmem]...]
    ppermute x4, starting transfers between devices: 32.1 us -> 48.2 us  [along_dp(): lax.ppermute(v, 'dp', partners)]
    ppermute x4, waiting for transfers between devices: 42.6 us -> 28.4 us  [along_dp(): lax.ppermute(v, 'dp', partners)]
    all_to_all x1, starting transfers between devices: 20.4 us -> 7.76 us  [per_device(): lax.all_to_all(output, 'dp', split_axis=0, concat_axis=0, tiled=True)]
    ppermute x0 -> x4, starting transfers between devices: none -> 6.53 us  [the longest x3 6.52 us: tree_gather(): other = lax.ppermute(blocks, 'dp', [(i, i ^ step) for i in range(n_dp)])]
  transfers between devices with their start and end apart: 18 -> 22, of which waited for: 7 -> 9; matrix products, arithmetic and copies ran while one was open for 19% -> 22% of each run, Pallas kernels for 27% -> 26%
where the time goes in v4:
time: 593 us; the launch traced here: 583 us
  Pallas kernels  149 us (25%)
  waiting for transfers between devices  126 us (21%)
  matrix products  126 us (21%)
  starting transfers between devices  93.5 us (16%)
  other arithmetic  42.9 us (7%)
  local copies, waits for them, and re-layouts  29.5 us (5%)
  between operations  16.4 us (3%)
    dot_general x21, matrix products, mm(): lax.dot_general(left, right, (((left_dim,), (right_dim,)), ((), ())), pre...  126 us
    ppermute x3, waiting for transfers between devices, tree_gather(): other = lax.ppermute(blocks, 'dp', [(i, i ^ step) for i in range(n_dp)])  66.4 us
    pallas_call x1, Pallas kernels, sum_small(): pl.pallas_call(functools.partial(sum_small_kernel, n_dp), in_specs=[vmem]...  59.5 us
    ppermute x4, starting transfers between devices, along_dp(): lax.ppermute(v, 'dp', partners)  48.2 us
    pallas_call x1, Pallas kernels, attention_back_own(): pl.pallas_call(functools.partial(own_backward, kblock=min(512, rows)), gr...  35 us
    ppermute x7, waiting for transfers between devices, swap(): return lax.ppermute(values, 'tensor', [(0, 1), (1, 0)])  31 us
    ppermute x4, waiting for transfers between devices, along_dp(): lax.ppermute(v, 'dp', partners)  28.4 us
    pallas_call x1, Pallas kernels, attention_own(): pl.pallas_call(functools.partial(own_forward, qblock=min(512, rows)), gri...  21.2 us
  transfers between devices with their start and end apart: 22, of which 9 were waited for; matrix products, arithmetic and copies ran while one was open for 22% of the time, Pallas kernels for 26%

profile of v4, /device:TPU:0, one launch (start us, length us, event | category | flops | bytes accessed | tf_op | source)
XLA Modules:
  0.0 583.3 jit_solution(3874803721685012075)
XLA Ops:
  11.5 7.8 %collective-permute-done.6 = bf16[48,3456]{1,0:T(8,128)(2,1)S(1)} collective-permute-done((bf16[48,3456]{1,0:T(8,128)(2,1)S(1)}, bf16[48,3456]{1,0:T(8,128)(2,1)S(1)}, u32[]{:S(2)}, u32[]{:S(2)}) %collective-permute-start.6) | collective-permute-done | bytes 331808 | tf_op jit(solution)/shard_map/ppermute | solution.py:447
  34.8 49.6 %collective-permute-done.1 = bf16[2,48,1152]{2,1,0:T(8,128)(2,1)S(1)} collective-permute-done((bf16[2,48,1152]{2,1,0:T(8,128)(2,1)S(1)}, bf16[2,48,1152]{2,1,0:T(8,128)(2,1)S(1)}, u32[]{:S(2)}, u32[]{:S(2)}) %collective-permute-start.1) | collective-permute-done | bytes 221216 | tf_op jit(solution)/shard_map/ppermute | solution.py:461
  86.2 16.8 %collective-permute-done.2 = bf16[4,48,1152]{2,1,0:T(8,128)(2,1)S(1)} collective-permute-done((bf16[4,48,1152]{2,1,0:T(8,128)(2,1)S(1)}, bf16[4,48,1152]{2,1,0:T(8,128)(2,1)S(1)}, u32[]{:S(2)}, u32[]{:S(2)}) %collective-permute-start.2) | collective-permute-done | bytes 442400 | tf_op jit(solution)/shard_map/ppermute | solution.py:461
  106.0 17.2 %share_small.1 = (f32[16,8,128]{2,1,0:T(8,128)}, f32[24,128]{1,0:T(8,128)}) custom-call(f32[8,128]{1,0:T(8,128)} %pad.13.slice_ref, f32[24,128]{1,0:T(8,128)} %fusion.72.bias_ref), custom_call_target="tpu_custom_call" | custom-call | tf_op jit(solution)/shard_map/share_small/pallas_call | solution.py:320
  133.9 12.3 %all-to-all-start.1 = ((bf16[16,64,768]{2,1,0:T(8,128)(2,1)}), bf16[16,64,768]{2,1,0:T(8,128)(2,1)S(1)}, u32[]{:S(2)}, u32[]{:S(2)}) async-start(bf16[16,64,768]{2,1,0:T(8,128)(2,1)} %bitcast.193), calls=%async_computation.1 | async-start | bytes 3145728 | tf_op jit(solution)/shard_map/all_to_all | solution.py:587
  153.8 7.9 %add_convert_fusion.1.q_ref.kv_ref = bf16[1024,2304]{1,0:T(8,128)(2,1)} fusion(bf16[768,2304]{1,0:T(8,128)(2,1)} %bitcast.27, f32[2304]{0:T(1024)S(1)} %pad_maximum_fusion.8, f32[2304]{0:T(1024)S(1)} %copy-done.46, bf16[1024,768]{1,0:T(8,128)(2,1)S(1)} %bitcast.175, f32[768]{0:T(1024)S(1)} %add.189, f32[768]{0:T(1024)S(1)} %mul.170, ...), kind=kOutput, calls=%fused_computation.8 | convolution fusion | flops 3635675136 | bytes 9863168 | tf_op jit(solution)/shard_map/dot_general | solution.py:37
  161.7 21.2 %attend_own.1 = (f32[1024,768]{1,0:T(8,128)}, f32[1024,768]{1,0:T(8,128)}) custom-call(bf16[1024,2304]{1,0:T(8,128)(2,1)} %add_convert_fusion.1.q_ref.kv_ref, bf16[1024,2304]{1,0:T(8,128)(2,1)} %add_convert_fusion.1.q_ref.kv_ref), custom_call_target="tpu_custom_call" | custom-call | flops 12884901888 | bytes 4718592 | tf_op jit(solution)/shard_map/attend_own/pallas_call | solution.py:188
  184.0 6.0 %add_convert_fusion.2.kv_ref = bf16[1024,1536]{1,0:T(8,128)(2,1)} fusion(f32[1536]{0:T(1024)S(1)} %reshape.410, bf16[768,2304]{1,0:T(8,128)(2,1)} %bitcast.27, bf16[1024,768]{1,0:T(8,128)(2,1)S(1)} %collective-permute-done.5, f32[1024]{0:T(1024)S(1)} %add_rsqrt_fusion.1, f32[1024]{0:T(1024)S(1)} %broadcast_multiply_fusion.5, f32[768]{0:T(1024)S(1)} %add.189, ...), kind=kOutput, calls=%fused_computation.11 | convolution fusion | flops 2423783424 | bytes 7098368 | tf_op jit(solution)/shard_map/dot_general | solution.py:37
  190.0 7.6 %attend_pair.1 = (bf16[1024,768]{1,0:T(8,128)(2,1)}, f32[1024,768]{1,0:T(8,128)}) custom-call(s32[1]{0:T(128)S(6)} %convert_element_type.194.joined_ref, bf16[1024,2304]{1,0:T(8,128)(2,1)} %add_convert_fusion.1.q_ref.kv_ref, bf16[1024,1536]{1,0:T(8,128)(2,1)} %add_convert_fusion.2.kv_ref, f32[1024,768]{1,0:T(8,128)} %get-tuple-element.45.own_ref, ...), custom_call_target="tpu_custom_call" | custom-call | flops 12884901888 | bytes 4718592 | tf_op jit(solution)/shard_map/attend_pair/pallas_call | solution.py:205
  201.5 15.8 %add_convert_fusion = (bf16[1024,3072]{1,0:T(8,128)(2,1)}, bf16[1024,3072]{1,0:T(8,128)(2,1)}) fusion(f32[3072]{0:T(1024)S(1)} %maximum_select_fusion.10, bf16[768,6912]{1,0:T(8,128)(2,1)} %all-gather.2.cloned.1.call-done, f32[1024,768]{1,0:T(8,128)S(1)} %get-tuple-element.111, f32[768]{0:T(1024)S(1)} %add.207, f32[768]{0:T(1024)S(1)} %mul.185, ...), kind=kOutput, calls=%fused_computation.2 | convolution fusion | flops 4892393472 | bytes 20473856 | tf_op jit(solution)/shard_map/dot_general | solution.py:37
  217.4 8.8 %convolution_convert_fusion.1 = bf16[768,3072]{1,0:T(8,128)(2,1)S(1)} fusion(bf16[1024,768]{1,0:T(8,128)(2,1)S(1)} %bitcast.181, bf16[1024,3072]{1,0:T(8,128)(2,1)} %get-tuple-element.48), kind=kOutput, calls=%fused_computation.13 | convolution fusion | flops 4834197504 | bytes 12582912 | tf_op jit(solution)/shard_map/dot_general | solution.py:37
  226.2 8.5 %convert_reduce_fusion = (f32[3072]{0:T(1024)}, bf16[1024,3072]{1,0:T(8,128)(2,1)S(1)}) fusion(bf16[1024,3072]{1,0:T(8,128)(2,1)S(1)} %copy-done.49, bf16[1024,768]{1,0:T(8,128)(2,1)S(1)} %bitcast.182, bf16[768,6912]{1,0:T(8,128)(2,1)} %all-gather.2.cloned.1.call-done), kind=kOutput, calls=%fused_computation | convolution fusion | flops 4847563776 | bytes 18886656 | tf_op jit(solution)/shard_map/dot_general | solution.py:37
  234.7 6.7 %convolution_convert_fusion = bf16[768,3072]{1,0:T(8,128)(2,1)S(1)} fusion(bf16[1024,3072]{1,0:T(8,128)(2,1)S(1)} %get-tuple-element.50, f32[1024,768]{1,0:T(8,128)S(1)} %copy-done.7, f32[768]{0:T(1024)S(1)} %add.207, f32[768]{0:T(1024)S(1)} %mul.185, f32[1024]{0:T(1024)S(1)} %add_rsqrt_fusion, f32[1024]{0:T(1024)S(1)} %broadcast_multiply_fusion.4), kind=kOutput, calls=%fused_computation.12 | convolution fusion | flops 4838129664 | bytes 14170112 | tf_op jit(solution)/shard_map/dot_general | solution.py:37
  245.4 9.8 %multiply_reduce_fusion = (f32[768]{0:T(1024)S(1)}, f32[1024]{0:T(1024)S(1)}, f32[1024]{0:T(1024)S(1)}, f32[768]{0:T(1024)S(1)}, f32[1024,768]{1,0:T(8,128)S(1)}) fusion(f32[1024,768]{1,0:T(8,128)} %copy-done.6, f32[1024]{0:T(1024)S(1)} %add_rsqrt_fusion, f32[1024]{0:T(1024)S(1)} %broadcast_multiply_fusion.4, f32[768]{0:T(1024)S(1)} %mul.185, ...), kind=kOutput, calls=%fused_computation.59 | convolution fusion | flops 4838912000 | bytes 17327104 | tf_op jit(solution)/shard_map/dot_general | solution.py:37
  267.2 9.5 %add_convert_fusion.4 = bf16[1024,768]{1,0:T(8,128)(2,1)} fusion(f32[1024,768]{1,0:T(8,128)S(1)} %copy-done.9, bf16[1024,3072]{1,0:T(8,128)(2,1)} %get-tuple-element.48, bf16[768,6912]{1,0:T(8,128)(2,1)} %all-gather.2.cloned.1.call-done, f32[768]{0:T(1024)S(1)} %add.218), kind=kOutput, calls=%fused_computation.62 | convolution fusion | flops 4834197504 | bytes 15731712 | tf_op jit(solution)/shard_map/dot_general | solution.py:37
  276.8 8.5 %attend_back_pair.1 = (f32[768,1024]{1,0:T(8,128)}, bf16[1024,1536]{1,0:T(8,128)(2,1)}) custom-call(s32[1]{0:T(128)S(6)} %convert_element_type.194.joined_ref, bf16[1024,2304]{1,0:T(8,128)(2,1)} %add_convert_fusion.1.q_ref.kv_ref, bf16[1024,768]{1,0:T(8,128)(2,1)} %convolution_convert_fusion.2.grad_ref, bf16[1024,768]{1,0:T(8,128)(2,1)} %get-tuple-element.47.mixed_ref, ...), custom_call_target="tpu_custom_call" | custom-call | flops 32212254720 | bytes 4718592 | tf_op jit(solution)/shard_map/attend_back_pair/pallas_call | solution.py:226
  285.3 6.5 %fusion.45 = bf16[1024,768]{1,0:T(8,128)(2,1)} fusion(bf16[1024,1536]{1,0:T(8,128)(2,1)} %get-tuple-element.57, bf16[768,2304]{1,0:T(8,128)(2,1)} %bitcast.27), kind=kOutput, calls=%fused_computation.84 | convolution fusion | flops 2416705536 | bytes 7077888 | tf_op jit(solution)/shard_map/dot_general | solution.py:37
  293.2 35.0 %attend_back_own.1 = (bf16[1024,768]{1,0:T(8,128)(2,1)}, bf16[1024,1536]{1,0:T(8,128)(2,1)}) custom-call(bf16[1024,2304]{1,0:T(8,128)(2,1)} %add_convert_fusion.1.q_ref.kv_ref, bf16[1024,768]{1,0:T(8,128)(2,1)} %convolution_convert_fusion.2.grad_ref, bf16[1024,768]{1,0:T(8,128)(2,1)} %get-tuple-element.47.mixed_ref, f32[1024,768]{1,0:T(8,128)} %get-tuple-element.53.lse_ref, ...), custom_call_target="tpu_custom_call" | custom-call | flops 32212254720 | bytes 4718592 | tf_op jit(solution)/shard_map/attend_back_own/pallas_call | solution.py:249
  332.5 6.3 %fusion.27 = (f32[768]{0:T(1024)}, f32[1024]{0:T(1024)S(1)}, f32[1024]{0:T(1024)S(1)}, f32[768]{0:T(1024)}, f32[1024,768]{1,0:T(8,128)S(1)}) fusion(bf16[1024,768]{1,0:T(8,128)(2,1)S(1)} %bitcast.177, f32[1024]{0:T(1024)S(1)} %copy-done.27, f32[1024]{0:T(1024)S(1)} %copy-done.22, f32[768]{0:T(1024)S(1)} %copy-done.25, ...), kind=kOutput, calls=%fused_computation.51 | convolution fusion | flops 2426139136 | bytes 14967808 | tf_op jit(solution)/shard_map/dot_general | solution.py:37
  357.8 42.1 %collective-permute-start.8 = (bf16[8,48,2304]{2,1,0:T(8,128)(2,1)}, bf16[8,48,2304]{2,1,0:T(8,128)(2,1)}, u32[]{:S(2)}, u32[]{:S(2)}) collective-permute-start(bf16[8,48,2304]{2,1,0:T(8,128)(2,1)} %select_bitcast_fusion), channel_id=1, source_target_pairs={{0,2},{2,0},{4,6},{6,4},{8,10},{10,8},{12,14},{14,12},{16,18},{18,... | collective-permute-start | bytes 5308424 | tf_op jit(solution)/shard_map/ppermute | solution.py:494
  405.8 7.8 %all-to-all-start.2 = ((bf16[16,64,768]{2,1,0:T(8,128)(2,1)}), bf16[16,64,768]{2,1,0:T(8,128)(2,1)}, u32[]{:S(2)}, u32[]{:S(2)}) async-start(bf16[16,64,768]{2,1,0:T(8,128)(2,1)} %bitcast.192), calls=%async_computation.2 | async-start | bytes 3145728 | tf_op jit(solution)/shard_map/all_to_all | solution.py:714
  429.3 59.5 %sum_small.1 = (f32[16,128]{1,0:T(8,128)}, f32[16,8,128]{2,1,0:T(8,128)}) custom-call(f32[16,16,128]{2,1,0:T(8,128)} %pad.15.parts_ref), custom_call_target="tpu_custom_call" | custom-call | tf_op jit(solution)/shard_map/sum_small/pallas_call | solution.py:417
  498.3 17.6 %collective-permute-done.9 = bf16[8,48,1152]{2,1,0:T(8,128)(2,1)S(1)} collective-permute-done((bf16[8,48,1152]{2,1,0:T(8,128)(2,1)S(1)}, bf16[8,48,1152]{2,1,0:T(8,128)(2,1)S(1)}, u32[]{:S(2)}, u32[]{:S(2)}) %collective-permute-start.9) | collective-permute-done | bytes 884768 | tf_op jit(solution)/shard_map/ppermute | solution.py:447
  525.9 21.3 %collective-permute-done.10 = bf16[4,48,1152]{2,1,0:T(8,128)(2,1)S(1)} collective-permute-done((bf16[4,48,1152]{2,1,0:T(8,128)(2,1)S(1)}, bf16[4,48,1152]{2,1,0:T(8,128)(2,1)S(1)}, u32[]{:S(2)}, u32[]{:S(2)}) %collective-permute-start.10) | collective-permute-done | bytes 442400 | tf_op jit(solution)/shard_map/ppermute | solution.py:494
  (272 shorter events, 156.8 us)
Async XLA Ops:
  7.2 190.4 %all-gather.2.cloned.1.call-start = ((), (), s32[]{:S(2)}) async-start(), calls=%async_computation.6 | async-start | bytes 11280384 | tf_op jit(solution)/shard_map/all_gather | solution.py:569
  8.4 10.9 %collective-permute-start.6 = (bf16[48,3456]{1,0:T(8,128)(2,1)S(1)}, bf16[48,3456]{1,0:T(8,128)(2,1)S(1)}, u32[]{:S(2)}, u32[]{:S(2)}) collective-permute-start(bf16[48,3456]{1,0:T(8,128)(2,1)S(1)} %pad_maximum_fusion.4), channel_id=1, source_target_pairs={{0,1},{1,0},{2,3},{3,2},{4,5},{5,4},{6,7},{7,6},{8,9},{9,8},{10,11... | collective-permute-start | bytes 995336 | tf_op jit(solution)/shard_map/ppermute | solution.py:447
  22.6 10.2 %collective-permute-start = (bf16[1,48,1152]{2,1,0:T(8,128)(2,1)S(1)}, bf16[1,48,1152]{2,1,0:T(8,128)(2,1)S(1)}, u32[]{:S(2)}, u32[]{:S(2)}) collective-permute-start(bf16[1,48,1152]{2,1,0:T(8,128)(2,1)S(1)} %get-tuple-element.98), channel_id=1, source_target_pairs={{0,16},{2,18},{4,20},{6,22},{8,24},{10,26},{12,28},{14,30},{16,0},... | collective-permute-start | bytes 331784 | tf_op jit(solution)/shard_map/ppermute | solution.py:461
  28.6 76.1 %copy-start.40 = (f32[48]{0:T(128)S(1)}, f32[48]{0:T(128)}, u32[]{:S(2)}) copy-start(f32[48]{0:T(128)} %param.26) | copy-start | bytes 580
  28.6 76.7 %copy-start.23 = (f32[1536]{0:T(1024)S(1)}, f32[1536]{0:T(1024)}, u32[]{:S(2)}) copy-start(f32[1536]{0:T(1024)} %param.29) | copy-start | bytes 18436
  28.7 102.2 %all-to-all-start = ((bf16[16,64,768]{2,1,0:T(8,128)(2,1)}), bf16[16,64,768]{2,1,0:T(8,128)(2,1)S(1)}, u32[]{:S(2)}, u32[]{:S(2)}) async-start(bf16[16,64,768]{2,1,0:T(8,128)(2,1)} %bitcast.1), calls=%async_computation | async-start | bytes 3145728 | tf_op jit(solution)/shard_map/all_to_all | solution.py:584
  32.8 51.6 %collective-permute-start.1 = (bf16[2,48,1152]{2,1,0:T(8,128)(2,1)S(1)}, bf16[2,48,1152]{2,1,0:T(8,128)(2,1)S(1)}, u32[]{:S(2)}, u32[]{:S(2)}) collective-permute-start(bf16[2,48,1152]{2,1,0:T(8,128)(2,1)S(1)} %maximum_select_fusion.7), channel_id=1, source_target_pairs={{0,8},{2,10},{4,12},{6,14},{8,0},{10,2},{12,4},{14,6},{16,24},{18,... | collective-permute-start | bytes 663560 | tf_op jit(solution)/shard_map/ppermute | solution.py:461
  84.5 18.5 %collective-permute-start.2 = (bf16[4,48,1152]{2,1,0:T(8,128)(2,1)S(1)}, bf16[4,48,1152]{2,1,0:T(8,128)(2,1)S(1)}, u32[]{:S(2)}, u32[]{:S(2)}) collective-permute-start(bf16[4,48,1152]{2,1,0:T(8,128)(2,1)S(1)} %bitcast.190), channel_id=1, source_target_pairs={{0,4},{2,6},{4,0},{6,2},{8,12},{10,14},{12,8},{14,10},{16,20},{18,... | collective-permute-start | bytes 1327112 | tf_op jit(solution)/shard_map/ppermute | solution.py:461
  103.0 22.0 %collective-permute-start.3 = (bf16[8,48,1152]{2,1,0:T(8,128)(2,1)S(1)}, bf16[8,48,1152]{2,1,0:T(8,128)(2,1)S(1)}, u32[]{:S(2)}, u32[]{:S(2)}) collective-permute-start(bf16[8,48,1152]{2,1,0:T(8,128)(2,1)S(1)} %bitcast.187), channel_id=1, source_target_pairs={{0,1},{1,0},{2,3},{3,2},{4,5},{5,4},{6,7},{7,6},{8,9},{9,8},{10,11... | collective-permute-start | bytes 2654216 | tf_op jit(solution)/shard_map/ppermute | solution.py:447
  127.7 21.0 %collective-permute-start.4 = (bf16[8,48,2304]{2,1,0:T(8,128)(2,1)}, bf16[8,48,2304]{2,1,0:T(8,128)(2,1)}, u32[]{:S(2)}, u32[]{:S(2)}) collective-permute-start(bf16[8,48,2304]{2,1,0:T(8,128)(2,1)} %get-tuple-element.86), channel_id=1, source_target_pairs={{0,2},{2,0},{4,6},{6,4},{8,10},{10,8},{12,14},{14,12},{16,18},{18,... | collective-permute-start | bytes 5308424 | tf_op jit(solution)/shard_map/ppermute | solution.py:472
  133.9 83.4 %all-to-all-start.1 = ((bf16[16,64,768]{2,1,0:T(8,128)(2,1)}), bf16[16,64,768]{2,1,0:T(8,128)(2,1)S(1)}, u32[]{:S(2)}, u32[]{:S(2)}) async-start(bf16[16,64,768]{2,1,0:T(8,128)(2,1)} %bitcast.193), calls=%async_computation.1 | async-start | bytes 3145728 | tf_op jit(solution)/shard_map/all_to_all | solution.py:587
  146.2 349.8 %reduce-scatter.3.cloned.1.call-start = ((), (), s32[]{:S(2)}) async-start(), calls=%async_computation.7 | async-start | bytes 1253376 | tf_op jit(solution)/shard_map/reduce_scatter | solution.py:540
  146.3 36.8 %collective-permute-start.5 = (bf16[1024,768]{1,0:T(8,128)(2,1)S(1)}, bf16[1024,768]{1,0:T(8,128)(2,1)S(1)}, u32[]{:S(2)}, u32[]{:S(2)}) collective-permute-start(bf16[1024,768]{1,0:T(8,128)(2,1)S(1)} %bitcast.172), channel_id=1, source_target_pairs={{0,1},{1,0},{2,3},{3,2},{4,5},{5,4},{6,7},{7,6},{8,9},{9,8},{10,11... | collective-permute-start | bytes 4718600 | tf_op jit(solution)/shard_map/ppermute | solution.py:447
  276.8 290.7 %reduce-scatter.5.cloned.1.call-start = ((), (), s32[]{:S(2)}) async-start(), calls=%async_computation.8 | async-start | bytes 10027008 | tf_op jit(solution)/shard_map/reduce_scatter | solution.py:540
  291.8 40.7 %collective-permute-start.7 = (bf16[1024,768]{1,0:T(8,128)(2,1)}, bf16[1024,768]{1,0:T(8,128)(2,1)}, u32[]{:S(2)}, u32[]{:S(2)}) collective-permute-start(bf16[1024,768]{1,0:T(8,128)(2,1)} %fusion.45), channel_id=1, source_target_pairs={{0,1},{1,0},{2,3},{3,2},{4,5},{5,4},{6,7},{7,6},{8,9},{9,8},{10,11... | collective-permute-start | bytes 4718600 | tf_op jit(solution)/shard_map/ppermute | solution.py:447
  357.8 131.0 %collective-permute-start.8 = (bf16[8,48,2304]{2,1,0:T(8,128)(2,1)}, bf16[8,48,2304]{2,1,0:T(8,128)(2,1)}, u32[]{:S(2)}, u32[]{:S(2)}) collective-permute-start(bf16[8,48,2304]{2,1,0:T(8,128)(2,1)} %select_bitcast_fusion), channel_id=1, source_target_pairs={{0,2},{2,0},{4,6},{6,4},{8,10},{10,8},{12,14},{14,12},{16,18},{18,... | collective-permute-start | bytes 5308424 | tf_op jit(solution)/shard_map/ppermute | solution.py:494
  405.8 111.9 %all-to-all-start.2 = ((bf16[16,64,768]{2,1,0:T(8,128)(2,1)}), bf16[16,64,768]{2,1,0:T(8,128)(2,1)}, u32[]{:S(2)}, u32[]{:S(2)}) async-start(bf16[16,64,768]{2,1,0:T(8,128)(2,1)} %bitcast.192), calls=%async_computation.2 | async-start | bytes 3145728 | tf_op jit(solution)/shard_map/all_to_all | solution.py:714
  493.8 22.1 %collective-permute-start.9 = (bf16[8,48,1152]{2,1,0:T(8,128)(2,1)S(1)}, bf16[8,48,1152]{2,1,0:T(8,128)(2,1)S(1)}, u32[]{:S(2)}, u32[]{:S(2)}) collective-permute-start(bf16[8,48,1152]{2,1,0:T(8,128)(2,1)S(1)} %broadcast_select_fusion), channel_id=1, source_target_pairs={{0,1},{1,0},{2,3},{3,2},{4,5},{5,4},{6,7},{7,6},{8,9},{9,8},{10,11... | collective-permute-start | bytes 2654216 | tf_op jit(solution)/shard_map/ppermute | solution.py:447
  496.8 28.4 %collective-permute-start.13 = (bf16[48,384]{1,0:T(8,128)(2,1)S(1)}, bf16[48,384]{1,0:T(8,128)(2,1)S(1)}, u32[]{:S(2)}, u32[]{:S(2)}) collective-permute-start(bf16[48,384]{1,0:T(8,128)(2,1)S(1)} %broadcast_select_fusion.5), channel_id=1, source_target_pairs={{0,1},{1,0},{2,3},{3,2},{4,5},{5,4},{6,7},{7,6},{8,9},{9,8},{10,11... | collective-permute-start | bytes 110600 | tf_op jit(solution)/shard_map/ppermute | solution.py:447
  517.7 44.4 %all-to-all-start.3 = ((bf16[16,64,768]{2,1,0:T(8,128)(2,1)}), bf16[16,64,768]{2,1,0:T(8,128)(2,1)S(1)}, u32[]{:S(2)}, u32[]{:S(2)}) async-start(bf16[16,64,768]{2,1,0:T(8,128)(2,1)} %bitcast.33), calls=%async_computation.3 | async-start | bytes 3145728 | tf_op jit(solution)/shard_map/all_to_all | solution.py:715
  522.0 25.2 %collective-permute-start.10 = (bf16[4,48,1152]{2,1,0:T(8,128)(2,1)S(1)}, bf16[4,48,1152]{2,1,0:T(8,128)(2,1)S(1)}, u32[]{:S(2)}, u32[]{:S(2)}) collective-permute-start(bf16[4,48,1152]{2,1,0:T(8,128)(2,1)S(1)} %fusion.61), channel_id=1, source_target_pairs={{0,4},{2,6},{4,0},{6,2},{8,12},{10,14},{12,8},{14,10},{16,20},{18,... | collective-permute-start | bytes 1327112 | tf_op jit(solution)/shard_map/ppermute | solution.py:494
  547.4 11.5 %collective-permute-start.11 = (bf16[2,48,1152]{2,1,0:T(8,128)(2,1)S(1)}, bf16[2,48,1152]{2,1,0:T(8,128)(2,1)S(1)}, u32[]{:S(2)}, u32[]{:S(2)}) collective-permute-start(bf16[2,48,1152]{2,1,0:T(8,128)(2,1)S(1)} %fusion.64), channel_id=1, source_target_pairs={{0,8},{2,10},{4,12},{6,14},{8,0},{10,2},{12,4},{14,6},{16,24},{18,... | collective-permute-start | bytes 663560 | tf_op jit(solution)/shard_map/ppermute | solution.py:494
  559.0 8.2 %collective-permute-start.12 = (bf16[1,48,1152]{2,1,0:T(8,128)(2,1)S(1)}, bf16[1,48,1152]{2,1,0:T(8,128)(2,1)S(1)}, u32[]{:S(2)}, u32[]{:S(2)}) collective-permute-start(bf16[1,48,1152]{2,1,0:T(8,128)(2,1)S(1)} %select_bitcast_fusion.1), channel_id=1, source_target_pairs={{0,16},{2,18},{4,20},{6,22},{8,24},{10,26},{12,28},{14,30},{16,0},... | collective-permute-start | bytes 331784 | tf_op jit(solution)/shard_map/ppermute | solution.py:494
  568.8 6.8 %collective-permute-start.14 = (bf16[48,3072]{1,0:T(8,128)(2,1)S(1)}, bf16[48,3072]{1,0:T(8,128)(2,1)S(1)}, u32[]{:S(2)}, u32[]{:S(2)}) collective-permute-start(bf16[48,3072]{1,0:T(8,128)(2,1)S(1)} %pad_maximum_fusion.5), channel_id=1, source_target_pairs={{0,1},{1,0},{2,3},{3,2},{4,5},{5,4},{6,7},{7,6},{8,9},{9,8},{10,11... | collective-permute-start | bytes 884744 | tf_op jit(solution)/shard_map/ppermute | solution.py:447
  (49 other events, 987.7 us)
Sparse Core Ops, SparseCore 0:
  22.5 124.5 all-gather.1
  276.9 74.6 reduce-scatter.2
  355.6 160.9 reduce-scatter.4

commit v5 on v4

--- a/solution.py
+++ b/solution.py
@@ -334,107 +334,6 @@
     )(slices, biases)
 
 
-def sum_small_kernel(
-    n_dp, parts_ref, total_ref, bias_ref, landed, pair_sum, pair_in, own_bias, send_sem, recv_sem
-):
-    me = lax.axis_index("dp")
-    t = lax.axis_index("tensor")
-    mesh_id = pl.DeviceIdType.MESH
-
-    barrier = pltpu.get_barrier_semaphore()
-
-    def greet(step, carry):
-        pl.semaphore_signal(
-            barrier, inc=1, device_id=(lax.rem(me + step, n_dp), t), device_id_type=mesh_id
-        )
-        return carry
-
-    lax.fori_loop(1, n_dp, greet, 0)
-    pl.semaphore_signal(barrier, inc=1, device_id=(me, 1 - t), device_id_type=mesh_id)
-    pl.semaphore_wait(barrier, n_dp)
-
-    def part_to(step):
-        peer = lax.rem(me + step, n_dp)
-        return pltpu.make_async_remote_copy(
-            src_ref=parts_ref.at[peer],
-            dst_ref=landed.at[step],
-            send_sem=send_sem.at[0, step],
-            recv_sem=recv_sem.at[0, step],
-            device_id=(peer, t),
-            device_id_type=mesh_id,
-        )
-
-    def bias_to(step):
-        return pltpu.make_async_remote_copy(
-            src_ref=own_bias,
-            dst_ref=bias_ref.at[me],
-            send_sem=send_sem.at[1, step],
-            recv_sem=recv_sem.at[1, step],
-            device_id=(lax.rem(me + step, n_dp), t),
-            device_id_type=mesh_id,
-        )
-
-    def start_part(step, carry):
-        part_to(step).start()
-        return carry
-
-    def add_part(step, carry):
-        part_to(step).wait()
-        return carry + landed[step]
-
-    lax.fori_loop(1, n_dp, start_part, 0)
-    pair_sum[...] = lax.fori_loop(1, n_dp, add_part, parts_ref[me])
-    to_partner = pltpu.make_async_remote_copy(
-        src_ref=pair_sum,
-        dst_ref=pair_in,
-        send_sem=send_sem.at[1, 0],
-        recv_sem=recv_sem.at[1, 0],
-        device_id=(me, 1 - t),
-        device_id_type=mesh_id,
-    )
-    to_partner.start()
-    to_partner.wait()
-    total = pair_sum[...] + pair_in[...]
-    total_ref[...] = total
-    own_bias[...] = total[:8]
-    bias_ref[me] = total[:8]
-
-    def start_bias(step, carry):
-        bias_to(step).start()
-        return carry
-
-    def finish_bias(step, carry):
-        bias_to(step).wait()
-        return carry
-
-    lax.fori_loop(1, n_dp, start_bias, 0)
-    lax.fori_loop(1, n_dp, finish_bias, 0)
-
-
-def sum_small(n_dp, parts):
-    vmem = pl.BlockSpec(memory_space=pltpu.VMEM)
-    block = parts.shape[1:]
-    return pl.pallas_call(
-        functools.partial(sum_small_kernel, n_dp),
-        in_specs=[vmem],
-        out_specs=[vmem, vmem],
-        out_shape=[
-            jax.ShapeDtypeStruct(block, F32),
-            jax.ShapeDtypeStruct((n_dp, 8, LANES), F32),
-        ],
-        scratch_shapes=[
-            pltpu.VMEM(parts.shape, F32),
-            pltpu.VMEM(block, F32),
-            pltpu.VMEM(block, F32),
-            pltpu.VMEM((8, LANES), F32),
-            pltpu.SemaphoreType.DMA((2, n_dp)),
-            pltpu.SemaphoreType.DMA((2, n_dp)),
-        ],
-        compiler_params=pltpu.CompilerParams(collective_id=1, has_side_effects=True),
-        name="sum_small",
-    )(parts)
-
-
 def by_rows(values):
     return with_layout_constraint(values, Layout((0, 1)))
 
@@ -475,32 +374,36 @@
     return full
 
 
-def tree_sum(n_dp, piece, t, values):
+def tree_sum(n_dp, piece, t, values, rows):
     me = lax.axis_index("dp")
     columns = values.shape[1]
 
-    def add(first, second, upper, exchange):
+    def add(first, second, upper, rows, exchange):
         mine = jnp.where(upper, second, first)
-        arrived = exchange(jnp.where(upper, first, second))
-        return mine.astype(F32) + arrived.astype(F32)
-
-    def along_dp(total, step):
+        sent, rows = after(jnp.where(upper, first, second), rows)
+        arrived, arrived_rows = after(exchange(sent), exchange(rows))
+        total = (mine.astype(F32) + arrived.astype(F32)).astype(BF16)
+        return total, rows + arrived_rows
+
+    def along_dp(total, rows, step):
         blocks = total.reshape(-1, 2, piece, total.shape[-1])
         partners = [(i, i ^ step) for i in range(n_dp)]
         return add(
             blocks[:, 0],
             blocks[:, 1],
             (me // step) % 2 == 1,
+            rows,
             lambda v: lax.ppermute(v, "dp", partners),
-        ).astype(BF16)
-
-    total = along_dp(values, 1)
-    total = add(total[..., : columns // 2], total[..., columns // 2 :], t == 1, swap).astype(BF16)
+        )
+
+    total, rows = along_dp(values, rows, 1)
+    low, high = total[..., : columns // 2], total[..., columns // 2 :]
+    total, rows = add(low, high, t == 1, rows, swap)
     step = 2
     while step < n_dp:
-        total = along_dp(total, step)
+        total, rows = along_dp(total, rows, step)
         step *= 2
-    return total.reshape(piece, columns // 2).astype(F32)
+    return total.reshape(piece, columns // 2).astype(F32), rows
 
 
 def per_device(
@@ -622,15 +525,12 @@
     gate = 0.5 + 0.5 * bend
     slope = gate + (0.5 * pre_act) * (1.0 - bend * bend) * (GELU_ONE + 3.0 * GELU_THREE * square)
     act, slope = after((pre_act * gate).astype(BF16), slope.astype(BF16))
-    output = by_rows((hidden + mm(act, wdown_t, 1, 1) + small_full[5]).astype(BF16))
 
     grad_down_t = mm(grad_out, act, 0, 0).astype(BF16)
     grad_pre = (mm(grad_out, wdown_t) * slope.astype(F32)).astype(BF16)
     bias_up_grad = jnp.sum(grad_pre, axis=0, dtype=F32)
     grad_up = mm(ln_two, grad_pre, 0, 0).astype(BF16)
-    mlp_grads = jnp.concatenate([grad_down_t, grad_up], axis=1)
-    mlp_grads, grad_pre = after(mlp_grads, grad_pre)
-    mlp_sum = reduced(mlp_grads)
+    grad_down_t, grad_up, grad_pre = after(grad_down_t, grad_up, grad_pre)
     grad_ln_two = by_rows(mm(grad_pre, wup, 1, 1))
     gain_two_grad = jnp.sum(grad_ln_two * normed_two, axis=0)
     bias_two_grad = jnp.sum(grad_ln_two, axis=0)
@@ -639,8 +539,11 @@
     )
     grad_branch = grad_hidden.astype(BF16)
     grad_wout_t = mm(grad_branch, attended, 0, 0).astype(BF16)
-    wout_sum = reduced(grad_wout_t)
+    mlp_grads = jnp.concatenate([grad_down_t, grad_up, grad_wout_t], axis=1)
+    mlp_grads, grad_branch, act = after(mlp_grads, grad_branch, act)
+    mlp_sum = reduced(mlp_grads)
     grad_att = mm(grad_branch, wout_t).astype(BF16)
+    output = by_rows((hidden + mm(act, wdown_t, 1, 1) + small_full[5]).astype(BF16))
     grad_att, output = after(grad_att, output)
 
     pair_dq, pair_dkv = attention_back_pair(
@@ -663,7 +566,29 @@
         [grad_wq[:, :half], grad_wkv[:, : 2 * half], grad_wq[:, half:], grad_wkv[:, 2 * half :]],
         axis=1,
     )
-    qkv_part = tree_sum(n_dp, piece, t, grad_wqkv)
+    row_sums = jnp.concatenate(
+        [
+            jnp.stack(
+                [
+                    jnp.sum(grad_ln_one * normed_one, axis=0),
+                    jnp.sum(grad_ln_one, axis=0),
+                    jnp.sum(grad_hidden, axis=0),
+                    gain_two_grad,
+                    bias_two_grad,
+                    jnp.sum(grad_out, axis=0, dtype=F32),
+                    bias_q_grad,
+                    bias_v_grad,
+                ]
+            ),
+            bias_up_grad.reshape(-1, width),
+        ]
+    )
+    qkv_part, row_sums = tree_sum(n_dp, piece, t, grad_wqkv, row_sums)
+    small_part = lax.dynamic_slice_in_dim(
+        row_sums[:6], lax.axis_index("dp") * piece, piece, 1
+    )
+    qv_part = mine_of(row_sums[6:8], 1)[0]
+    bias_up_part = mine_of(row_sums[8:].reshape(-1), 0)[0]
 
     def paired(values, sizes):
         columns, start = [], 0
@@ -676,40 +601,13 @@
         cuts = [sum(sizes[:i]) // 2 for i in range(1, len(sizes))]
         return jnp.split(total, cuts, axis=1)
 
-    down_part, up_part = paired(mlp_sum, (2 * hidden_half, 2 * hidden_half))
-    wout_part = paired(wout_sum, (width,))[0].T
-    down_part = down_part.T
+    down_part, up_part, wout_part = paired(mlp_sum, (2 * hidden_half, 2 * hidden_half, width))
+    down_part, wout_part = down_part.T, wout_part.T
     q_part, kv_part = qkv_part[:, :half], qkv_part[:, half:]
     kv_part = kv_part.reshape(piece, pairs // 2, 2, LANES).transpose(0, 2, 1, 3)
     qkv_part = jnp.concatenate(
         [q_part.reshape(piece, 1, half), kv_part.reshape(piece, 2, half)], axis=1
     )
-
-    row_sums = jnp.concatenate(
-        [
-            jnp.stack([bias_q_grad, bias_v_grad]),
-            bias_up_grad.reshape(-1, width),
-            jnp.zeros((2, width), F32),
-            jnp.stack(
-                [
-                    jnp.sum(grad_ln_one * normed_one, axis=0),
-                    jnp.sum(grad_ln_one, axis=0),
-                    jnp.sum(grad_hidden, axis=0),
-                    gain_two_grad,
-                    bias_two_grad,
-                    jnp.sum(grad_out, axis=0, dtype=F32),
-                ]
-            ),
-            jnp.zeros((2, width), F32),
-        ]
-    )
-    row_sums = row_sums.reshape(16, n_dp, piece).transpose(1, 0, 2)
-    row_sums = jnp.pad(row_sums, ((0, 0), (0, 0), (0, LANES - piece)))
-    slice_total, bias_total = sum_small(n_dp, row_sums)
-    small_part = slice_total[8:14, :piece]
-    bias_total = bias_total[:, :6, :piece].transpose(1, 0, 2).reshape(6, width)
-    qv_part = mine_of(bias_total[:2], 1)[0]
-    bias_up_part = mine_of(bias_total[2:].reshape(-1), 0)[0]
 
     sent_out = lax.all_to_all(output, "dp", split_axis=0, concat_axis=0, tiled=True)
     sent_grad = lax.all_to_all(grad_input, "dp", split_axis=0, concat_axis=0, tiled=True)

time: 593 us -> 524 us (0.88)
  Pallas kernels: 149 us -> 89.7 us
  matrix products: 126 us -> 114 us
  waiting for transfers between devices: 126 us -> 138 us
  local copies, waits for them, and re-layouts: 29.5 us -> 18.3 us
  starting transfers between devices: 93.5 us -> 99.6 us
    pallas_call x1 -> x0, Pallas kernels: 59.5 us -> none  [sum_small(): pl.pallas_call(functools.partial(sum_small_kernel, n_dp), in_specs=[vmem]...]
    dot_general x21, matrix products: 126 us -> 114 us  [mm(): lax.dot_general(left, right, (((left_dim,), (right_dim,)), ((), ())), pre...]
    concatenate x12 -> x1, local copies, waits for them, and re-layouts: 11.9 us -> 1.27 us  [per_device(): jnp.concatenate([jnp.stack([jnp.sum(grad_ln_one * normed_one, axis=0), jn...]
    ppermute x4 -> x8, waiting for transfers between devices: 28.4 us -> 34.9 us  [along_dp(): lax.ppermute(v, 'dp', partners)]
    ppermute x4 -> x8, starting transfers between devices: 48.2 us -> 49.9 us  [along_dp(): lax.ppermute(v, 'dp', partners)]
  transfers between devices with their start and end apart: 22 -> 25, of which waited for: 9 -> 11; matrix products, arithmetic and copies ran while one was open for 22% -> 17% of each run, Pallas kernels for 26% -> 17%
where the time goes in v5:
time: 524 us; the launch traced here: 516 us
  waiting for transfers between devices  138 us (26%)
  matrix products  114 us (22%)
  starting transfers between devices  99.6 us (19%)
  Pallas kernels  89.7 us (17%)
  other arithmetic  39.2 us (7%)
  local copies, waits for them, and re-layouts  18.3 us (3%)
  between operations  16.9 us (3%)
    dot_general x21, matrix products, mm(): lax.dot_general(left, right, (((left_dim,), (right_dim,)), ((), ())), pre...  114 us
    ppermute x3, waiting for transfers between devices, tree_gather(): other = lax.ppermute(blocks, 'dp', [(i, i ^ step) for i in range(n_dp)])  66.4 us
    ppermute x8, starting transfers between devices, along_dp(): lax.ppermute(v, 'dp', partners)  49.9 us
    pallas_call x1, Pallas kernels, attention_back_own(): pl.pallas_call(functools.partial(own_backward, kblock=min(512, rows)), gr...  35 us
    ppermute x8, waiting for transfers between devices, along_dp(): lax.ppermute(v, 'dp', partners)  34.9 us
    ppermute x7, waiting for transfers between devices, swap(): return lax.ppermute(values, 'tensor', [(0, 1), (1, 0)])  32.8 us
    pallas_call x1, Pallas kernels, attention_own(): pl.pallas_call(functools.partial(own_forward, qblock=min(512, rows)), gri...  21.3 us
    pallas_call x1, Pallas kernels, share_small(): pl.pallas_call(functools.partial(small_kernel, n_dp), in_specs=[vmem, vme...  17.2 us
  transfers between devices with their start and end apart: 25, of which 11 were waited for; matrix products, arithmetic and copies ran while one was open for 17% of the time, Pallas kernels for 17%

profile of v5, /device:TPU:0, one launch (start us, length us, event | category | flops | bytes accessed | tf_op | source)
XLA Modules:
  0.0 516.2 jit_solution(13672776792738491304)
XLA Ops:
  11.5 7.8 %collective-permute-done.6 = bf16[48,3456]{1,0:T(8,128)(2,1)S(1)} collective-permute-done((bf16[48,3456]{1,0:T(8,128)(2,1)S(1)}, bf16[48,3456]{1,0:T(8,128)(2,1)S(1)}, u32[]{:S(2)}, u32[]{:S(2)}) %collective-permute-start.6) | collective-permute-done | bytes 331808 | tf_op jit(solution)/shard_map/ppermute | solution.py:346
  34.8 49.6 %collective-permute-done.1 = bf16[2,48,1152]{2,1,0:T(8,128)(2,1)S(1)} collective-permute-done((bf16[2,48,1152]{2,1,0:T(8,128)(2,1)S(1)}, bf16[2,48,1152]{2,1,0:T(8,128)(2,1)S(1)}, u32[]{:S(2)}, u32[]{:S(2)}) %collective-permute-start.1) | collective-permute-done | bytes 221216 | tf_op jit(solution)/shard_map/ppermute | solution.py:360
  86.2 16.8 %collective-permute-done.2 = bf16[4,48,1152]{2,1,0:T(8,128)(2,1)S(1)} collective-permute-done((bf16[4,48,1152]{2,1,0:T(8,128)(2,1)S(1)}, bf16[4,48,1152]{2,1,0:T(8,128)(2,1)S(1)}, u32[]{:S(2)}, u32[]{:S(2)}) %collective-permute-start.2) | collective-permute-done | bytes 442400 | tf_op jit(solution)/shard_map/ppermute | solution.py:360
  105.9 17.2 %share_small.1 = (f32[16,8,128]{2,1,0:T(8,128)}, f32[24,128]{1,0:T(8,128)}) custom-call(f32[8,128]{1,0:T(8,128)} %pad.9.slice_ref, f32[24,128]{1,0:T(8,128)} %fusion.70.bias_ref), custom_call_target="tpu_custom_call" | custom-call | tf_op jit(solution)/shard_map/share_small/pallas_call | solution.py:320
  133.8 12.2 %all-to-all-start.1 = ((bf16[16,64,768]{2,1,0:T(8,128)(2,1)}), bf16[16,64,768]{2,1,0:T(8,128)(2,1)S(1)}, u32[]{:S(2)}, u32[]{:S(2)}) async-start(bf16[16,64,768]{2,1,0:T(8,128)(2,1)} %bitcast.194), calls=%async_computation.1 | async-start | bytes 3145728 | tf_op jit(solution)/shard_map/all_to_all | solution.py:490
  153.6 7.9 %add_convert_fusion.1.q_ref.kv_ref = bf16[1024,2304]{1,0:T(8,128)(2,1)} fusion(bf16[768,2304]{1,0:T(8,128)(2,1)} %bitcast.27, f32[2304]{0:T(1024)S(1)} %pad_maximum_fusion.8, f32[2304]{0:T(1024)S(1)} %copy-done.46, bf16[1024,768]{1,0:T(8,128)(2,1)S(1)} %bitcast.175, f32[768]{0:T(1024)S(1)} %add.200, f32[768]{0:T(1024)S(1)} %mul.173, ...), kind=kOutput, calls=%fused_computation.8 | convolution fusion | flops 3635675136 | bytes 9863168 | tf_op jit(solution)/shard_map/dot_general | solution.py:37
  161.5 21.3 %attend_own.1 = (f32[1024,768]{1,0:T(8,128)}, f32[1024,768]{1,0:T(8,128)}) custom-call(bf16[1024,2304]{1,0:T(8,128)(2,1)} %add_convert_fusion.1.q_ref.kv_ref, bf16[1024,2304]{1,0:T(8,128)(2,1)} %add_convert_fusion.1.q_ref.kv_ref), custom_call_target="tpu_custom_call" | custom-call | flops 12884901888 | bytes 4718592 | tf_op jit(solution)/shard_map/attend_own/pallas_call | solution.py:188
  183.8 6.0 %add_convert_fusion.2.kv_ref = bf16[1024,1536]{1,0:T(8,128)(2,1)} fusion(f32[1536]{0:T(1024)S(1)} %reshape.387, bf16[768,2304]{1,0:T(8,128)(2,1)} %bitcast.27, bf16[1024,768]{1,0:T(8,128)(2,1)S(1)} %collective-permute-done.5, f32[1024]{0:T(1024)S(1)} %add_rsqrt_fusion.1, f32[1024]{0:T(1024)S(1)} %broadcast_multiply_fusion.5, f32[768]{0:T(1024)S(1)} %add.200, ...), kind=kOutput, calls=%fused_computation.11 | convolution fusion | flops 2423783424 | bytes 7098368 | tf_op jit(solution)/shard_map/dot_general | solution.py:37
  189.8 7.6 %attend_pair.1 = (bf16[1024,768]{1,0:T(8,128)(2,1)}, f32[1024,768]{1,0:T(8,128)}) custom-call(s32[1]{0:T(128)S(6)} %convert_element_type.185.joined_ref, bf16[1024,2304]{1,0:T(8,128)(2,1)} %add_convert_fusion.1.q_ref.kv_ref, bf16[1024,1536]{1,0:T(8,128)(2,1)} %add_convert_fusion.2.kv_ref, f32[1024,768]{1,0:T(8,128)} %get-tuple-element.67.own_ref, ...), custom_call_target="tpu_custom_call" | custom-call | flops 12884901888 | bytes 4718592 | tf_op jit(solution)/shard_map/attend_pair/pallas_call | solution.py:205
  204.5 13.9 %add_convert_fusion = (bf16[1024,3072]{1,0:T(8,128)(2,1)}, bf16[1024,3072]{1,0:T(8,128)(2,1)}) fusion(f32[3072]{0:T(1024)S(1)} %maximum_select_fusion.10, bf16[768,6912]{1,0:T(8,128)(2,1)S(1)} %bitcast.212, f32[1024,768]{1,0:T(8,128)S(1)} %get-tuple-element.155, f32[768]{0:T(1024)S(1)} %add.218, f32[768]{0:T(1024)S(1)} %mul.188, ...), kind=kOutput, calls=%fused_computation.2 | convolution fusion | flops 4892393472 | bytes 20475904 | tf_op jit(solution)/shard_map/dot_general | solution.py:37
  218.4 7.2 %convert_reduce_fusion = (f32[3072]{0:T(1024)S(1)}, bf16[1024,3072]{1,0:T(8,128)(2,1)S(1)}) fusion(bf16[1024,3072]{1,0:T(8,128)(2,1)} %get-tuple-element.71, bf16[1024,768]{1,0:T(8,128)(2,1)S(1)} %bitcast.181, bf16[768,6912]{1,0:T(8,128)(2,1)S(1)} %bitcast.212), kind=kOutput, calls=%fused_computation | convolution fusion | flops 4847563776 | bytes 18886656 | tf_op jit(solution)/shard_map/dot_general | solution.py:37
  225.6 6.4 %convolution_convert_fusion = bf16[768,3072]{1,0:T(8,128)(2,1)S(1)} fusion(bf16[1024,3072]{1,0:T(8,128)(2,1)S(1)} %get-tuple-element.74, f32[1024,768]{1,0:T(8,128)S(1)} %get-tuple-element.155, f32[768]{0:T(1024)S(1)} %add.218, f32[768]{0:T(1024)S(1)} %mul.188, f32[1024]{0:T(1024)S(1)} %add_rsqrt_fusion, f32[1024]{0:T(1024)S(1)} %broadcast_multiply_fusion.4), kind=kOutput, calls=%fused_computation.12 | convolution fusion | flops 4838129664 | bytes 14170112 | tf_op jit(solution)/shard_map/dot_general | solution.py:37
  237.7 8.3 %multiply_reduce_fusion = (f32[768]{0:T(1024)S(1)}, f32[1024]{0:T(1024)S(1)}, f32[1024]{0:T(1024)S(1)}, f32[768]{0:T(1024)S(1)}, f32[1024,768]{1,0:T(8,128)S(1)}) fusion(f32[1024,768]{1,0:T(8,128)S(1)} %get-tuple-element.155, f32[1024]{0:T(1024)S(1)} %add_rsqrt_fusion, f32[1024]{0:T(1024)S(1)} %broadcast_multiply_fusion.4, f32[768]{0:T(1024)S(1)} %mul.188, ...), kind=kOutput, calls=%fused_computation.60 | convolution fusion | flops 4838912000 | bytes 17327104 | tf_op jit(solution)/shard_map/dot_general | solution.py:37
  250.4 8.1 %pad_maximum_fusion = bf16[768,6912]{1,0:T(8,128)(2,1)} fusion(bf16[768,768]{1,0:T(8,128)(2,1)S(1)} %convolution_convert_fusion.4, bf16[768,3072]{1,0:T(8,128)(2,1)S(1)} %convolution_convert_fusion, bf16[768,3072]{1,0:T(8,128)(2,1)S(1)} %convolution_convert_fusion.1), kind=kLoop, calls=%fused_computation.7 | loop fusion | flops 31850496 | bytes 21233664 | tf_op jit(solution)/shard_map/concatenate | solution.py:542
  262.9 9.5 %add_convert_fusion.4 = bf16[1024,768]{1,0:T(8,128)(2,1)} fusion(f32[1024,768]{1,0:T(8,128)S(1)} %copy-done.8, bf16[1024,3072]{1,0:T(8,128)(2,1)} %get-tuple-element.76, bf16[768,6912]{1,0:T(8,128)(2,1)} %all-gather.2.cloned.1.call-done, f32[768]{0:T(1024)S(1)} %add.229), kind=kOutput, calls=%fused_computation.62 | convolution fusion | flops 4834197504 | bytes 15731712 | tf_op jit(solution)/shard_map/dot_general | solution.py:37
  272.5 8.5 %attend_back_pair.1 = (f32[768,1024]{1,0:T(8,128)}, bf16[1024,1536]{1,0:T(8,128)(2,1)}) custom-call(s32[1]{0:T(128)S(6)} %convert_element_type.185.joined_ref, bf16[1024,2304]{1,0:T(8,128)(2,1)} %add_convert_fusion.1.q_ref.kv_ref, bf16[1024,768]{1,0:T(8,128)(2,1)} %convolution_convert_fusion.2.grad_ref, bf16[1024,768]{1,0:T(8,128)(2,1)} %get-tuple-element.69.mixed_ref, ...), custom_call_target="tpu_custom_call" | custom-call | flops 32212254720 | bytes 4718592 | tf_op jit(solution)/shard_map/attend_back_pair/pallas_call | solution.py:226
  280.9 6.5 %fusion.45 = bf16[1024,768]{1,0:T(8,128)(2,1)} fusion(bf16[1024,1536]{1,0:T(8,128)(2,1)} %get-tuple-element.83, bf16[768,2304]{1,0:T(8,128)(2,1)} %bitcast.27), kind=kOutput, calls=%fused_computation.84 | convolution fusion | flops 2416705536 | bytes 7077888 | tf_op jit(solution)/shard_map/dot_general | solution.py:37
  288.9 35.0 %attend_back_own.1 = (bf16[1024,768]{1,0:T(8,128)(2,1)}, bf16[1024,1536]{1,0:T(8,128)(2,1)}) custom-call(bf16[1024,2304]{1,0:T(8,128)(2,1)} %add_convert_fusion.1.q_ref.kv_ref, bf16[1024,768]{1,0:T(8,128)(2,1)} %convolution_convert_fusion.2.grad_ref, bf16[1024,768]{1,0:T(8,128)(2,1)} %get-tuple-element.69.mixed_ref, f32[1024,768]{1,0:T(8,128)} %get-tuple-element.79.lse_ref, ...), custom_call_target="tpu_custom_call" | custom-call | flops 32212254720 | bytes 4718592 | tf_op jit(solution)/shard_map/attend_back_own/pallas_call | solution.py:249
  329.4 5.8 %fusion.27 = (f32[768]{0:T(1024)S(1)}, f32[1024]{0:T(1024)S(1)}, f32[1024]{0:T(1024)S(1)}, f32[768]{0:T(1024)S(1)}, f32[1024,768]{1,0:T(8,128)S(1)}) fusion(bf16[1024,768]{1,0:T(8,128)(2,1)S(1)} %bitcast.177, f32[1024]{0:T(1024)S(1)} %copy-done.27, f32[1024]{0:T(1024)S(1)} %copy-done.22, f32[768]{0:T(1024)S(1)} %copy-done.25, ...), kind=kOutput, calls=%fused_computation.51 | convolution fusion | flops 2426139136 | bytes 14967808 | tf_op jit(solution)/shard_map/dot_general | solution.py:37
  357.0 42.0 %collective-permute-start.8 = (bf16[8,48,2304]{2,1,0:T(8,128)(2,1)}, bf16[8,48,2304]{2,1,0:T(8,128)(2,1)}, u32[]{:S(2)}, u32[]{:S(2)}) collective-permute-start(bf16[8,48,2304]{2,1,0:T(8,128)(2,1)} %select_bitcast_fusion), channel_id=1, source_target_pairs={{0,2},{2,0},{4,6},{6,4},{8,10},{10,8},{12,14},{14,12},{16,18},{18,... | collective-permute-start | bytes 5308424 | tf_op jit(solution)/shard_map/ppermute | solution.py:396
  399.0 6.3 %all-to-all-start.2 = ((bf16[16,64,768]{2,1,0:T(8,128)(2,1)}), bf16[16,64,768]{2,1,0:T(8,128)(2,1)}, u32[]{:S(2)}, u32[]{:S(2)}) async-start(bf16[16,64,768]{2,1,0:T(8,128)(2,1)} %bitcast.192), calls=%async_computation.2 | async-start | bytes 3145728 | tf_op jit(solution)/shard_map/all_to_all | solution.py:612
  412.0 20.9 %collective-permute-done.11 = f32[12,768]{1,0:T(8,128)S(1)} collective-permute-done((f32[12,768]{1,0:T(8,128)S(1)}, f32[12,768]{1,0:T(8,128)S(1)}, u32[]{:S(2)}, u32[]{:S(2)}) %collective-permute-start.11) | collective-permute-done | bytes 36896 | tf_op jit(solution)/shard_map/ppermute | solution.py:346
  437.5 9.0 %all-to-all-start.3 = ((bf16[16,64,768]{2,1,0:T(8,128)(2,1)}), bf16[16,64,768]{2,1,0:T(8,128)(2,1)S(1)}, u32[]{:S(2)}, u32[]{:S(2)}) async-start(bf16[16,64,768]{2,1,0:T(8,128)(2,1)} %bitcast.33), calls=%async_computation.3 | async-start | bytes 3145728 | tf_op jit(solution)/shard_map/all_to_all | solution.py:613
  448.7 24.1 %collective-permute-done.13 = f32[12,768]{1,0:T(8,128)S(1)} collective-permute-done((f32[12,768]{1,0:T(8,128)S(1)}, f32[12,768]{1,0:T(8,128)S(1)}, u32[]{:S(2)}, u32[]{:S(2)}) %collective-permute-start.13) | collective-permute-done | bytes 36896 | tf_op jit(solution)/shard_map/ppermute | solution.py:396
  (281 shorter events, 141.6 us)
Async XLA Ops:
  7.2 191.3 %all-gather.2.cloned.1.call-start = ((), (), s32[]{:S(2)}) async-start(), calls=%async_computation.5 | async-start | bytes 11280384 | tf_op jit(solution)/shard_map/all_gather | solution.py:472
  8.4 10.9 %collective-permute-start.6 = (bf16[48,3456]{1,0:T(8,128)(2,1)S(1)}, bf16[48,3456]{1,0:T(8,128)(2,1)S(1)}, u32[]{:S(2)}, u32[]{:S(2)}) collective-permute-start(bf16[48,3456]{1,0:T(8,128)(2,1)S(1)} %pad_maximum_fusion.4), channel_id=1, source_target_pairs={{0,1},{1,0},{2,3},{3,2},{4,5},{5,4},{6,7},{7,6},{8,9},{9,8},{10,11... | collective-permute-start | bytes 995336 | tf_op jit(solution)/shard_map/ppermute | solution.py:346
  22.6 10.1 %collective-permute-start = (bf16[1,48,1152]{2,1,0:T(8,128)(2,1)S(1)}, bf16[1,48,1152]{2,1,0:T(8,128)(2,1)S(1)}, u32[]{:S(2)}, u32[]{:S(2)}) collective-permute-start(bf16[1,48,1152]{2,1,0:T(8,128)(2,1)S(1)} %get-tuple-element.144), channel_id=1, source_target_pairs={{0,16},{2,18},{4,20},{6,22},{8,24},{10,26},{12,28},{14,30},{16,0},... | collective-permute-start | bytes 331784 | tf_op jit(solution)/shard_map/ppermute | solution.py:360
  28.6 102.0 %all-to-all-start = ((bf16[16,64,768]{2,1,0:T(8,128)(2,1)}), bf16[16,64,768]{2,1,0:T(8,128)(2,1)S(1)}, u32[]{:S(2)}, u32[]{:S(2)}) async-start(bf16[16,64,768]{2,1,0:T(8,128)(2,1)} %bitcast.1), calls=%async_computation | async-start | bytes 3145728 | tf_op jit(solution)/shard_map/all_to_all | solution.py:487
  32.8 51.6 %collective-permute-start.1 = (bf16[2,48,1152]{2,1,0:T(8,128)(2,1)S(1)}, bf16[2,48,1152]{2,1,0:T(8,128)(2,1)S(1)}, u32[]{:S(2)}, u32[]{:S(2)}) collective-permute-start(bf16[2,48,1152]{2,1,0:T(8,128)(2,1)S(1)} %maximum_select_fusion.7), channel_id=1, source_target_pairs={{0,8},{2,10},{4,12},{6,14},{8,0},{10,2},{12,4},{14,6},{16,24},{18,... | collective-permute-start | bytes 663560 | tf_op jit(solution)/shard_map/ppermute | solution.py:360
  84.4 18.5 %collective-permute-start.2 = (bf16[4,48,1152]{2,1,0:T(8,128)(2,1)S(1)}, bf16[4,48,1152]{2,1,0:T(8,128)(2,1)S(1)}, u32[]{:S(2)}, u32[]{:S(2)}) collective-permute-start(bf16[4,48,1152]{2,1,0:T(8,128)(2,1)S(1)} %bitcast.190), channel_id=1, source_target_pairs={{0,4},{2,6},{4,0},{6,2},{8,12},{10,14},{12,8},{14,10},{16,20},{18,... | collective-permute-start | bytes 1327112 | tf_op jit(solution)/shard_map/ppermute | solution.py:360
  103.0 22.0 %collective-permute-start.3 = (bf16[8,48,1152]{2,1,0:T(8,128)(2,1)S(1)}, bf16[8,48,1152]{2,1,0:T(8,128)(2,1)S(1)}, u32[]{:S(2)}, u32[]{:S(2)}) collective-permute-start(bf16[8,48,1152]{2,1,0:T(8,128)(2,1)S(1)} %bitcast.187), channel_id=1, source_target_pairs={{0,1},{1,0},{2,3},{3,2},{4,5},{5,4},{6,7},{7,6},{8,9},{9,8},{10,11... | collective-permute-start | bytes 2654216 | tf_op jit(solution)/shard_map/ppermute | solution.py:346
  127.5 21.0 %collective-permute-start.4 = (bf16[8,48,2304]{2,1,0:T(8,128)(2,1)}, bf16[8,48,2304]{2,1,0:T(8,128)(2,1)}, u32[]{:S(2)}, u32[]{:S(2)}) collective-permute-start(bf16[8,48,2304]{2,1,0:T(8,128)(2,1)} %get-tuple-element.130), channel_id=1, source_target_pairs={{0,2},{2,0},{4,6},{6,4},{8,10},{10,8},{12,14},{14,12},{16,18},{18,... | collective-permute-start | bytes 5308424 | tf_op jit(solution)/shard_map/ppermute | solution.py:371
  133.8 63.6 %all-to-all-start.1 = ((bf16[16,64,768]{2,1,0:T(8,128)(2,1)}), bf16[16,64,768]{2,1,0:T(8,128)(2,1)S(1)}, u32[]{:S(2)}, u32[]{:S(2)}) async-start(bf16[16,64,768]{2,1,0:T(8,128)(2,1)} %bitcast.194), calls=%async_computation.1 | async-start | bytes 3145728 | tf_op jit(solution)/shard_map/all_to_all | solution.py:490
  146.0 352.3 %reduce-scatter.2.cloned.1.call-start = ((), (), s32[]{:S(2)}) async-start(), calls=%async_computation.6 | async-start | bytes 11280384 | tf_op jit(solution)/shard_map/reduce_scatter | solution.py:443
  146.1 36.8 %collective-permute-start.5 = (bf16[1024,768]{1,0:T(8,128)(2,1)S(1)}, bf16[1024,768]{1,0:T(8,128)(2,1)S(1)}, u32[]{:S(2)}, u32[]{:S(2)}) collective-permute-start(bf16[1024,768]{1,0:T(8,128)(2,1)S(1)} %bitcast.172), channel_id=1, source_target_pairs={{0,1},{1,0},{2,3},{3,2},{4,5},{5,4},{6,7},{7,6},{8,9},{9,8},{10,11... | collective-permute-start | bytes 4718600 | tf_op jit(solution)/shard_map/ppermute | solution.py:346
  287.4 41.9 %collective-permute-start.7 = (bf16[1024,768]{1,0:T(8,128)(2,1)}, bf16[1024,768]{1,0:T(8,128)(2,1)}, u32[]{:S(2)}, u32[]{:S(2)}) collective-permute-start(bf16[1024,768]{1,0:T(8,128)(2,1)} %fusion.45), channel_id=1, source_target_pairs={{0,1},{1,0},{2,3},{3,2},{4,5},{5,4},{6,7},{7,6},{8,9},{9,8},{10,11... | collective-permute-start | bytes 4718600 | tf_op jit(solution)/shard_map/ppermute | solution.py:346
  357.0 49.8 %collective-permute-start.8 = (bf16[8,48,2304]{2,1,0:T(8,128)(2,1)}, bf16[8,48,2304]{2,1,0:T(8,128)(2,1)}, u32[]{:S(2)}, u32[]{:S(2)}) collective-permute-start(bf16[8,48,2304]{2,1,0:T(8,128)(2,1)} %select_bitcast_fusion), channel_id=1, source_target_pairs={{0,2},{2,0},{4,6},{6,4},{8,10},{10,8},{12,14},{14,12},{16,18},{18,... | collective-permute-start | bytes 5308424 | tf_op jit(solution)/shard_map/ppermute | solution.py:396
  399.0 38.5 %all-to-all-start.2 = ((bf16[16,64,768]{2,1,0:T(8,128)(2,1)}), bf16[16,64,768]{2,1,0:T(8,128)(2,1)}, u32[]{:S(2)}, u32[]{:S(2)}) async-start(bf16[16,64,768]{2,1,0:T(8,128)(2,1)} %bitcast.192), calls=%async_computation.2 | async-start | bytes 3145728 | tf_op jit(solution)/shard_map/all_to_all | solution.py:612
  409.9 23.0 %collective-permute-start.10 = (bf16[8,48,1152]{2,1,0:T(8,128)(2,1)S(1)}, bf16[8,48,1152]{2,1,0:T(8,128)(2,1)S(1)}, u32[]{:S(2)}, u32[]{:S(2)}) collective-permute-start(bf16[8,48,1152]{2,1,0:T(8,128)(2,1)S(1)} %broadcast_select_fusion), channel_id=1, source_target_pairs={{0,1},{1,0},{2,3},{3,2},{4,5},{5,4},{6,7},{7,6},{8,9},{9,8},{10,11... | collective-permute-start | bytes 2654216 | tf_op jit(solution)/shard_map/ppermute | solution.py:346
  410.7 22.2 %collective-permute-start.11 = (f32[12,768]{1,0:T(8,128)S(1)}, f32[12,768]{1,0:T(8,128)S(1)}, u32[]{:S(2)}, u32[]{:S(2)}) collective-permute-start(f32[12,768]{1,0:T(8,128)S(1)} %add.239), channel_id=1, source_target_pairs={{0,1},{1,0},{2,3},{3,2},{4,5},{5,4},{6,7},{7,6},{8,9},{9,8},{10,11... | collective-permute-start | bytes 110600 | tf_op jit(solution)/shard_map/ppermute | solution.py:346
  437.5 51.4 %all-to-all-start.3 = ((bf16[16,64,768]{2,1,0:T(8,128)(2,1)}), bf16[16,64,768]{2,1,0:T(8,128)(2,1)S(1)}, u32[]{:S(2)}, u32[]{:S(2)}) async-start(bf16[16,64,768]{2,1,0:T(8,128)(2,1)} %bitcast.33), calls=%async_computation.3 | async-start | bytes 3145728 | tf_op jit(solution)/shard_map/all_to_all | solution.py:613
  446.6 26.2 %collective-permute-start.12 = (bf16[4,48,1152]{2,1,0:T(8,128)(2,1)S(1)}, bf16[4,48,1152]{2,1,0:T(8,128)(2,1)S(1)}, u32[]{:S(2)}, u32[]{:S(2)}) collective-permute-start(bf16[4,48,1152]{2,1,0:T(8,128)(2,1)S(1)} %fusion.59), channel_id=1, source_target_pairs={{0,4},{2,6},{4,0},{6,2},{8,12},{10,14},{12,8},{14,10},{16,20},{18,... | collective-permute-start | bytes 1327112 | tf_op jit(solution)/shard_map/ppermute | solution.py:396
  448.6 24.2 %collective-permute-start.13 = (f32[12,768]{1,0:T(8,128)S(1)}, f32[12,768]{1,0:T(8,128)S(1)}, u32[]{:S(2)}, u32[]{:S(2)}) collective-permute-start(f32[12,768]{1,0:T(8,128)S(1)} %add.241), channel_id=1, source_target_pairs={{0,4},{2,6},{4,0},{6,2},{8,12},{10,14},{12,8},{14,10},{16,20},{18,... | collective-permute-start | bytes 110600 | tf_op jit(solution)/shard_map/ppermute | solution.py:396
  473.0 8.2 %collective-permute-start.15 = (f32[12,768]{1,0:T(8,128)S(1)}, f32[12,768]{1,0:T(8,128)S(1)}, u32[]{:S(2)}, u32[]{:S(2)}) collective-permute-start(f32[12,768]{1,0:T(8,128)S(1)} %add.243), channel_id=1, source_target_pairs={{0,8},{2,10},{4,12},{6,14},{8,0},{10,2},{12,4},{14,6},{16,24},{18,... | collective-permute-start | bytes 110600 | tf_op jit(solution)/shard_map/ppermute | solution.py:396
  474.9 10.5 %collective-permute-start.14 = (bf16[2,48,1152]{2,1,0:T(8,128)(2,1)S(1)}, bf16[2,48,1152]{2,1,0:T(8,128)(2,1)S(1)}, u32[]{:S(2)}, u32[]{:S(2)}) collective-permute-start(bf16[2,48,1152]{2,1,0:T(8,128)(2,1)S(1)} %fusion.62), channel_id=1, source_target_pairs={{0,8},{2,10},{4,12},{6,14},{8,0},{10,2},{12,4},{14,6},{16,24},{18,... | collective-permute-start | bytes 663560 | tf_op jit(solution)/shard_map/ppermute | solution.py:396
  485.5 6.9 %collective-permute-start.17 = (f32[12,768]{1,0:T(8,128)S(1)}, f32[12,768]{1,0:T(8,128)S(1)}, u32[]{:S(2)}, u32[]{:S(2)}) collective-permute-start(f32[12,768]{1,0:T(8,128)S(1)} %add.245), channel_id=1, source_target_pairs={{0,16},{2,18},{4,20},{6,22},{8,24},{10,26},{12,28},{14,30},{16,0},... | collective-permute-start | bytes 110600 | tf_op jit(solution)/shard_map/ppermute | solution.py:396
  488.8 7.9 %collective-permute-start.16 = (bf16[1,48,1152]{2,1,0:T(8,128)(2,1)S(1)}, bf16[1,48,1152]{2,1,0:T(8,128)(2,1)S(1)}, u32[]{:S(2)}, u32[]{:S(2)}) collective-permute-start(bf16[1,48,1152]{2,1,0:T(8,128)(2,1)S(1)} %select_bitcast_fusion.1), channel_id=1, source_target_pairs={{0,16},{2,18},{4,20},{6,22},{8,24},{10,26},{12,28},{14,30},{16,0},... | collective-permute-start | bytes 331784 | tf_op jit(solution)/shard_map/ppermute | solution.py:396
  500.3 7.2 %collective-permute-start.18 = (bf16[48,3456]{1,0:T(8,128)(2,1)S(1)}, bf16[48,3456]{1,0:T(8,128)(2,1)S(1)}, u32[]{:S(2)}, u32[]{:S(2)}) collective-permute-start(bf16[48,3456]{1,0:T(8,128)(2,1)S(1)} %pad_maximum_fusion.5), channel_id=1, source_target_pairs={{0,1},{1,0},{2,3},{3,2},{4,5},{5,4},{6,7},{7,6},{8,9},{9,8},{10,11... | collective-permute-start | bytes 995336 | tf_op jit(solution)/shard_map/ppermute | solution.py:346
  (54 other events, 1152.2 us)
Sparse Core Ops, SparseCore 0:
  22.5 124.5 all-gather.1
  272.6 137.2 reduce-scatter.1

commit v6 on v5

--- a/solution.py
+++ b/solution.py
@@ -374,36 +374,49 @@
     return full
 
 
-def tree_sum(n_dp, piece, t, values, rows):
+def dp_partners(n_dp, step):
+    return [(i, i ^ step) for i in range(n_dp)]
+
+
+def add_half(first, second, upper, exchange):
+    mine = jnp.where(upper, second, first)
+    arrived = exchange(jnp.where(upper, first, second))
+    return (mine.astype(F32) + arrived.astype(F32)).astype(BF16)
+
+
+def sum_on_chip(n_dp, piece, values):
+    odd = lax.axis_index("dp") % 2 == 1
+    blocks = values.reshape(n_dp // 2, 2, piece, values.shape[-1])
+    return add_half(
+        blocks[:, 0], blocks[:, 1], odd, lambda v: lax.ppermute(v, "dp", dp_partners(n_dp, 1))
+    )
+
+
+def sum_over_tensor(t, values):
+    low, high = jnp.split(values, 2, axis=-1)
+    return add_half(low, high, t == 1, swap)
+
+
+def tree_sum(n_dp, piece, total, rows):
     me = lax.axis_index("dp")
-    columns = values.shape[1]
-
-    def add(first, second, upper, rows, exchange):
-        mine = jnp.where(upper, second, first)
-        sent, rows = after(jnp.where(upper, first, second), rows)
-        arrived, arrived_rows = after(exchange(sent), exchange(rows))
-        total = (mine.astype(F32) + arrived.astype(F32)).astype(BF16)
-        return total, rows + arrived_rows
-
-    def along_dp(total, rows, step):
-        blocks = total.reshape(-1, 2, piece, total.shape[-1])
-        partners = [(i, i ^ step) for i in range(n_dp)]
-        return add(
-            blocks[:, 0],
-            blocks[:, 1],
-            (me // step) % 2 == 1,
-            rows,
-            lambda v: lax.ppermute(v, "dp", partners),
-        )
-
-    total, rows = along_dp(values, rows, 1)
-    low, high = total[..., : columns // 2], total[..., columns // 2 :]
-    total, rows = add(low, high, t == 1, rows, swap)
+    arrived_rows = lax.ppermute(rows, "dp", dp_partners(n_dp, 1))
+    rows = rows + arrived_rows
+    arrived_rows = swap(rows)
+    rows = rows + arrived_rows
     step = 2
     while step < n_dp:
-        total, rows = along_dp(total, rows, step)
+        blocks = total.reshape(-1, 2, piece, total.shape[-1])
+        upper = (me // step) % 2 == 1
+        sent, rows = after(jnp.where(upper, blocks[:, 0], blocks[:, 1]), rows)
+        partners = dp_partners(n_dp, step)
+        arrived, arrived_rows = after(
+            lax.ppermute(sent, "dp", partners), lax.ppermute(rows, "dp", partners)
+        )
+        mine = jnp.where(upper, blocks[:, 1], blocks[:, 0])
+        total = (mine.astype(F32) + arrived.astype(F32)).astype(BF16)
+        rows = rows + arrived_rows
         step *= 2
-    return total.reshape(piece, columns // 2).astype(F32), rows
+    return total.reshape(piece, -1).astype(F32), rows
 
 
 def per_device(
@@ -552,20 +565,19 @@
     for_pair = mm(pair_dkv, wkv, 1, 1).astype(BF16)
     for_pair = swap(for_pair)
     dq, dkv = attention_back_own(qkv, grad_att, attended, lse, pair_dq)
+    grad_wq = mm(ln_one, dq, 0, 0).astype(BF16)
+    grad_wkv = (mm(ln_one, dkv, 0, 0) + mm(ln_of_pair, pair_dkv, 0, 0)).astype(BF16)
+    dq, dkv, grad_wq, grad_wkv = after(dq, dkv, grad_wq, grad_wkv)
+    wq_sum = sum_on_chip(n_dp, piece, grad_wq)
+    wkv_sum = sum_on_chip(n_dp, piece, grad_wkv)
+    wqkv_sum = jnp.concatenate([sum_over_tensor(t, wq_sum), sum_over_tensor(t, wkv_sum)], axis=-1)
     grad_ln_one = by_rows(mm(dq, wq, 1, 1) + mm(dkv, wkv, 1, 1) + for_pair.astype(F32))
     grad_input = (
         grad_hidden + norm_back(grad_ln_one, normed_one, factor_one, small_full[0])
     ).astype(BF16)
-    dq, dkv, grad_input = after(dq, dkv, grad_input)
-    grad_wq = mm(ln_one, dq, 0, 0).astype(BF16)
-    grad_wkv = (mm(ln_one, dkv, 0, 0) + mm(ln_of_pair, pair_dkv, 0, 0)).astype(BF16)
     bias_q_grad = jnp.sum(dq, axis=0, dtype=F32)
     kv_sum = jnp.sum(dkv, axis=0, dtype=F32) + jnp.sum(pair_dkv, axis=0, dtype=F32)
     bias_v_grad = kv_sum.reshape(pairs, 2, LANES)[:, 1].reshape(-1)
-    grad_wqkv = jnp.concatenate(
-        [grad_wq[:, :half], grad_wkv[:, : 2 * half], grad_wq[:, half:], grad_wkv[:, 2 * half :]],
-        axis=1,
-    )
     row_sums = jnp.concatenate(
         [
             jnp.stack(
@@ -583,7 +595,7 @@
             bias_up_grad.reshape(-1, width),
         ]
     )
-    qkv_part, row_sums = tree_sum(n_dp, piece, t, grad_wqkv, row_sums)
+    qkv_part, row_sums = tree_sum(n_dp, piece, wqkv_sum, row_sums)
     small_part = lax.dynamic_slice_in_dim(
         row_sums[:6], lax.axis_index("dp") * piece, piece, 1
     )
@@ -597,7 +609,8 @@
             start += size
         mine = jnp.concatenate([c[0] for c in columns], axis=1)
         other = jnp.concatenate([c[1] for c in columns], axis=1)
-        total = mine.astype(F32) + swap(other).astype(F32)
+        other = swap(other)
+        total = mine.astype(F32) + other.astype(F32)
         cuts = [sum(sizes[:i]) // 2 for i in range(1, len(sizes))]
         return jnp.split(total, cuts, axis=1)
 

time: 524 us -> 529 us (level)
  the two profiles are of different devices: /device:TPU:0 before, /device:TPU:11 now
where the time goes in v6:
time: 529 us; the launch traced here: 522 us
  waiting for transfers between devices  150 us (28%)
  Pallas kernels  134 us (25%)
  matrix products  112 us (21%)
  other arithmetic  50.4 us (10%)
  starting transfers between devices  43 us (8%)
  between operations  16.9 us (3%)
  local copies, waits for them, and re-layouts  15.4 us (3%)
    dot_general x21, matrix products, mm(): lax.dot_general(left, right, (((left_dim,), (right_dim,)), ((), ())), pre...  112 us
    ppermute x3, waiting for transfers between devices, tree_gather(): other = lax.ppermute(blocks, 'dp', [(i, i ^ step) for i in range(n_dp)])  74.7 us
    pallas_call x1, Pallas kernels, attention_back_pair(): pl.pallas_call(functools.partial(pair_backward, kblock=min(512, rows)), g...  35.5 us
    pallas_call x1, Pallas kernels, attention_back_own(): pl.pallas_call(functools.partial(own_backward, kblock=min(512, rows)), gr...  35.1 us
    all_to_all x1, waiting for transfers between devices, per_device(): lax.all_to_all(grad_input, 'dp', split_axis=0, concat_axis=0, tiled=True)  25.7 us
    ppermute x3, waiting for transfers between devices, tree_sum(): lax.ppermute(rows, 'dp', partners)  25.4 us
    pallas_call x1, Pallas kernels, attention_pair(): pl.pallas_call(functools.partial(pair_forward, qblock=min(512, rows)), gr...  23.1 us
    pallas_call x1, Pallas kernels, attention_own(): pl.pallas_call(functools.partial(own_forward, qblock=min(512, rows)), gri...  21.3 us
  transfers between devices with their start and end apart: 27, of which 12 were waited for; matrix products, arithmetic and copies ran while one was open for 18% of the time, Pallas kernels for 26%

profile of v6, /device:TPU:11, one launch (start us, length us, event | category | flops | bytes accessed | tf_op | source)
XLA Modules:
  0.0 522.0 jit_solution(10933028385019253862)
XLA Ops:
  9.7 7.4 %collective-permute-done.6 = bf16[48,3456]{1,0:T(8,128)(2,1)S(1)} collective-permute-done((bf16[48,3456]{1,0:T(8,128)(2,1)S(1)}, bf16[48,3456]{1,0:T(8,128)(2,1)S(1)}, u32[]{:S(2)}, u32[]{:S(2)}) %collective-permute-start.6) | collective-permute-done | bytes 331808 | tf_op jit(solution)/shard_map/ppermute | solution.py:346
  26.0 5.6 %all-to-all-start = ((bf16[16,64,768]{2,1,0:T(8,128)(2,1)}), bf16[16,64,768]{2,1,0:T(8,128)(2,1)S(1)}, u32[]{:S(2)}, u32[]{:S(2)}) async-start(bf16[16,64,768]{2,1,0:T(8,128)(2,1)} %bitcast.1), calls=%async_computation | async-start | bytes 3145728 | tf_op jit(solution)/shard_map/all_to_all | solution.py:500
  32.2 51.9 %collective-permute-done.1 = bf16[2,48,1152]{2,1,0:T(8,128)(2,1)S(1)} collective-permute-done((bf16[2,48,1152]{2,1,0:T(8,128)(2,1)S(1)}, bf16[2,48,1152]{2,1,0:T(8,128)(2,1)S(1)}, u32[]{:S(2)}, u32[]{:S(2)}) %collective-permute-start.1) | collective-permute-done | bytes 221216 | tf_op jit(solution)/shard_map/ppermute | solution.py:360
  84.4 22.8 %collective-permute-done.2 = bf16[4,48,1152]{2,1,0:T(8,128)(2,1)S(1)} collective-permute-done((bf16[4,48,1152]{2,1,0:T(8,128)(2,1)S(1)}, bf16[4,48,1152]{2,1,0:T(8,128)(2,1)S(1)}, u32[]{:S(2)}, u32[]{:S(2)}) %collective-permute-start.2) | collective-permute-done | bytes 442400 | tf_op jit(solution)/shard_map/ppermute | solution.py:360
  109.9 19.1 %share_small.1 = (f32[16,8,128]{2,1,0:T(8,128)}, f32[24,128]{1,0:T(8,128)}) custom-call(f32[8,128]{1,0:T(8,128)} %pad.9.slice_ref, f32[24,128]{1,0:T(8,128)} %fusion.66.bias_ref), custom_call_target="tpu_custom_call" | custom-call | tf_op jit(solution)/shard_map/share_small/pallas_call | solution.py:320
  152.2 5.9 %add_convert_fusion.1.q_ref.kv_ref = bf16[1024,2304]{1,0:T(8,128)(2,1)} fusion(bf16[768,2304]{1,0:T(8,128)(2,1)S(1)} %bitcast.199, f32[2304]{0:T(1024)S(1)} %pad_maximum_fusion.8, f32[2304]{0:T(1024)S(1)} %copy-done.50, bf16[1024,768]{1,0:T(8,128)(2,1)S(1)} %bitcast.184, f32[768]{0:T(1024)S(1)} %add.206, f32[768]{0:T(1024)S(1)} %mul.173, ...), kind=kOutput, calls=%fused_computation.8 | convolution fusion | flops 3635675136 | bytes 9863168 | tf_op jit(solution)/shard_map/dot_general | solution.py:37
  158.2 21.3 %attend_own.1 = (f32[1024,768]{1,0:T(8,128)}, f32[1024,768]{1,0:T(8,128)}) custom-call(bf16[1024,2304]{1,0:T(8,128)(2,1)} %add_convert_fusion.1.q_ref.kv_ref, bf16[1024,2304]{1,0:T(8,128)(2,1)} %add_convert_fusion.1.q_ref.kv_ref), custom_call_target="tpu_custom_call" | custom-call | flops 12884901888 | bytes 4718592 | tf_op jit(solution)/shard_map/attend_own/pallas_call | solution.py:188
  182.4 6.0 %add_convert_fusion.2.kv_ref = bf16[1024,1536]{1,0:T(8,128)(2,1)} fusion(f32[1536]{0:T(1024)S(1)} %reshape.396, bf16[768,2304]{1,0:T(8,128)(2,1)} %bitcast.200, bf16[1024,768]{1,0:T(8,128)(2,1)S(1)} %collective-permute-done.5, f32[1024]{0:T(1024)S(1)} %add_rsqrt_fusion.1, f32[1024]{0:T(1024)S(1)} %broadcast_multiply_fusion.5, f32[768]{0:T(1024)S(1)} %add.206, ...), kind=kOutput, calls=%fused_computation.11 | convolution fusion | flops 2423783424 | bytes 7098368 | tf_op jit(solution)/shard_map/dot_general | solution.py:37
  188.4 23.1 %attend_pair.1 = (bf16[1024,768]{1,0:T(8,128)(2,1)}, f32[1024,768]{1,0:T(8,128)}) custom-call(s32[1]{0:T(128)S(6)} %convert_element_type.206.joined_ref, bf16[1024,2304]{1,0:T(8,128)(2,1)} %add_convert_fusion.1.q_ref.kv_ref, bf16[1024,1536]{1,0:T(8,128)(2,1)} %add_convert_fusion.2.kv_ref, f32[1024,768]{1,0:T(8,128)} %get-tuple-element.60.own_ref, ...), custom_call_target="tpu_custom_call" | custom-call | flops 12884901888 | bytes 4718592 | tf_op jit(solution)/shard_map/attend_pair/pallas_call | solution.py:205
  218.7 13.7 %add_convert_fusion = (bf16[1024,3072]{1,0:T(8,128)(2,1)}, bf16[1024,3072]{1,0:T(8,128)(2,1)}) fusion(f32[3072]{0:T(1024)S(1)} %maximum_select_fusion.10, bf16[768,6912]{1,0:T(8,128)(2,1)S(1)} %bitcast.229, f32[1024,768]{1,0:T(8,128)S(1)} %get-tuple-element.137, f32[768]{0:T(1024)S(1)} %add.224, f32[768]{0:T(1024)S(1)} %mul.188, ...), kind=kOutput, calls=%fused_computation.2 | convolution fusion | flops 4892393472 | bytes 20475904 | tf_op jit(solution)/shard_map/dot_general | solution.py:37
  232.4 7.2 %convert_reduce_fusion = (f32[3072]{0:T(1024)S(1)}, bf16[1024,3072]{1,0:T(8,128)(2,1)S(1)}) fusion(bf16[1024,3072]{1,0:T(8,128)(2,1)} %get-tuple-element.64, bf16[1024,768]{1,0:T(8,128)(2,1)S(1)} %bitcast.190, bf16[768,6912]{1,0:T(8,128)(2,1)S(1)} %bitcast.229), kind=kOutput, calls=%fused_computation | convolution fusion | flops 4847563776 | bytes 18886656 | tf_op jit(solution)/shard_map/dot_general | solution.py:37
  239.6 6.4 %convolution_convert_fusion = bf16[768,3072]{1,0:T(8,128)(2,1)S(1)} fusion(bf16[1024,3072]{1,0:T(8,128)(2,1)S(1)} %get-tuple-element.67, f32[1024,768]{1,0:T(8,128)S(1)} %get-tuple-element.137, f32[768]{0:T(1024)S(1)} %add.224, f32[768]{0:T(1024)S(1)} %mul.188, f32[1024]{0:T(1024)S(1)} %add_rsqrt_fusion, f32[1024]{0:T(1024)S(1)} %broadcast_multiply_fusion.4), kind=kOutput, calls=%fused_computation.12 | convolution fusion | flops 4838129664 | bytes 14170112 | tf_op jit(solution)/shard_map/dot_general | solution.py:37
  251.6 8.3 %multiply_reduce_fusion = (f32[768]{0:T(1024)S(1)}, f32[1024]{0:T(1024)S(1)}, f32[1024]{0:T(1024)S(1)}, f32[768]{0:T(1024)S(1)}, f32[1024,768]{1,0:T(8,128)S(1)}) fusion(f32[1024,768]{1,0:T(8,128)S(1)} %get-tuple-element.137, f32[1024]{0:T(1024)S(1)} %add_rsqrt_fusion, f32[1024]{0:T(1024)S(1)} %broadcast_multiply_fusion.4, f32[768]{0:T(1024)S(1)} %mul.188, ...), kind=kOutput, calls=%fused_computation.57 | convolution fusion | flops 4838912000 | bytes 17327104 | tf_op jit(solution)/shard_map/dot_general | solution.py:37
  264.4 8.0 %pad_maximum_fusion = bf16[768,6912]{1,0:T(8,128)(2,1)} fusion(bf16[768,768]{1,0:T(8,128)(2,1)S(1)} %convolution_convert_fusion.4, bf16[768,3072]{1,0:T(8,128)(2,1)S(1)} %convolution_convert_fusion, bf16[768,3072]{1,0:T(8,128)(2,1)S(1)} %convolution_convert_fusion.1), kind=kLoop, calls=%fused_computation.7 | loop fusion | flops 31850496 | bytes 21233664 | tf_op jit(solution)/shard_map/concatenate | solution.py:555
  276.8 9.5 %add_convert_fusion.4 = bf16[1024,768]{1,0:T(8,128)(2,1)} fusion(f32[1024,768]{1,0:T(8,128)S(1)} %copy-done.9, bf16[1024,3072]{1,0:T(8,128)(2,1)} %get-tuple-element.69, bf16[768,6912]{1,0:T(8,128)(2,1)} %all-gather.2.cloned.1.call-done, f32[768]{0:T(1024)S(1)} %add.235), kind=kOutput, calls=%fused_computation.59 | convolution fusion | flops 4834197504 | bytes 15731712 | tf_op jit(solution)/shard_map/dot_general | solution.py:37
  286.3 35.5 %attend_back_pair.1 = (f32[768,1024]{1,0:T(8,128)}, bf16[1024,1536]{1,0:T(8,128)(2,1)}) custom-call(s32[1]{0:T(128)S(6)} %convert_element_type.206.joined_ref, bf16[1024,2304]{1,0:T(8,128)(2,1)} %add_convert_fusion.1.q_ref.kv_ref, bf16[1024,768]{1,0:T(8,128)(2,1)} %convolution_convert_fusion.2.grad_ref, bf16[1024,768]{1,0:T(8,128)(2,1)} %get-tuple-element.62.mixed_ref, ...), custom_call_target="tpu_custom_call" | custom-call | flops 32212254720 | bytes 4718592 | tf_op jit(solution)/shard_map/attend_back_pair/pallas_call | solution.py:226
  321.8 6.0 %fusion.45 = bf16[1024,768]{1,0:T(8,128)(2,1)} fusion(bf16[1024,1536]{1,0:T(8,128)(2,1)} %get-tuple-element.76, bf16[768,2304]{1,0:T(8,128)(2,1)S(1)} %bitcast.202), kind=kOutput, calls=%fused_computation.79 | convolution fusion | flops 2416705536 | bytes 7077888 | tf_op jit(solution)/shard_map/dot_general | solution.py:37
  329.0 35.1 %attend_back_own.1 = (bf16[1024,768]{1,0:T(8,128)(2,1)}, bf16[1024,1536]{1,0:T(8,128)(2,1)}) custom-call(bf16[1024,2304]{1,0:T(8,128)(2,1)} %add_convert_fusion.1.q_ref.kv_ref, bf16[1024,768]{1,0:T(8,128)(2,1)} %convolution_convert_fusion.2.grad_ref, bf16[1024,768]{1,0:T(8,128)(2,1)} %get-tuple-element.62.mixed_ref, f32[1024,768]{1,0:T(8,128)} %get-tuple-element.72.lse_ref, ...), custom_call_target="tpu_custom_call" | custom-call | flops 32212254720 | bytes 4718592 | tf_op jit(solution)/shard_map/attend_back_own/pallas_call | solution.py:249
  404.2 7.0 %collective-permute-done.13 = f32[12,768]{1,0:T(8,128)S(1)} collective-permute-done((f32[12,768]{1,0:T(8,128)S(1)}, f32[12,768]{1,0:T(8,128)S(1)}, u32[]{:S(2)}, u32[]{:S(2)}) %collective-permute-start.13) | collective-permute-done | bytes 36896 | tf_op jit(solution)/shard_map/ppermute | solution.py:346
  415.8 6.9 %all-to-all-start.2 = ((bf16[16,64,768]{2,1,0:T(8,128)(2,1)}), bf16[16,64,768]{2,1,0:T(8,128)(2,1)}, u32[]{:S(2)}, u32[]{:S(2)}) async-start(bf16[16,64,768]{2,1,0:T(8,128)(2,1)} %bitcast.209), calls=%async_computation.2 | async-start | bytes 3145728 | tf_op jit(solution)/shard_map/all_to_all | solution.py:625
  423.1 13.5 %collective-permute-done.15 = f32[12,768]{1,0:T(8,128)S(1)} collective-permute-done((f32[12,768]{1,0:T(8,128)S(1)}, f32[12,768]{1,0:T(8,128)S(1)}, u32[]{:S(2)}, u32[]{:S(2)}) %collective-permute-start.15) | collective-permute-done | bytes 36896 | tf_op jit(solution)/shard_map/ppermute | solution.py:413
  439.6 10.9 %collective-permute-done.17 = f32[12,768]{1,0:T(8,128)S(1)} collective-permute-done((f32[12,768]{1,0:T(8,128)S(1)}, f32[12,768]{1,0:T(8,128)S(1)}, u32[]{:S(2)}, u32[]{:S(2)}) %collective-permute-start.17) | collective-permute-done | bytes 36896 | tf_op jit(solution)/shard_map/ppermute | solution.py:413
  465.4 7.3 %all-to-all-start.3 = ((bf16[16,64,768]{2,1,0:T(8,128)(2,1)}), bf16[16,64,768]{2,1,0:T(8,128)(2,1)S(1)}, u32[]{:S(2)}, u32[]{:S(2)}) async-start(bf16[16,64,768]{2,1,0:T(8,128)(2,1)} %bitcast.194), calls=%async_computation.3 | async-start | bytes 3145728 | tf_op jit(solution)/shard_map/all_to_all | solution.py:626
  483.2 25.7 %all-to-all-done.3 = bf16[16,64,768]{2,1,0:T(8,128)(2,1)S(1)} async-done(((bf16[16,64,768]{2,1,0:T(8,128)(2,1)}), bf16[16,64,768]{2,1,0:T(8,128)(2,1)S(1)}, u32[]{:S(2)}, u32[]{:S(2)}) %all-to-all-start.3) | async-done | bytes 1572896 | tf_op jit(solution)/shard_map/all_to_all | solution.py:626
  (295 shorter events, 141.0 us)
Async XLA Ops:
  7.2 205.4 %all-gather.2.cloned.1.call-start = ((), (), s32[]{:S(2)}) async-start(), calls=%async_computation.5 | async-start | bytes 11280384 | tf_op jit(solution)/shard_map/all_gather | solution.py:485
  8.4 8.7 %collective-permute-start.6 = (bf16[48,3456]{1,0:T(8,128)(2,1)S(1)}, bf16[48,3456]{1,0:T(8,128)(2,1)S(1)}, u32[]{:S(2)}, u32[]{:S(2)}) collective-permute-start(bf16[48,3456]{1,0:T(8,128)(2,1)S(1)} %pad_maximum_fusion.4), channel_id=1, source_target_pairs={{0,1},{1,0},{2,3},{3,2},{4,5},{5,4},{6,7},{7,6},{8,9},{9,8},{10,11... | collective-permute-start | bytes 995336 | tf_op jit(solution)/shard_map/ppermute | solution.py:346
  20.5 11.3 %collective-permute-start = (bf16[1,48,1152]{2,1,0:T(8,128)(2,1)S(1)}, bf16[1,48,1152]{2,1,0:T(8,128)(2,1)S(1)}, u32[]{:S(2)}, u32[]{:S(2)}) collective-permute-start(bf16[1,48,1152]{2,1,0:T(8,128)(2,1)S(1)} %get-tuple-element.126), channel_id=1, source_target_pairs={{0,16},{2,18},{4,20},{6,22},{8,24},{10,26},{12,28},{14,30},{16,0},... | collective-permute-start | bytes 331784 | tf_op jit(solution)/shard_map/ppermute | solution.py:360
  26.0 112.2 %all-to-all-start = ((bf16[16,64,768]{2,1,0:T(8,128)(2,1)}), bf16[16,64,768]{2,1,0:T(8,128)(2,1)S(1)}, u32[]{:S(2)}, u32[]{:S(2)}) async-start(bf16[16,64,768]{2,1,0:T(8,128)(2,1)} %bitcast.1), calls=%async_computation | async-start | bytes 3145728 | tf_op jit(solution)/shard_map/all_to_all | solution.py:500
  31.8 52.3 %collective-permute-start.1 = (bf16[2,48,1152]{2,1,0:T(8,128)(2,1)S(1)}, bf16[2,48,1152]{2,1,0:T(8,128)(2,1)S(1)}, u32[]{:S(2)}, u32[]{:S(2)}) collective-permute-start(bf16[2,48,1152]{2,1,0:T(8,128)(2,1)S(1)} %maximum_select_fusion.7), channel_id=1, source_target_pairs={{0,8},{2,10},{4,12},{6,14},{8,0},{10,2},{12,4},{14,6},{16,24},{18,... | collective-permute-start | bytes 663560 | tf_op jit(solution)/shard_map/ppermute | solution.py:360
  84.2 23.0 %collective-permute-start.2 = (bf16[4,48,1152]{2,1,0:T(8,128)(2,1)S(1)}, bf16[4,48,1152]{2,1,0:T(8,128)(2,1)S(1)}, u32[]{:S(2)}, u32[]{:S(2)}) collective-permute-start(bf16[4,48,1152]{2,1,0:T(8,128)(2,1)S(1)} %bitcast.207), channel_id=1, source_target_pairs={{0,4},{2,6},{4,0},{6,2},{8,12},{10,14},{12,8},{14,10},{16,20},{18,... | collective-permute-start | bytes 1327112 | tf_op jit(solution)/shard_map/ppermute | solution.py:360
  107.4 23.5 %collective-permute-start.3 = (bf16[8,48,1152]{2,1,0:T(8,128)(2,1)S(1)}, bf16[8,48,1152]{2,1,0:T(8,128)(2,1)S(1)}, u32[]{:S(2)}, u32[]{:S(2)}) collective-permute-start(bf16[8,48,1152]{2,1,0:T(8,128)(2,1)S(1)} %bitcast.204), channel_id=1, source_target_pairs={{0,1},{1,0},{2,3},{3,2},{4,5},{5,4},{6,7},{7,6},{8,9},{9,8},{10,11... | collective-permute-start | bytes 2654216 | tf_op jit(solution)/shard_map/ppermute | solution.py:346
  133.4 14.6 %collective-permute-start.4 = (bf16[8,48,2304]{2,1,0:T(8,128)(2,1)}, bf16[8,48,2304]{2,1,0:T(8,128)(2,1)}, u32[]{:S(2)}, u32[]{:S(2)}) collective-permute-start(bf16[8,48,2304]{2,1,0:T(8,128)(2,1)} %get-tuple-element.114), channel_id=1, source_target_pairs={{0,2},{2,0},{4,6},{6,4},{8,10},{10,8},{12,14},{14,12},{16,18},{18,... | collective-permute-start | bytes 5308424 | tf_op jit(solution)/shard_map/ppermute | solution.py:371
  141.4 70.2 %all-to-all-start.1 = ((bf16[16,64,768]{2,1,0:T(8,128)(2,1)}), bf16[16,64,768]{2,1,0:T(8,128)(2,1)S(1)}, u32[]{:S(2)}, u32[]{:S(2)}) async-start(bf16[16,64,768]{2,1,0:T(8,128)(2,1)} %bitcast.211), calls=%async_computation.1 | async-start | bytes 3145728 | tf_op jit(solution)/shard_map/all_to_all | solution.py:503
  145.3 335.1 %reduce-scatter.2.cloned.1.call-start = ((), (), s32[]{:S(2)}) async-start(), calls=%async_computation.6 | async-start | bytes 11280384 | tf_op jit(solution)/shard_map/reduce_scatter | solution.py:456
  145.8 35.6 %collective-permute-start.5 = (bf16[1024,768]{1,0:T(8,128)(2,1)S(1)}, bf16[1024,768]{1,0:T(8,128)(2,1)S(1)}, u32[]{:S(2)}, u32[]{:S(2)}) collective-permute-start(bf16[1024,768]{1,0:T(8,128)(2,1)S(1)} %bitcast.181), channel_id=1, source_target_pairs={{0,1},{1,0},{2,3},{3,2},{4,5},{5,4},{6,7},{7,6},{8,9},{9,8},{10,11... | collective-permute-start | bytes 4718600 | tf_op jit(solution)/shard_map/ppermute | solution.py:346
  327.8 67.8 %collective-permute-start.7 = (bf16[1024,768]{1,0:T(8,128)(2,1)}, bf16[1024,768]{1,0:T(8,128)(2,1)}, u32[]{:S(2)}, u32[]{:S(2)}) collective-permute-start(bf16[1024,768]{1,0:T(8,128)(2,1)} %fusion.45), channel_id=1, source_target_pairs={{0,1},{1,0},{2,3},{3,2},{4,5},{5,4},{6,7},{7,6},{8,9},{9,8},{10,11... | collective-permute-start | bytes 4718600 | tf_op jit(solution)/shard_map/ppermute | solution.py:346
  374.9 10.1 %collective-permute-start.8 = (bf16[8,48,768]{2,1,0:T(8,128)(2,1)}, bf16[8,48,768]{2,1,0:T(8,128)(2,1)}, u32[]{:S(2)}, u32[]{:S(2)}) collective-permute-start(bf16[8,48,768]{2,1,0:T(8,128)(2,1)} %select_bitcast_fusion.1), channel_id=1, source_target_pairs={{0,2},{2,0},{4,6},{6,4},{8,10},{10,8},{12,14},{14,12},{16,18},{18,... | collective-permute-start | bytes 1769480 | tf_op jit(solution)/shard_map/ppermute | solution.py:391
  377.3 11.7 %collective-permute-start.10 = (bf16[8,48,1536]{2,1,0:T(8,128)(2,1)}, bf16[8,48,1536]{2,1,0:T(8,128)(2,1)}, u32[]{:S(2)}, u32[]{:S(2)}) collective-permute-start(bf16[8,48,1536]{2,1,0:T(8,128)(2,1)} %select_bitcast_fusion), channel_id=1, source_target_pairs={{0,2},{2,0},{4,6},{6,4},{8,10},{10,8},{12,14},{14,12},{16,18},{18,... | collective-permute-start | bytes 3538952 | tf_op jit(solution)/shard_map/ppermute | solution.py:391
  388.7 14.2 %collective-permute-start.9 = (bf16[8,48,384]{2,1,0:T(8,128)(2,1)S(1)}, bf16[8,48,384]{2,1,0:T(8,128)(2,1)}, u32[]{:S(2)}, u32[]{:S(2)}) collective-permute-start(bf16[8,48,384]{2,1,0:T(8,128)(2,1)S(1)} %broadcast_select_fusion.1), channel_id=1, source_target_pairs={{0,1},{1,0},{2,3},{3,2},{4,5},{5,4},{6,7},{7,6},{8,9},{9,8},{10,11... | collective-permute-start | bytes 884744 | tf_op jit(solution)/shard_map/ppermute | solution.py:346
  394.0 17.2 %collective-permute-start.11 = (bf16[8,48,768]{2,1,0:T(8,128)(2,1)}, bf16[8,48,768]{2,1,0:T(8,128)(2,1)}, u32[]{:S(2)}, u32[]{:S(2)}) collective-permute-start(bf16[8,48,768]{2,1,0:T(8,128)(2,1)} %broadcast_select_fusion), channel_id=1, source_target_pairs={{0,1},{1,0},{2,3},{3,2},{4,5},{5,4},{6,7},{7,6},{8,9},{9,8},{10,11... | collective-permute-start | bytes 1769480 | tf_op jit(solution)/shard_map/ppermute | solution.py:346
  402.5 8.7 %collective-permute-start.13 = (f32[12,768]{1,0:T(8,128)S(1)}, f32[12,768]{1,0:T(8,128)S(1)}, u32[]{:S(2)}, u32[]{:S(2)}) collective-permute-start(f32[12,768]{1,0:T(8,128)S(1)} %add.248), channel_id=1, source_target_pairs={{0,1},{1,0},{2,3},{3,2},{4,5},{5,4},{6,7},{7,6},{8,9},{9,8},{10,11... | collective-permute-start | bytes 110600 | tf_op jit(solution)/shard_map/ppermute | solution.py:346
  415.8 20.8 %collective-permute-start.14 = (bf16[4,48,1152]{2,1,0:T(8,128)(2,1)}, bf16[4,48,1152]{2,1,0:T(8,128)(2,1)}, u32[]{:S(2)}, u32[]{:S(2)}) collective-permute-start(bf16[4,48,1152]{2,1,0:T(8,128)(2,1)} %select_bitcast_fusion.2), channel_id=1, source_target_pairs={{0,4},{2,6},{4,0},{6,2},{8,12},{10,14},{12,8},{14,10},{16,20},{18,... | collective-permute-start | bytes 1327112 | tf_op jit(solution)/shard_map/ppermute | solution.py:413
  415.8 49.6 %all-to-all-start.2 = ((bf16[16,64,768]{2,1,0:T(8,128)(2,1)}), bf16[16,64,768]{2,1,0:T(8,128)(2,1)}, u32[]{:S(2)}, u32[]{:S(2)}) async-start(bf16[16,64,768]{2,1,0:T(8,128)(2,1)} %bitcast.209), calls=%async_computation.2 | async-start | bytes 3145728 | tf_op jit(solution)/shard_map/all_to_all | solution.py:625
  422.7 13.9 %collective-permute-start.15 = (f32[12,768]{1,0:T(8,128)S(1)}, f32[12,768]{1,0:T(8,128)S(1)}, u32[]{:S(2)}, u32[]{:S(2)}) collective-permute-start(f32[12,768]{1,0:T(8,128)S(1)} %add.249), channel_id=1, source_target_pairs={{0,4},{2,6},{4,0},{6,2},{8,12},{10,14},{12,8},{14,10},{16,20},{18,... | collective-permute-start | bytes 110600 | tf_op jit(solution)/shard_map/ppermute | solution.py:413
  438.1 12.4 %collective-permute-start.17 = (f32[12,768]{1,0:T(8,128)S(1)}, f32[12,768]{1,0:T(8,128)S(1)}, u32[]{:S(2)}, u32[]{:S(2)}) collective-permute-start(f32[12,768]{1,0:T(8,128)S(1)} %add.251), channel_id=1, source_target_pairs={{0,8},{2,10},{4,12},{6,14},{8,0},{10,2},{12,4},{14,6},{16,24},{18,... | collective-permute-start | bytes 110600 | tf_op jit(solution)/shard_map/ppermute | solution.py:413
  439.1 16.0 %collective-permute-start.16 = (bf16[2,48,1152]{2,1,0:T(8,128)(2,1)S(1)}, bf16[2,48,1152]{2,1,0:T(8,128)(2,1)S(1)}, u32[]{:S(2)}, u32[]{:S(2)}) collective-permute-start(bf16[2,48,1152]{2,1,0:T(8,128)(2,1)S(1)} %fusion.58), channel_id=1, source_target_pairs={{0,8},{2,10},{4,12},{6,14},{8,0},{10,2},{12,4},{14,6},{16,24},{18,... | collective-permute-start | bytes 663560 | tf_op jit(solution)/shard_map/ppermute | solution.py:413
  465.4 43.5 %all-to-all-start.3 = ((bf16[16,64,768]{2,1,0:T(8,128)(2,1)}), bf16[16,64,768]{2,1,0:T(8,128)(2,1)S(1)}, u32[]{:S(2)}, u32[]{:S(2)}) async-start(bf16[16,64,768]{2,1,0:T(8,128)(2,1)} %bitcast.194), calls=%async_computation.3 | async-start | bytes 3145728 | tf_op jit(solution)/shard_map/all_to_all | solution.py:626
  483.2 29.2 %collective-permute-start.20 = (bf16[48,3456]{1,0:T(8,128)(2,1)}, bf16[48,3456]{1,0:T(8,128)(2,1)}, u32[]{:S(2)}, u32[]{:S(2)}) collective-permute-start(bf16[48,3456]{1,0:T(8,128)(2,1)} %pad_maximum_fusion.5), channel_id=1, source_target_pairs={{0,1},{1,0},{2,3},{3,2},{4,5},{5,4},{6,7},{7,6},{8,9},{9,8},{10,11... | collective-permute-start | bytes 995336 | tf_op jit(solution)/shard_map/ppermute | solution.py:346
  (61 other events, 1344.3 us)
Sparse Core Ops, SparseCore 0:
  20.4 124.8 all-gather.1
  286.4 121.6 reduce-scatter.1

commit v7 on v6

--- a/solution.py
+++ b/solution.py
@@ -9,6 +9,7 @@
 from jax.sharding import PartitionSpec as P
 
 
+DP, TP = "dp", "tensor"
 HD = 64
 LANES = 128
 EPS = 1e-06
@@ -263,8 +264,8 @@
 
 
 def small_kernel(n_dp, slice_ref, bias_ref, all_ref, partner_ref, send_sem, recv_sem):
-    me = lax.axis_index("dp")
-    t = lax.axis_index("tensor")
+    me = lax.axis_index(DP)
+    t = lax.axis_index(TP)
 
     barrier = pltpu.get_barrier_semaphore()
 
@@ -343,11 +344,11 @@
 
 
 def swap(values):
-    return lax.ppermute(values, "tensor", [(0, 1), (1, 0)])
+    return lax.ppermute(values, TP, [(0, 1), (1, 0)])
 
 
 def tree_gather(n_dp, t, values, split):
-    me = lax.axis_index("dp")
+    me = lax.axis_index(DP)
 
     def joined(own, other, upper, axis):
         return jnp.where(
@@ -357,7 +358,7 @@
     blocks = values[None]
     steps = [1 << bit for bit in range(n_dp.bit_length() - 1)]
     for step in reversed(steps[1:]):
-        other = lax.ppermute(blocks, "dp", [(i, i ^ step) for i in range(n_dp)])
+        other = lax.ppermute(blocks, DP, [(i, i ^ step) for i in range(n_dp)])
         upper = (me // step) % 2 == 1
         blocks = joined(blocks[:, None], other[:, None], upper, 1).reshape((-1,) + values.shape)
     other = swap(blocks)
@@ -368,7 +369,7 @@
         ],
         axis=2,
     )
-    other = lax.ppermute(blocks, "dp", [(i, i ^ 1) for i in range(n_dp)])
+    other = lax.ppermute(blocks, DP, [(i, i ^ 1) for i in range(n_dp)])
     full = joined(blocks[:, None], other[:, None], me % 2 == 1, 1)
     full = full.reshape(n_dp * values.shape[0], 2 * values.shape[1])
     return full
@@ -385,10 +386,10 @@
 
 
 def sum_on_chip(n_dp, piece, values):
-    odd = lax.axis_index("dp") % 2 == 1
+    odd = lax.axis_index(DP) % 2 == 1
     blocks = values.reshape(n_dp // 2, 2, piece, values.shape[-1])
     return add_half(
-        blocks[:, 0], blocks[:, 1], odd, lambda v: lax.ppermute(v, "dp", dp_partners(n_dp, 1))
+        blocks[:, 0], blocks[:, 1], odd, lambda v: lax.ppermute(v, DP, dp_partners(n_dp, 1))
     )
 
 
@@ -398,8 +399,8 @@
 
 
 def tree_sum(n_dp, piece, total, rows):
-    me = lax.axis_index("dp")
-    arrived_rows = lax.ppermute(rows, "dp", dp_partners(n_dp, 1))
+    me = lax.axis_index(DP)
+    arrived_rows = lax.ppermute(rows, DP, dp_partners(n_dp, 1))
     rows = rows + arrived_rows
     arrived_rows = swap(rows)
     rows = rows + arrived_rows
@@ -410,7 +411,7 @@
         sent, rows = after(jnp.where(upper, blocks[:, 0], blocks[:, 1]), rows)
         partners = dp_partners(n_dp, step)
         arrived, arrived_rows = after(
-            lax.ppermute(sent, "dp", partners), lax.ppermute(rows, "dp", partners)
+            lax.ppermute(sent, DP, partners), lax.ppermute(rows, DP, partners)
         )
         mine = jnp.where(upper, blocks[:, 1], blocks[:, 0])
         total = (mine.astype(F32) + arrived.astype(F32)).astype(BF16)
@@ -437,8 +438,8 @@
     w_down,
     b_down,
 ):
-    n_dp = lax.axis_size("dp")
-    t = lax.axis_index("tensor")
+    n_dp = lax.axis_size(DP)
+    t = lax.axis_index(TP)
     rows, width = tokens.shape
     piece = ln1_gain.shape[0]
     half = b_qv.shape[1]
@@ -453,7 +454,7 @@
         )
 
     def reduced(values):
-        return lax.psum_scatter(values, "dp", scatter_dimension=0, tiled=True)
+        return lax.psum_scatter(values, DP, scatter_dimension=0, tiled=True)
 
     def mine_of(values, axis):
         size = values.shape[axis] // 2
@@ -482,7 +483,7 @@
         ],
         axis=1,
     )
-    rest = lax.all_gather(rest_local, "dp", axis=0, tiled=True)
+    rest = lax.all_gather(rest_local, DP, axis=0, tiled=True)
     wout_t = rest[:, :width]
     wup = rest[:, width : width + 2 * hidden_half]
     wdown_t = rest[:, width + 2 * hidden_half :]
@@ -497,10 +498,10 @@
     row_order = dealing[0]
     picks = (row_order[:, None] == jnp.arange(rows, dtype=jnp.int32)[None, :]).astype(BF16)
     sent_rows = mm(picks, tokens).astype(BF16)
-    dealt = lax.all_to_all(sent_rows, "dp", split_axis=0, concat_axis=0, tiled=True)
+    dealt = lax.all_to_all(sent_rows, DP, split_axis=0, concat_axis=0, tiled=True)
     grad_tokens, dealt = after(grad_tokens, dealt)
     sent_grads = mm(picks, grad_tokens).astype(BF16)
-    grad_out = lax.all_to_all(sent_grads, "dp", split_axis=0, concat_axis=0, tiled=True)
+    grad_out = lax.all_to_all(sent_grads, DP, split_axis=0, concat_axis=0, tiled=True)
     dealt_of_pair = by_rows(swap(dealt))
     joined = (segment_ids[:1] == segment_ids[-1:]).astype(jnp.int32)
 
@@ -570,7 +571,9 @@
     dq, dkv, grad_wq, grad_wkv = after(dq, dkv, grad_wq, grad_wkv)
     wq_sum = sum_on_chip(n_dp, piece, grad_wq)
     wkv_sum = sum_on_chip(n_dp, piece, grad_wkv)
-    wqkv_sum = jnp.concatenate([sum_over_tensor(t, wq_sum), sum_over_tensor(t, wkv_sum)], axis=-1)
+    wqkv_sum = jnp.concatenate(
+        [sum_over_tensor(t, wq_sum), sum_over_tensor(t, wkv_sum)], axis=-1
+    )
     grad_ln_one = by_rows(mm(dq, wq, 1, 1) + mm(dkv, wkv, 1, 1) + for_pair.astype(F32))
     grad_input = (
         grad_hidden + norm_back(grad_ln_one, normed_one, factor_one, small_full[0])
@@ -597,7 +600,7 @@
     )
     qkv_part, row_sums = tree_sum(n_dp, piece, wqkv_sum, row_sums)
     small_part = lax.dynamic_slice_in_dim(
-        row_sums[:6], lax.axis_index("dp") * piece, piece, 1
+        row_sums[:6], lax.axis_index(DP) * piece, piece, 1
     )
     qv_part = mine_of(row_sums[6:8], 1)[0]
     bias_up_part = mine_of(row_sums[8:].reshape(-1), 0)[0]
@@ -622,8 +625,8 @@
         [q_part.reshape(piece, 1, half), kv_part.reshape(piece, 2, half)], axis=1
     )
 
-    sent_out = lax.all_to_all(output, "dp", split_axis=0, concat_axis=0, tiled=True)
-    sent_grad = lax.all_to_all(grad_input, "dp", split_axis=0, concat_axis=0, tiled=True)
+    sent_out = lax.all_to_all(output, DP, split_axis=0, concat_axis=0, tiled=True)
+    sent_grad = lax.all_to_all(grad_input, DP, split_axis=0, concat_axis=0, tiled=True)
     restored_out = mm(picks, sent_out, 0, 0).astype(BF16)
     restored_grad = mm(picks, sent_grad, 0, 0).astype(BF16)
     return (
@@ -645,44 +648,14 @@
 
 
 def solution(mesh):
-    placed = (
-        P(("dp", "tensor"), None),
-        P(("dp", "tensor"), None),
-        P(("dp", "tensor"), None),
-        P("dp"),
-        P("dp"),
-        P("dp"),
-        P("dp", None, "tensor"),
-        P(None, "tensor"),
-        P("tensor", "dp"),
-        P("dp"),
-        P("dp"),
-        P("dp"),
-        P("dp", "tensor"),
-        P("tensor"),
-        P("tensor", "dp"),
-        P("dp"),
-    )
+    both, dp, tp, by_both = P((DP, TP), None), P(DP), P(TP), P(DP, TP)
+    placed = (both, both, both, dp, dp, dp, P(DP, None, TP), P(None, TP), P(TP, DP), dp, dp, dp)
+    placed += (by_both, tp, P(TP, DP), dp)
 
     return jax.shard_map(
         per_device,
         mesh=mesh,
         in_specs=placed,
-        out_specs=(
-            P(("dp", "tensor"), None),
-            P(("dp", "tensor"), None),
-            P("dp"),
-            P("dp"),
-            P("dp", None, "tensor"),
-            P(None, "tensor"),
-            P("tensor", "dp"),
-            P("dp"),
-            P("dp"),
-            P("dp"),
-            P("dp", "tensor"),
-            P("tensor"),
-            P("tensor", "dp"),
-            P("dp"),
-        ),
+        out_specs=placed[:2] + placed[4:],
         check_vma=False,
     )

time: 529 us -> 529 us (level)
  no operation moved by 1% of the time
where the time goes in v7:
time: 529 us; the launch traced here: 522 us
  waiting for transfers between devices  150 us (28%)
  Pallas kernels  134 us (25%)
  matrix products  112 us (21%)
  other arithmetic  50.4 us (10%)
  starting transfers between devices  43 us (8%)
  between operations  16.9 us (3%)
  local copies, waits for them, and re-layouts  15.4 us (3%)
    dot_general x21, matrix products, mm(): lax.dot_general(left, right, (((left_dim,), (right_dim,)), ((), ())), pre...  112 us
    ppermute x3, waiting for transfers between devices, tree_gather(): other = lax.ppermute(blocks, DP, [(i, i ^ step) for i in range(n_dp)])  74.7 us
    pallas_call x1, Pallas kernels, attention_back_pair(): pl.pallas_call(functools.partial(pair_backward, kblock=min(512, rows)), g...  35.5 us
    pallas_call x1, Pallas kernels, attention_back_own(): pl.pallas_call(functools.partial(own_backward, kblock=min(512, rows)), gr...  35.1 us
    all_to_all x1, waiting for transfers between devices, per_device(): lax.all_to_all(grad_input, DP, split_axis=0, concat_axis=0, tiled=True)  25.7 us
    ppermute x3, waiting for transfers between devices, tree_sum(): lax.ppermute(rows, DP, partners)  25.4 us
    pallas_call x1, Pallas kernels, attention_pair(): pl.pallas_call(functools.partial(pair_forward, qblock=min(512, rows)), gr...  23.1 us
    pallas_call x1, Pallas kernels, attention_own(): pl.pallas_call(functools.partial(own_forward, qblock=min(512, rows)), gri...  21.3 us
  transfers between devices with their start and end apart: 27, of which 12 were waited for; matrix products, arithmetic and copies ran while one was open for 18% of the time, Pallas kernels for 26%

profile of v7, /device:TPU:11, one launch (start us, length us, event | category | flops | bytes accessed | tf_op | source)
XLA Modules:
  0.0 522.0 jit_solution(10933028385019253862)
XLA Ops:
  9.7 7.4 %collective-permute-done.6 = bf16[48,3456]{1,0:T(8,128)(2,1)S(1)} collective-permute-done((bf16[48,3456]{1,0:T(8,128)(2,1)S(1)}, bf16[48,3456]{1,0:T(8,128)(2,1)S(1)}, u32[]{:S(2)}, u32[]{:S(2)}) %collective-permute-start.6) | collective-permute-done | bytes 331808 | tf_op jit(solution)/shard_map/ppermute | solution.py:347
  26.0 5.6 %all-to-all-start = ((bf16[16,64,768]{2,1,0:T(8,128)(2,1)}), bf16[16,64,768]{2,1,0:T(8,128)(2,1)S(1)}, u32[]{:S(2)}, u32[]{:S(2)}) async-start(bf16[16,64,768]{2,1,0:T(8,128)(2,1)} %bitcast.1), calls=%async_computation | async-start | bytes 3145728 | tf_op jit(solution)/shard_map/all_to_all | solution.py:501
  32.2 51.9 %collective-permute-done.1 = bf16[2,48,1152]{2,1,0:T(8,128)(2,1)S(1)} collective-permute-done((bf16[2,48,1152]{2,1,0:T(8,128)(2,1)S(1)}, bf16[2,48,1152]{2,1,0:T(8,128)(2,1)S(1)}, u32[]{:S(2)}, u32[]{:S(2)}) %collective-permute-start.1) | collective-permute-done | bytes 221216 | tf_op jit(solution)/shard_map/ppermute | solution.py:361
  84.4 22.8 %collective-permute-done.2 = bf16[4,48,1152]{2,1,0:T(8,128)(2,1)S(1)} collective-permute-done((bf16[4,48,1152]{2,1,0:T(8,128)(2,1)S(1)}, bf16[4,48,1152]{2,1,0:T(8,128)(2,1)S(1)}, u32[]{:S(2)}, u32[]{:S(2)}) %collective-permute-start.2) | collective-permute-done | bytes 442400 | tf_op jit(solution)/shard_map/ppermute | solution.py:361
  109.9 19.1 %share_small.1 = (f32[16,8,128]{2,1,0:T(8,128)}, f32[24,128]{1,0:T(8,128)}) custom-call(f32[8,128]{1,0:T(8,128)} %pad.9.slice_ref, f32[24,128]{1,0:T(8,128)} %fusion.66.bias_ref), custom_call_target="tpu_custom_call" | custom-call | tf_op jit(solution)/shard_map/share_small/pallas_call | solution.py:321
  152.2 5.9 %add_convert_fusion.1.q_ref.kv_ref = bf16[1024,2304]{1,0:T(8,128)(2,1)} fusion(bf16[768,2304]{1,0:T(8,128)(2,1)S(1)} %bitcast.199, f32[2304]{0:T(1024)S(1)} %pad_maximum_fusion.8, f32[2304]{0:T(1024)S(1)} %copy-done.50, bf16[1024,768]{1,0:T(8,128)(2,1)S(1)} %bitcast.184, f32[768]{0:T(1024)S(1)} %add.206, f32[768]{0:T(1024)S(1)} %mul.173, ...), kind=kOutput, calls=%fused_computation.8 | convolution fusion | flops 3635675136 | bytes 9863168 | tf_op jit(solution)/shard_map/dot_general | solution.py:38
  158.2 21.3 %attend_own.1 = (f32[1024,768]{1,0:T(8,128)}, f32[1024,768]{1,0:T(8,128)}) custom-call(bf16[1024,2304]{1,0:T(8,128)(2,1)} %add_convert_fusion.1.q_ref.kv_ref, bf16[1024,2304]{1,0:T(8,128)(2,1)} %add_convert_fusion.1.q_ref.kv_ref), custom_call_target="tpu_custom_call" | custom-call | flops 12884901888 | bytes 4718592 | tf_op jit(solution)/shard_map/attend_own/pallas_call | solution.py:189
  182.4 6.0 %add_convert_fusion.2.kv_ref = bf16[1024,1536]{1,0:T(8,128)(2,1)} fusion(f32[1536]{0:T(1024)S(1)} %reshape.396, bf16[768,2304]{1,0:T(8,128)(2,1)} %bitcast.200, bf16[1024,768]{1,0:T(8,128)(2,1)S(1)} %collective-permute-done.5, f32[1024]{0:T(1024)S(1)} %add_rsqrt_fusion.1, f32[1024]{0:T(1024)S(1)} %broadcast_multiply_fusion.5, f32[768]{0:T(1024)S(1)} %add.206, ...), kind=kOutput, calls=%fused_computation.11 | convolution fusion | flops 2423783424 | bytes 7098368 | tf_op jit(solution)/shard_map/dot_general | solution.py:38
  188.4 23.1 %attend_pair.1 = (bf16[1024,768]{1,0:T(8,128)(2,1)}, f32[1024,768]{1,0:T(8,128)}) custom-call(s32[1]{0:T(128)S(6)} %convert_element_type.206.joined_ref, bf16[1024,2304]{1,0:T(8,128)(2,1)} %add_convert_fusion.1.q_ref.kv_ref, bf16[1024,1536]{1,0:T(8,128)(2,1)} %add_convert_fusion.2.kv_ref, f32[1024,768]{1,0:T(8,128)} %get-tuple-element.60.own_ref, ...), custom_call_target="tpu_custom_call" | custom-call | flops 12884901888 | bytes 4718592 | tf_op jit(solution)/shard_map/attend_pair/pallas_call | solution.py:206
  218.7 13.7 %add_convert_fusion = (bf16[1024,3072]{1,0:T(8,128)(2,1)}, bf16[1024,3072]{1,0:T(8,128)(2,1)}) fusion(f32[3072]{0:T(1024)S(1)} %maximum_select_fusion.10, bf16[768,6912]{1,0:T(8,128)(2,1)S(1)} %bitcast.229, f32[1024,768]{1,0:T(8,128)S(1)} %get-tuple-element.137, f32[768]{0:T(1024)S(1)} %add.224, f32[768]{0:T(1024)S(1)} %mul.188, ...), kind=kOutput, calls=%fused_computation.2 | convolution fusion | flops 4892393472 | bytes 20475904 | tf_op jit(solution)/shard_map/dot_general | solution.py:38
  232.4 7.2 %convert_reduce_fusion = (f32[3072]{0:T(1024)S(1)}, bf16[1024,3072]{1,0:T(8,128)(2,1)S(1)}) fusion(bf16[1024,3072]{1,0:T(8,128)(2,1)} %get-tuple-element.64, bf16[1024,768]{1,0:T(8,128)(2,1)S(1)} %bitcast.190, bf16[768,6912]{1,0:T(8,128)(2,1)S(1)} %bitcast.229), kind=kOutput, calls=%fused_computation | convolution fusion | flops 4847563776 | bytes 18886656 | tf_op jit(solution)/shard_map/dot_general | solution.py:38
  239.6 6.4 %convolution_convert_fusion = bf16[768,3072]{1,0:T(8,128)(2,1)S(1)} fusion(bf16[1024,3072]{1,0:T(8,128)(2,1)S(1)} %get-tuple-element.67, f32[1024,768]{1,0:T(8,128)S(1)} %get-tuple-element.137, f32[768]{0:T(1024)S(1)} %add.224, f32[768]{0:T(1024)S(1)} %mul.188, f32[1024]{0:T(1024)S(1)} %add_rsqrt_fusion, f32[1024]{0:T(1024)S(1)} %broadcast_multiply_fusion.4), kind=kOutput, calls=%fused_computation.12 | convolution fusion | flops 4838129664 | bytes 14170112 | tf_op jit(solution)/shard_map/dot_general | solution.py:38
  251.6 8.3 %multiply_reduce_fusion = (f32[768]{0:T(1024)S(1)}, f32[1024]{0:T(1024)S(1)}, f32[1024]{0:T(1024)S(1)}, f32[768]{0:T(1024)S(1)}, f32[1024,768]{1,0:T(8,128)S(1)}) fusion(f32[1024,768]{1,0:T(8,128)S(1)} %get-tuple-element.137, f32[1024]{0:T(1024)S(1)} %add_rsqrt_fusion, f32[1024]{0:T(1024)S(1)} %broadcast_multiply_fusion.4, f32[768]{0:T(1024)S(1)} %mul.188, ...), kind=kOutput, calls=%fused_computation.57 | convolution fusion | flops 4838912000 | bytes 17327104 | tf_op jit(solution)/shard_map/dot_general | solution.py:38
  264.4 8.0 %pad_maximum_fusion = bf16[768,6912]{1,0:T(8,128)(2,1)} fusion(bf16[768,768]{1,0:T(8,128)(2,1)S(1)} %convolution_convert_fusion.4, bf16[768,3072]{1,0:T(8,128)(2,1)S(1)} %convolution_convert_fusion, bf16[768,3072]{1,0:T(8,128)(2,1)S(1)} %convolution_convert_fusion.1), kind=kLoop, calls=%fused_computation.7 | loop fusion | flops 31850496 | bytes 21233664 | tf_op jit(solution)/shard_map/concatenate | solution.py:556
  276.8 9.5 %add_convert_fusion.4 = bf16[1024,768]{1,0:T(8,128)(2,1)} fusion(f32[1024,768]{1,0:T(8,128)S(1)} %copy-done.9, bf16[1024,3072]{1,0:T(8,128)(2,1)} %get-tuple-element.69, bf16[768,6912]{1,0:T(8,128)(2,1)} %all-gather.2.cloned.1.call-done, f32[768]{0:T(1024)S(1)} %add.235), kind=kOutput, calls=%fused_computation.59 | convolution fusion | flops 4834197504 | bytes 15731712 | tf_op jit(solution)/shard_map/dot_general | solution.py:38
  286.3 35.5 %attend_back_pair.1 = (f32[768,1024]{1,0:T(8,128)}, bf16[1024,1536]{1,0:T(8,128)(2,1)}) custom-call(s32[1]{0:T(128)S(6)} %convert_element_type.206.joined_ref, bf16[1024,2304]{1,0:T(8,128)(2,1)} %add_convert_fusion.1.q_ref.kv_ref, bf16[1024,768]{1,0:T(8,128)(2,1)} %convolution_convert_fusion.2.grad_ref, bf16[1024,768]{1,0:T(8,128)(2,1)} %get-tuple-element.62.mixed_ref, ...), custom_call_target="tpu_custom_call" | custom-call | flops 32212254720 | bytes 4718592 | tf_op jit(solution)/shard_map/attend_back_pair/pallas_call | solution.py:227
  321.8 6.0 %fusion.45 = bf16[1024,768]{1,0:T(8,128)(2,1)} fusion(bf16[1024,1536]{1,0:T(8,128)(2,1)} %get-tuple-element.76, bf16[768,2304]{1,0:T(8,128)(2,1)S(1)} %bitcast.202), kind=kOutput, calls=%fused_computation.79 | convolution fusion | flops 2416705536 | bytes 7077888 | tf_op jit(solution)/shard_map/dot_general | solution.py:38
  329.0 35.1 %attend_back_own.1 = (bf16[1024,768]{1,0:T(8,128)(2,1)}, bf16[1024,1536]{1,0:T(8,128)(2,1)}) custom-call(bf16[1024,2304]{1,0:T(8,128)(2,1)} %add_convert_fusion.1.q_ref.kv_ref, bf16[1024,768]{1,0:T(8,128)(2,1)} %convolution_convert_fusion.2.grad_ref, bf16[1024,768]{1,0:T(8,128)(2,1)} %get-tuple-element.62.mixed_ref, f32[1024,768]{1,0:T(8,128)} %get-tuple-element.72.lse_ref, ...), custom_call_target="tpu_custom_call" | custom-call | flops 32212254720 | bytes 4718592 | tf_op jit(solution)/shard_map/attend_back_own/pallas_call | solution.py:250
  404.2 7.0 %collective-permute-done.13 = f32[12,768]{1,0:T(8,128)S(1)} collective-permute-done((f32[12,768]{1,0:T(8,128)S(1)}, f32[12,768]{1,0:T(8,128)S(1)}, u32[]{:S(2)}, u32[]{:S(2)}) %collective-permute-start.13) | collective-permute-done | bytes 36896 | tf_op jit(solution)/shard_map/ppermute | solution.py:347
  415.8 6.9 %all-to-all-start.2 = ((bf16[16,64,768]{2,1,0:T(8,128)(2,1)}), bf16[16,64,768]{2,1,0:T(8,128)(2,1)}, u32[]{:S(2)}, u32[]{:S(2)}) async-start(bf16[16,64,768]{2,1,0:T(8,128)(2,1)} %bitcast.209), calls=%async_computation.2 | async-start | bytes 3145728 | tf_op jit(solution)/shard_map/all_to_all | solution.py:628
  423.1 13.5 %collective-permute-done.15 = f32[12,768]{1,0:T(8,128)S(1)} collective-permute-done((f32[12,768]{1,0:T(8,128)S(1)}, f32[12,768]{1,0:T(8,128)S(1)}, u32[]{:S(2)}, u32[]{:S(2)}) %collective-permute-start.15) | collective-permute-done | bytes 36896 | tf_op jit(solution)/shard_map/ppermute | solution.py:414
  439.6 10.9 %collective-permute-done.17 = f32[12,768]{1,0:T(8,128)S(1)} collective-permute-done((f32[12,768]{1,0:T(8,128)S(1)}, f32[12,768]{1,0:T(8,128)S(1)}, u32[]{:S(2)}, u32[]{:S(2)}) %collective-permute-start.17) | collective-permute-done | bytes 36896 | tf_op jit(solution)/shard_map/ppermute | solution.py:414
  465.4 7.3 %all-to-all-start.3 = ((bf16[16,64,768]{2,1,0:T(8,128)(2,1)}), bf16[16,64,768]{2,1,0:T(8,128)(2,1)S(1)}, u32[]{:S(2)}, u32[]{:S(2)}) async-start(bf16[16,64,768]{2,1,0:T(8,128)(2,1)} %bitcast.194), calls=%async_computation.3 | async-start | bytes 3145728 | tf_op jit(solution)/shard_map/all_to_all | solution.py:629
  483.2 25.7 %all-to-all-done.3 = bf16[16,64,768]{2,1,0:T(8,128)(2,1)S(1)} async-done(((bf16[16,64,768]{2,1,0:T(8,128)(2,1)}), bf16[16,64,768]{2,1,0:T(8,128)(2,1)S(1)}, u32[]{:S(2)}, u32[]{:S(2)}) %all-to-all-start.3) | async-done | bytes 1572896 | tf_op jit(solution)/shard_map/all_to_all | solution.py:629
  (295 shorter events, 141.0 us)
Async XLA Ops:
  7.2 205.4 %all-gather.2.cloned.1.call-start = ((), (), s32[]{:S(2)}) async-start(), calls=%async_computation.5 | async-start | bytes 11280384 | tf_op jit(solution)/shard_map/all_gather | solution.py:486
  8.4 8.7 %collective-permute-start.6 = (bf16[48,3456]{1,0:T(8,128)(2,1)S(1)}, bf16[48,3456]{1,0:T(8,128)(2,1)S(1)}, u32[]{:S(2)}, u32[]{:S(2)}) collective-permute-start(bf16[48,3456]{1,0:T(8,128)(2,1)S(1)} %pad_maximum_fusion.4), channel_id=1, source_target_pairs={{0,1},{1,0},{2,3},{3,2},{4,5},{5,4},{6,7},{7,6},{8,9},{9,8},{10,11... | collective-permute-start | bytes 995336 | tf_op jit(solution)/shard_map/ppermute | solution.py:347
  20.5 11.3 %collective-permute-start = (bf16[1,48,1152]{2,1,0:T(8,128)(2,1)S(1)}, bf16[1,48,1152]{2,1,0:T(8,128)(2,1)S(1)}, u32[]{:S(2)}, u32[]{:S(2)}) collective-permute-start(bf16[1,48,1152]{2,1,0:T(8,128)(2,1)S(1)} %get-tuple-element.126), channel_id=1, source_target_pairs={{0,16},{2,18},{4,20},{6,22},{8,24},{10,26},{12,28},{14,30},{16,0},... | collective-permute-start | bytes 331784 | tf_op jit(solution)/shard_map/ppermute | solution.py:361
  26.0 112.2 %all-to-all-start = ((bf16[16,64,768]{2,1,0:T(8,128)(2,1)}), bf16[16,64,768]{2,1,0:T(8,128)(2,1)S(1)}, u32[]{:S(2)}, u32[]{:S(2)}) async-start(bf16[16,64,768]{2,1,0:T(8,128)(2,1)} %bitcast.1), calls=%async_computation | async-start | bytes 3145728 | tf_op jit(solution)/shard_map/all_to_all | solution.py:501
  31.8 52.3 %collective-permute-start.1 = (bf16[2,48,1152]{2,1,0:T(8,128)(2,1)S(1)}, bf16[2,48,1152]{2,1,0:T(8,128)(2,1)S(1)}, u32[]{:S(2)}, u32[]{:S(2)}) collective-permute-start(bf16[2,48,1152]{2,1,0:T(8,128)(2,1)S(1)} %maximum_select_fusion.7), channel_id=1, source_target_pairs={{0,8},{2,10},{4,12},{6,14},{8,0},{10,2},{12,4},{14,6},{16,24},{18,... | collective-permute-start | bytes 663560 | tf_op jit(solution)/shard_map/ppermute | solution.py:361
  84.2 23.0 %collective-permute-start.2 = (bf16[4,48,1152]{2,1,0:T(8,128)(2,1)S(1)}, bf16[4,48,1152]{2,1,0:T(8,128)(2,1)S(1)}, u32[]{:S(2)}, u32[]{:S(2)}) collective-permute-start(bf16[4,48,1152]{2,1,0:T(8,128)(2,1)S(1)} %bitcast.207), channel_id=1, source_target_pairs={{0,4},{2,6},{4,0},{6,2},{8,12},{10,14},{12,8},{14,10},{16,20},{18,... | collective-permute-start | bytes 1327112 | tf_op jit(solution)/shard_map/ppermute | solution.py:361
  107.4 23.5 %collective-permute-start.3 = (bf16[8,48,1152]{2,1,0:T(8,128)(2,1)S(1)}, bf16[8,48,1152]{2,1,0:T(8,128)(2,1)S(1)}, u32[]{:S(2)}, u32[]{:S(2)}) collective-permute-start(bf16[8,48,1152]{2,1,0:T(8,128)(2,1)S(1)} %bitcast.204), channel_id=1, source_target_pairs={{0,1},{1,0},{2,3},{3,2},{4,5},{5,4},{6,7},{7,6},{8,9},{9,8},{10,11... | collective-permute-start | bytes 2654216 | tf_op jit(solution)/shard_map/ppermute | solution.py:347
  133.4 14.6 %collective-permute-start.4 = (bf16[8,48,2304]{2,1,0:T(8,128)(2,1)}, bf16[8,48,2304]{2,1,0:T(8,128)(2,1)}, u32[]{:S(2)}, u32[]{:S(2)}) collective-permute-start(bf16[8,48,2304]{2,1,0:T(8,128)(2,1)} %get-tuple-element.114), channel_id=1, source_target_pairs={{0,2},{2,0},{4,6},{6,4},{8,10},{10,8},{12,14},{14,12},{16,18},{18,... | collective-permute-start | bytes 5308424 | tf_op jit(solution)/shard_map/ppermute | solution.py:372
  141.4 70.2 %all-to-all-start.1 = ((bf16[16,64,768]{2,1,0:T(8,128)(2,1)}), bf16[16,64,768]{2,1,0:T(8,128)(2,1)S(1)}, u32[]{:S(2)}, u32[]{:S(2)}) async-start(bf16[16,64,768]{2,1,0:T(8,128)(2,1)} %bitcast.211), calls=%async_computation.1 | async-start | bytes 3145728 | tf_op jit(solution)/shard_map/all_to_all | solution.py:504
  145.3 335.1 %reduce-scatter.2.cloned.1.call-start = ((), (), s32[]{:S(2)}) async-start(), calls=%async_computation.6 | async-start | bytes 11280384 | tf_op jit(solution)/shard_map/reduce_scatter | solution.py:457
  145.8 35.6 %collective-permute-start.5 = (bf16[1024,768]{1,0:T(8,128)(2,1)S(1)}, bf16[1024,768]{1,0:T(8,128)(2,1)S(1)}, u32[]{:S(2)}, u32[]{:S(2)}) collective-permute-start(bf16[1024,768]{1,0:T(8,128)(2,1)S(1)} %bitcast.181), channel_id=1, source_target_pairs={{0,1},{1,0},{2,3},{3,2},{4,5},{5,4},{6,7},{7,6},{8,9},{9,8},{10,11... | collective-permute-start | bytes 4718600 | tf_op jit(solution)/shard_map/ppermute | solution.py:347
  327.8 67.8 %collective-permute-start.7 = (bf16[1024,768]{1,0:T(8,128)(2,1)}, bf16[1024,768]{1,0:T(8,128)(2,1)}, u32[]{:S(2)}, u32[]{:S(2)}) collective-permute-start(bf16[1024,768]{1,0:T(8,128)(2,1)} %fusion.45), channel_id=1, source_target_pairs={{0,1},{1,0},{2,3},{3,2},{4,5},{5,4},{6,7},{7,6},{8,9},{9,8},{10,11... | collective-permute-start | bytes 4718600 | tf_op jit(solution)/shard_map/ppermute | solution.py:347
  374.9 10.1 %collective-permute-start.8 = (bf16[8,48,768]{2,1,0:T(8,128)(2,1)}, bf16[8,48,768]{2,1,0:T(8,128)(2,1)}, u32[]{:S(2)}, u32[]{:S(2)}) collective-permute-start(bf16[8,48,768]{2,1,0:T(8,128)(2,1)} %select_bitcast_fusion.1), channel_id=1, source_target_pairs={{0,2},{2,0},{4,6},{6,4},{8,10},{10,8},{12,14},{14,12},{16,18},{18,... | collective-permute-start | bytes 1769480 | tf_op jit(solution)/shard_map/ppermute | solution.py:392
  377.3 11.7 %collective-permute-start.10 = (bf16[8,48,1536]{2,1,0:T(8,128)(2,1)}, bf16[8,48,1536]{2,1,0:T(8,128)(2,1)}, u32[]{:S(2)}, u32[]{:S(2)}) collective-permute-start(bf16[8,48,1536]{2,1,0:T(8,128)(2,1)} %select_bitcast_fusion), channel_id=1, source_target_pairs={{0,2},{2,0},{4,6},{6,4},{8,10},{10,8},{12,14},{14,12},{16,18},{18,... | collective-permute-start | bytes 3538952 | tf_op jit(solution)/shard_map/ppermute | solution.py:392
  388.7 14.2 %collective-permute-start.9 = (bf16[8,48,384]{2,1,0:T(8,128)(2,1)S(1)}, bf16[8,48,384]{2,1,0:T(8,128)(2,1)}, u32[]{:S(2)}, u32[]{:S(2)}) collective-permute-start(bf16[8,48,384]{2,1,0:T(8,128)(2,1)S(1)} %broadcast_select_fusion.1), channel_id=1, source_target_pairs={{0,1},{1,0},{2,3},{3,2},{4,5},{5,4},{6,7},{7,6},{8,9},{9,8},{10,11... | collective-permute-start | bytes 884744 | tf_op jit(solution)/shard_map/ppermute | solution.py:347
  394.0 17.2 %collective-permute-start.11 = (bf16[8,48,768]{2,1,0:T(8,128)(2,1)}, bf16[8,48,768]{2,1,0:T(8,128)(2,1)}, u32[]{:S(2)}, u32[]{:S(2)}) collective-permute-start(bf16[8,48,768]{2,1,0:T(8,128)(2,1)} %broadcast_select_fusion), channel_id=1, source_target_pairs={{0,1},{1,0},{2,3},{3,2},{4,5},{5,4},{6,7},{7,6},{8,9},{9,8},{10,11... | collective-permute-start | bytes 1769480 | tf_op jit(solution)/shard_map/ppermute | solution.py:347
  402.5 8.7 %collective-permute-start.13 = (f32[12,768]{1,0:T(8,128)S(1)}, f32[12,768]{1,0:T(8,128)S(1)}, u32[]{:S(2)}, u32[]{:S(2)}) collective-permute-start(f32[12,768]{1,0:T(8,128)S(1)} %add.248), channel_id=1, source_target_pairs={{0,1},{1,0},{2,3},{3,2},{4,5},{5,4},{6,7},{7,6},{8,9},{9,8},{10,11... | collective-permute-start | bytes 110600 | tf_op jit(solution)/shard_map/ppermute | solution.py:347
  415.8 20.8 %collective-permute-start.14 = (bf16[4,48,1152]{2,1,0:T(8,128)(2,1)}, bf16[4,48,1152]{2,1,0:T(8,128)(2,1)}, u32[]{:S(2)}, u32[]{:S(2)}) collective-permute-start(bf16[4,48,1152]{2,1,0:T(8,128)(2,1)} %select_bitcast_fusion.2), channel_id=1, source_target_pairs={{0,4},{2,6},{4,0},{6,2},{8,12},{10,14},{12,8},{14,10},{16,20},{18,... | collective-permute-start | bytes 1327112 | tf_op jit(solution)/shard_map/ppermute | solution.py:414
  415.8 49.6 %all-to-all-start.2 = ((bf16[16,64,768]{2,1,0:T(8,128)(2,1)}), bf16[16,64,768]{2,1,0:T(8,128)(2,1)}, u32[]{:S(2)}, u32[]{:S(2)}) async-start(bf16[16,64,768]{2,1,0:T(8,128)(2,1)} %bitcast.209), calls=%async_computation.2 | async-start | bytes 3145728 | tf_op jit(solution)/shard_map/all_to_all | solution.py:628
  422.7 13.9 %collective-permute-start.15 = (f32[12,768]{1,0:T(8,128)S(1)}, f32[12,768]{1,0:T(8,128)S(1)}, u32[]{:S(2)}, u32[]{:S(2)}) collective-permute-start(f32[12,768]{1,0:T(8,128)S(1)} %add.249), channel_id=1, source_target_pairs={{0,4},{2,6},{4,0},{6,2},{8,12},{10,14},{12,8},{14,10},{16,20},{18,... | collective-permute-start | bytes 110600 | tf_op jit(solution)/shard_map/ppermute | solution.py:414
  438.1 12.4 %collective-permute-start.17 = (f32[12,768]{1,0:T(8,128)S(1)}, f32[12,768]{1,0:T(8,128)S(1)}, u32[]{:S(2)}, u32[]{:S(2)}) collective-permute-start(f32[12,768]{1,0:T(8,128)S(1)} %add.251), channel_id=1, source_target_pairs={{0,8},{2,10},{4,12},{6,14},{8,0},{10,2},{12,4},{14,6},{16,24},{18,... | collective-permute-start | bytes 110600 | tf_op jit(solution)/shard_map/ppermute | solution.py:414
  439.1 16.0 %collective-permute-start.16 = (bf16[2,48,1152]{2,1,0:T(8,128)(2,1)S(1)}, bf16[2,48,1152]{2,1,0:T(8,128)(2,1)S(1)}, u32[]{:S(2)}, u32[]{:S(2)}) collective-permute-start(bf16[2,48,1152]{2,1,0:T(8,128)(2,1)S(1)} %fusion.58), channel_id=1, source_target_pairs={{0,8},{2,10},{4,12},{6,14},{8,0},{10,2},{12,4},{14,6},{16,24},{18,... | collective-permute-start | bytes 663560 | tf_op jit(solution)/shard_map/ppermute | solution.py:414
  465.4 43.5 %all-to-all-start.3 = ((bf16[16,64,768]{2,1,0:T(8,128)(2,1)}), bf16[16,64,768]{2,1,0:T(8,128)(2,1)S(1)}, u32[]{:S(2)}, u32[]{:S(2)}) async-start(bf16[16,64,768]{2,1,0:T(8,128)(2,1)} %bitcast.194), calls=%async_computation.3 | async-start | bytes 3145728 | tf_op jit(solution)/shard_map/all_to_all | solution.py:629
  483.2 29.2 %collective-permute-start.20 = (bf16[48,3456]{1,0:T(8,128)(2,1)}, bf16[48,3456]{1,0:T(8,128)(2,1)}, u32[]{:S(2)}, u32[]{:S(2)}) collective-permute-start(bf16[48,3456]{1,0:T(8,128)(2,1)} %pad_maximum_fusion.5), channel_id=1, source_target_pairs={{0,1},{1,0},{2,3},{3,2},{4,5},{5,4},{6,7},{7,6},{8,9},{9,8},{10,11... | collective-permute-start | bytes 995336 | tf_op jit(solution)/shard_map/ppermute | solution.py:347
  (61 other events, 1344.3 us)
Sparse Core Ops, SparseCore 0:
  20.4 124.8 all-gather.1
  286.4 121.6 reduce-scatter.1

commit v8 on v7

--- a/solution.py
+++ b/solution.py
@@ -499,7 +499,6 @@
     picks = (row_order[:, None] == jnp.arange(rows, dtype=jnp.int32)[None, :]).astype(BF16)
     sent_rows = mm(picks, tokens).astype(BF16)
     dealt = lax.all_to_all(sent_rows, DP, split_axis=0, concat_axis=0, tiled=True)
-    grad_tokens, dealt = after(grad_tokens, dealt)
     sent_grads = mm(picks, grad_tokens).astype(BF16)
     grad_out = lax.all_to_all(sent_grads, DP, split_axis=0, concat_axis=0, tiled=True)
     dealt_of_pair = by_rows(swap(dealt))
@@ -535,10 +534,10 @@
     ln_two = ln_two.astype(BF16)
     pre_act = mm(ln_two, wup) + bup_full
     square = pre_act * pre_act
-    bend = jnp.tanh(pre_act * (GELU_ONE + GELU_THREE * square))
-    gate = 0.5 + 0.5 * bend
-    slope = gate + (0.5 * pre_act) * (1.0 - bend * bend) * (GELU_ONE + 3.0 * GELU_THREE * square)
-    act, slope = after((pre_act * gate).astype(BF16), slope.astype(BF16))
+    gate = 0.5 + 0.5 * jnp.tanh(pre_act * (GELU_ONE + GELU_THREE * square))
+    act = pre_act * gate
+    slope = gate + (act - act * gate) * (2.0 * GELU_ONE + 6.0 * GELU_THREE * square)
+    act, slope = after(act.astype(BF16), slope.astype(BF16))
 
     grad_down_t = mm(grad_out, act, 0, 0).astype(BF16)
     grad_pre = (mm(grad_out, wdown_t) * slope.astype(F32)).astype(BF16)

time: 529 us -> 558 us (1.055)
  the two profiles are of different devices: /device:TPU:11 before, /device:TPU:0 now
where the time goes in v8:
time: 558 us; the launch traced here: 548 us
  waiting for transfers between devices  162 us (29%)
  matrix products  110 us (20%)
  Pallas kernels  109 us (20%)
  starting transfers between devices  86.6 us (16%)
  other arithmetic  44.4 us (8%)
  local copies, waits for them, and re-layouts  18.3 us (3%)
  between operations  16.8 us (3%)
    dot_general x21, matrix products, mm(): lax.dot_general(left, right, (((left_dim,), (right_dim,)), ((), ())), pre...  110 us
    ppermute x3, waiting for transfers between devices, tree_gather(): other = lax.ppermute(blocks, DP, [(i, i ^ step) for i in range(n_dp)])  86.5 us
    ppermute x2, starting transfers between devices, sum_on_chip(): lax.ppermute(v, DP, dp_partners(n_dp, 1))  41.7 us
    pallas_call x1, Pallas kernels, share_small(): pl.pallas_call(functools.partial(small_kernel, n_dp), in_specs=[vmem, vme...  37.2 us
    pallas_call x1, Pallas kernels, attention_back_own(): pl.pallas_call(functools.partial(own_backward, kblock=min(512, rows)), gr...  35.1 us
    ppermute x3, waiting for transfers between devices, tree_sum(): lax.ppermute(rows, DP, partners)  25.5 us
    pallas_call x1, Pallas kernels, attention_own(): pl.pallas_call(functools.partial(own_forward, qblock=min(512, rows)), gri...  21.2 us
    all_to_all x1, waiting for transfers between devices, per_device(): lax.all_to_all(grad_input, DP, split_axis=0, concat_axis=0, tiled=True)  20.9 us
  transfers between devices with their start and end apart: 27, of which 13 were waited for; matrix products, arithmetic and copies ran while one was open for 17% of the time, Pallas kernels for 20%

profile of v8, /device:TPU:0, one launch (start us, length us, event | category | flops | bytes accessed | tf_op | source)
XLA Modules:
  0.0 548.2 jit_solution(15971663679019035389)
XLA Ops:
  11.4 7.8 %collective-permute-done.6 = bf16[48,3456]{1,0:T(8,128)(2,1)S(1)} collective-permute-done((bf16[48,3456]{1,0:T(8,128)(2,1)S(1)}, bf16[48,3456]{1,0:T(8,128)(2,1)S(1)}, u32[]{:S(2)}, u32[]{:S(2)}) %collective-permute-start.6) | collective-permute-done | bytes 331808 | tf_op jit(solution)/shard_map/ppermute | solution.py:347
  25.5 6.3 %all-to-all-start = ((bf16[16,64,768]{2,1,0:T(8,128)(2,1)}), bf16[16,64,768]{2,1,0:T(8,128)(2,1)S(1)}, u32[]{:S(2)}, u32[]{:S(2)}) async-start(bf16[16,64,768]{2,1,0:T(8,128)(2,1)} %bitcast.1), calls=%async_computation | async-start | bytes 3145728 | tf_op jit(solution)/shard_map/all_to_all | solution.py:503
  34.9 63.5 %collective-permute-done = bf16[1,48,1152]{2,1,0:T(8,128)(2,1)S(1)} collective-permute-done((bf16[1,48,1152]{2,1,0:T(8,128)(2,1)S(1)}, bf16[1,48,1152]{2,1,0:T(8,128)(2,1)S(1)}, u32[]{:S(2)}, u32[]{:S(2)}) %collective-permute-start) | collective-permute-done | bytes 110624 | tf_op jit(solution)/shard_map/ppermute | solution.py:361
  98.5 22.3 %collective-permute-done.1 = bf16[2,48,1152]{2,1,0:T(8,128)(2,1)S(1)} collective-permute-done((bf16[2,48,1152]{2,1,0:T(8,128)(2,1)S(1)}, bf16[2,48,1152]{2,1,0:T(8,128)(2,1)S(1)}, u32[]{:S(2)}, u32[]{:S(2)}) %collective-permute-start.1) | collective-permute-done | bytes 221216 | tf_op jit(solution)/shard_map/ppermute | solution.py:361
  140.9 37.2 %share_small.1 = (f32[16,8,128]{2,1,0:T(8,128)}, f32[24,128]{1,0:T(8,128)}) custom-call(f32[8,128]{1,0:T(8,128)} %pad.9.slice_ref, f32[24,128]{1,0:T(8,128)} %fusion.71.bias_ref), custom_call_target="tpu_custom_call" | custom-call | tf_op jit(solution)/shard_map/share_small/pallas_call | solution.py:321
  195.6 5.4 add_convert_fusion.q_ref.kv_ref
  201.0 21.2 %attend_own.1 = (f32[1024,768]{1,0:T(8,128)}, f32[1024,768]{1,0:T(8,128)}) custom-call(bf16[1024,2304]{1,0:T(8,128)(2,1)} %add_convert_fusion.q_ref.kv_ref, bf16[1024,2304]{1,0:T(8,128)(2,1)} %add_convert_fusion.q_ref.kv_ref), custom_call_target="tpu_custom_call" | custom-call | flops 12884901888 | bytes 4718592 | tf_op jit(solution)/shard_map/attend_own/pallas_call | solution.py:189
  225.6 5.9 %add_convert_fusion.1.kv_ref = bf16[1024,1536]{1,0:T(8,128)(2,1)} fusion(f32[1536]{0:T(1024)S(1)} %reshape.396, bf16[768,2304]{1,0:T(8,128)(2,1)} %bitcast.203, bf16[1024,768]{1,0:T(8,128)(2,1)S(1)} %collective-permute-done.5, f32[1024]{0:T(1024)S(1)} %add_rsqrt_fusion.1, f32[1024]{0:T(1024)S(1)} %broadcast_multiply_fusion.5, f32[768]{0:T(1024)S(1)} %add.212, ...), kind=kOutput, calls=%fused_computation.13 | convolution fusion | flops 2423783424 | bytes 7098368 | tf_op jit(solution)/shard_map/dot_general | solution.py:38
  231.5 7.6 %attend_pair.1 = (bf16[1024,768]{1,0:T(8,128)(2,1)}, f32[1024,768]{1,0:T(8,128)}) custom-call(s32[1]{0:T(128)S(6)} %convert_element_type.206.joined_ref, bf16[1024,2304]{1,0:T(8,128)(2,1)} %add_convert_fusion.q_ref.kv_ref, bf16[1024,1536]{1,0:T(8,128)(2,1)} %add_convert_fusion.1.kv_ref, f32[1024,768]{1,0:T(8,128)} %get-tuple-element.56.own_ref, ...), custom_call_target="tpu_custom_call" | custom-call | flops 12884901888 | bytes 4718592 | tf_op jit(solution)/shard_map/attend_pair/pallas_call | solution.py:206
  243.0 14.0 %fusion.2 = (bf16[1024,3072]{1,0:T(8,128)(2,1)S(1)}, bf16[1024,3072]{1,0:T(8,128)(2,1)}) fusion(f32[3072]{0:T(1024)S(1)} %maximum_select_fusion.10, bf16[768,6912]{1,0:T(8,128)(2,1)} %all-gather.2.cloned.1.call-done, f32[1024,768]{1,0:T(8,128)S(1)} %get-tuple-element.133, f32[768]{0:T(1024)S(1)} %add.230, f32[768]{0:T(1024)S(1)} %mul.182, ...), kind=kOutput, calls=%fused_computation.3 | convolution fusion | flops 4886102016 | bytes 20473856 | tf_op jit(solution)/shard_map/dot_general | solution.py:38
  257.0 7.7 %convert_reduce_fusion = (f32[3072]{0:T(1024)S(1)}, bf16[1024,3072]{1,0:T(8,128)(2,1)S(1)}) fusion(bf16[1024,3072]{1,0:T(8,128)(2,1)S(1)} %get-tuple-element.60, bf16[1024,768]{1,0:T(8,128)(2,1)S(1)} %bitcast.192, bf16[768,6912]{1,0:T(8,128)(2,1)} %all-gather.2.cloned.1.call-done), kind=kOutput, calls=%fused_computation.4 | convolution fusion | flops 4847563776 | bytes 18886656 | tf_op jit(solution)/shard_map/dot_general | solution.py:38
  264.7 6.6 %convolution_convert_fusion = bf16[768,3072]{1,0:T(8,128)(2,1)S(1)} fusion(bf16[1024,3072]{1,0:T(8,128)(2,1)S(1)} %get-tuple-element.63, f32[1024,768]{1,0:T(8,128)S(1)} %get-tuple-element.133, f32[768]{0:T(1024)S(1)} %add.230, f32[768]{0:T(1024)S(1)} %mul.182, f32[1024]{0:T(1024)S(1)} %add_rsqrt_fusion, f32[1024]{0:T(1024)S(1)} %broadcast_multiply_fusion.4), kind=kOutput, calls=%fused_computation.14 | convolution fusion | flops 4838129664 | bytes 14170112 | tf_op jit(solution)/shard_map/dot_general | solution.py:38
  276.7 8.1 %multiply_reduce_fusion = (f32[768]{0:T(1024)S(1)}, f32[1024]{0:T(1024)S(1)}, f32[1024]{0:T(1024)S(1)}, f32[768]{0:T(1024)S(1)}, f32[1024,768]{1,0:T(8,128)S(1)}) fusion(f32[1024,768]{1,0:T(8,128)S(1)} %get-tuple-element.133, f32[1024]{0:T(1024)S(1)} %add_rsqrt_fusion, f32[1024]{0:T(1024)S(1)} %broadcast_multiply_fusion.4, f32[768]{0:T(1024)S(1)} %mul.182, ...), kind=kOutput, calls=%fused_computation.59 | convolution fusion | flops 4838912000 | bytes 17327104 | tf_op jit(solution)/shard_map/dot_general | solution.py:38
  290.4 8.4 %pad_maximum_fusion = bf16[768,6912]{1,0:T(8,128)(2,1)} fusion(bf16[768,768]{1,0:T(8,128)(2,1)S(1)} %convolution_convert_fusion.4, bf16[768,3072]{1,0:T(8,128)(2,1)S(1)} %convolution_convert_fusion, bf16[768,3072]{1,0:T(8,128)(2,1)S(1)} %convolution_convert_fusion.1), kind=kLoop, calls=%fused_computation.9 | loop fusion | flops 31850496 | bytes 21233664 | tf_op jit(solution)/shard_map/concatenate | solution.py:555
  302.8 9.5 %add_convert_fusion.3 = bf16[1024,768]{1,0:T(8,128)(2,1)} fusion(f32[1024,768]{1,0:T(8,128)S(1)} %copy-done.7, bf16[1024,3072]{1,0:T(8,128)(2,1)} %get-tuple-element.65, bf16[768,6912]{1,0:T(8,128)(2,1)} %all-gather.2.cloned.1.call-done, f32[768]{0:T(1024)S(1)} %add.243), kind=kOutput, calls=%fused_computation.61 | convolution fusion | flops 4834197504 | bytes 15731712 | tf_op jit(solution)/shard_map/dot_general | solution.py:38
  312.3 8.4 %attend_back_pair.1 = (f32[768,1024]{1,0:T(8,128)}, bf16[1024,1536]{1,0:T(8,128)(2,1)}) custom-call(s32[1]{0:T(128)S(6)} %convert_element_type.206.joined_ref, bf16[1024,2304]{1,0:T(8,128)(2,1)} %add_convert_fusion.q_ref.kv_ref, bf16[1024,768]{1,0:T(8,128)(2,1)} %convolution_convert_fusion.2.grad_ref, bf16[1024,768]{1,0:T(8,128)(2,1)} %get-tuple-element.58.mixed_ref, ...), custom_call_target="tpu_custom_call" | custom-call | flops 32212254720 | bytes 4718592 | tf_op jit(solution)/shard_map/attend_back_pair/pallas_call | solution.py:227
  320.7 5.6 %fusion.50 = bf16[1024,768]{1,0:T(8,128)(2,1)} fusion(bf16[1024,1536]{1,0:T(8,128)(2,1)} %get-tuple-element.72, bf16[768,2304]{1,0:T(8,128)(2,1)S(1)} %bitcast.205), kind=kOutput, calls=%fused_computation.81 | convolution fusion | flops 2416705536 | bytes 7077888 | tf_op jit(solution)/shard_map/dot_general | solution.py:38
  327.8 35.1 %attend_back_own.1 = (bf16[1024,768]{1,0:T(8,128)(2,1)}, bf16[1024,1536]{1,0:T(8,128)(2,1)}) custom-call(bf16[1024,2304]{1,0:T(8,128)(2,1)} %add_convert_fusion.q_ref.kv_ref, bf16[1024,768]{1,0:T(8,128)(2,1)} %convolution_convert_fusion.2.grad_ref, bf16[1024,768]{1,0:T(8,128)(2,1)} %get-tuple-element.58.mixed_ref, f32[1024,768]{1,0:T(8,128)} %get-tuple-element.68.lse_ref, ...), custom_call_target="tpu_custom_call" | custom-call | flops 32212254720 | bytes 4718592 | tf_op jit(solution)/shard_map/attend_back_own/pallas_call | solution.py:250
  372.3 41.6 %collective-permute-start.8 = (bf16[8,48,768]{2,1,0:T(8,128)(2,1)S(1)}, bf16[8,48,768]{2,1,0:T(8,128)(2,1)}, u32[]{:S(2)}, u32[]{:S(2)}) collective-permute-start(bf16[8,48,768]{2,1,0:T(8,128)(2,1)S(1)} %select_bitcast_fusion.1), channel_id=1, source_target_pairs={{0,2},{2,0},{4,6},{6,4},{8,10},{10,8},{12,14},{14,12},{16,18},{18,... | collective-permute-start | bytes 1769480 | tf_op jit(solution)/shard_map/ppermute | solution.py:392
  436.8 9.6 %collective-permute-done.13 = f32[12,768]{1,0:T(8,128)S(1)} collective-permute-done((f32[12,768]{1,0:T(8,128)S(1)}, f32[12,768]{1,0:T(8,128)S(1)}, u32[]{:S(2)}, u32[]{:S(2)}) %collective-permute-start.13) | collective-permute-done | bytes 36896 | tf_op jit(solution)/shard_map/ppermute | solution.py:347
  456.0 17.0 %collective-permute-done.15 = f32[12,768]{1,0:T(8,128)S(1)} collective-permute-done((f32[12,768]{1,0:T(8,128)S(1)}, f32[12,768]{1,0:T(8,128)S(1)}, u32[]{:S(2)}, u32[]{:S(2)}) %collective-permute-start.15) | collective-permute-done | bytes 36896 | tf_op jit(solution)/shard_map/ppermute | solution.py:414
  475.3 6.5 %collective-permute-done.17 = f32[12,768]{1,0:T(8,128)S(1)} collective-permute-done((f32[12,768]{1,0:T(8,128)S(1)}, f32[12,768]{1,0:T(8,128)S(1)}, u32[]{:S(2)}, u32[]{:S(2)}) %collective-permute-start.17) | collective-permute-done | bytes 36896 | tf_op jit(solution)/shard_map/ppermute | solution.py:414
  481.8 6.3 %collective-permute-done.16 = bf16[2,48,1152]{2,1,0:T(8,128)(2,1)S(1)} collective-permute-done((bf16[2,48,1152]{2,1,0:T(8,128)(2,1)S(1)}, bf16[2,48,1152]{2,1,0:T(8,128)(2,1)S(1)}, u32[]{:S(2)}, u32[]{:S(2)}) %collective-permute-start.16) | collective-permute-done | bytes 221216 | tf_op jit(solution)/shard_map/ppermute | solution.py:414
  514.0 20.9 %all-to-all-done.3 = bf16[16,64,768]{2,1,0:T(8,128)(2,1)S(1)} async-done(((bf16[16,64,768]{2,1,0:T(8,128)(2,1)}), bf16[16,64,768]{2,1,0:T(8,128)(2,1)S(1)}, u32[]{:S(2)}, u32[]{:S(2)}) %all-to-all-start.3) | async-done | bytes 1572896 | tf_op jit(solution)/shard_map/all_to_all | solution.py:628
  (281 shorter events, 148.8 us)
Async XLA Ops:
  7.2 231.9 %all-gather.2.cloned.1.call-start = ((), (), s32[]{:S(2)}) async-start(), calls=%async_computation.5 | async-start | bytes 11280384 | tf_op jit(solution)/shard_map/all_gather | solution.py:486
  8.4 10.9 %collective-permute-start.6 = (bf16[48,3456]{1,0:T(8,128)(2,1)S(1)}, bf16[48,3456]{1,0:T(8,128)(2,1)S(1)}, u32[]{:S(2)}, u32[]{:S(2)}) collective-permute-start(bf16[48,3456]{1,0:T(8,128)(2,1)S(1)} %pad_maximum_fusion.4), channel_id=1, source_target_pairs={{0,1},{1,0},{2,3},{3,2},{4,5},{5,4},{6,7},{7,6},{8,9},{9,8},{10,11... | collective-permute-start | bytes 995336 | tf_op jit(solution)/shard_map/ppermute | solution.py:347
  25.5 102.1 %all-to-all-start = ((bf16[16,64,768]{2,1,0:T(8,128)(2,1)}), bf16[16,64,768]{2,1,0:T(8,128)(2,1)S(1)}, u32[]{:S(2)}, u32[]{:S(2)}) async-start(bf16[16,64,768]{2,1,0:T(8,128)(2,1)} %bitcast.1), calls=%async_computation | async-start | bytes 3145728 | tf_op jit(solution)/shard_map/all_to_all | solution.py:503
  32.0 66.4 %collective-permute-start = (bf16[1,48,1152]{2,1,0:T(8,128)(2,1)S(1)}, bf16[1,48,1152]{2,1,0:T(8,128)(2,1)S(1)}, u32[]{:S(2)}, u32[]{:S(2)}) collective-permute-start(bf16[1,48,1152]{2,1,0:T(8,128)(2,1)S(1)} %get-tuple-element.122), channel_id=1, source_target_pairs={{0,16},{2,18},{4,20},{6,22},{8,24},{10,26},{12,28},{14,30},{16,0},... | collective-permute-start | bytes 331784 | tf_op jit(solution)/shard_map/ppermute | solution.py:361
  98.4 22.4 %collective-permute-start.1 = (bf16[2,48,1152]{2,1,0:T(8,128)(2,1)S(1)}, bf16[2,48,1152]{2,1,0:T(8,128)(2,1)S(1)}, u32[]{:S(2)}, u32[]{:S(2)}) collective-permute-start(bf16[2,48,1152]{2,1,0:T(8,128)(2,1)S(1)} %maximum_select_fusion.7), channel_id=1, source_target_pairs={{0,8},{2,10},{4,12},{6,14},{8,0},{10,2},{12,4},{14,6},{16,24},{18,... | collective-permute-start | bytes 663560 | tf_op jit(solution)/shard_map/ppermute | solution.py:361
  121.7 11.1 %collective-permute-start.2 = (bf16[4,48,1152]{2,1,0:T(8,128)(2,1)}, bf16[4,48,1152]{2,1,0:T(8,128)(2,1)}, u32[]{:S(2)}, u32[]{:S(2)}) collective-permute-start(bf16[4,48,1152]{2,1,0:T(8,128)(2,1)} %bitcast.19), channel_id=1, source_target_pairs={{0,4},{2,6},{4,0},{6,2},{8,12},{10,14},{12,8},{14,10},{16,20},{18,... | collective-permute-start | bytes 1327112 | tf_op jit(solution)/shard_map/ppermute | solution.py:361
  127.6 60.3 %all-to-all-start.1 = ((bf16[16,64,768]{2,1,0:T(8,128)(2,1)}), bf16[16,64,768]{2,1,0:T(8,128)(2,1)S(1)}, u32[]{:S(2)}, u32[]{:S(2)}) async-start(bf16[16,64,768]{2,1,0:T(8,128)(2,1)} %bitcast.208), calls=%async_computation.1 | async-start | bytes 3145728 | tf_op jit(solution)/shard_map/all_to_all | solution.py:501
  131.5 379.4 %reduce-scatter.2.cloned.1.call-start = ((), (), s32[]{:S(2)}) async-start(), calls=%async_computation.6 | async-start | bytes 11280384 | tf_op jit(solution)/shard_map/reduce_scatter | solution.py:457
  135.4 47.0 %collective-permute-start.3 = (bf16[8,48,1152]{2,1,0:T(8,128)(2,1)}, bf16[8,48,1152]{2,1,0:T(8,128)(2,1)}, u32[]{:S(2)}, u32[]{:S(2)}) collective-permute-start(bf16[8,48,1152]{2,1,0:T(8,128)(2,1)} %bitcast.22), channel_id=1, source_target_pairs={{0,1},{1,0},{2,3},{3,2},{4,5},{5,4},{6,7},{7,6},{8,9},{9,8},{10,11... | collective-permute-start | bytes 2654216 | tf_op jit(solution)/shard_map/ppermute | solution.py:347
  188.0 36.7 %collective-permute-start.5 = (bf16[1024,768]{1,0:T(8,128)(2,1)S(1)}, bf16[1024,768]{1,0:T(8,128)(2,1)S(1)}, u32[]{:S(2)}, u32[]{:S(2)}) collective-permute-start(bf16[1024,768]{1,0:T(8,128)(2,1)S(1)} %bitcast.190), channel_id=1, source_target_pairs={{0,1},{1,0},{2,3},{3,2},{4,5},{5,4},{6,7},{7,6},{8,9},{9,8},{10,11... | collective-permute-start | bytes 4718600 | tf_op jit(solution)/shard_map/ppermute | solution.py:347
  326.3 102.4 %collective-permute-start.7 = (bf16[1024,768]{1,0:T(8,128)(2,1)}, bf16[1024,768]{1,0:T(8,128)(2,1)}, u32[]{:S(2)}, u32[]{:S(2)}) collective-permute-start(bf16[1024,768]{1,0:T(8,128)(2,1)} %fusion.50), channel_id=1, source_target_pairs={{0,1},{1,0},{2,3},{3,2},{4,5},{5,4},{6,7},{7,6},{8,9},{9,8},{10,11... | collective-permute-start | bytes 4718600 | tf_op jit(solution)/shard_map/ppermute | solution.py:347
  372.3 48.5 %collective-permute-start.8 = (bf16[8,48,768]{2,1,0:T(8,128)(2,1)S(1)}, bf16[8,48,768]{2,1,0:T(8,128)(2,1)}, u32[]{:S(2)}, u32[]{:S(2)}) collective-permute-start(bf16[8,48,768]{2,1,0:T(8,128)(2,1)S(1)} %select_bitcast_fusion.1), channel_id=1, source_target_pairs={{0,2},{2,0},{4,6},{6,4},{8,10},{10,8},{12,14},{14,12},{16,18},{18,... | collective-permute-start | bytes 1769480 | tf_op jit(solution)/shard_map/ppermute | solution.py:392
  414.0 9.4 %collective-permute-start.10 = (bf16[8,48,1536]{2,1,0:T(8,128)(2,1)S(1)}, bf16[8,48,1536]{2,1,0:T(8,128)(2,1)}, u32[]{:S(2)}, u32[]{:S(2)}) collective-permute-start(bf16[8,48,1536]{2,1,0:T(8,128)(2,1)S(1)} %select_bitcast_fusion), channel_id=1, source_target_pairs={{0,2},{2,0},{4,6},{6,4},{8,10},{10,8},{12,14},{14,12},{16,18},{18,... | collective-permute-start | bytes 3538952 | tf_op jit(solution)/shard_map/ppermute | solution.py:392
  422.9 12.9 %collective-permute-start.9 = (bf16[8,48,384]{2,1,0:T(8,128)(2,1)}, bf16[8,48,384]{2,1,0:T(8,128)(2,1)}, u32[]{:S(2)}, u32[]{:S(2)}) collective-permute-start(bf16[8,48,384]{2,1,0:T(8,128)(2,1)} %broadcast_select_fusion.1), channel_id=1, source_target_pairs={{0,1},{1,0},{2,3},{3,2},{4,5},{5,4},{6,7},{7,6},{8,9},{9,8},{10,11... | collective-permute-start | bytes 884744 | tf_op jit(solution)/shard_map/ppermute | solution.py:347
  427.0 19.4 %collective-permute-start.11 = (bf16[8,48,768]{2,1,0:T(8,128)(2,1)}, bf16[8,48,768]{2,1,0:T(8,128)(2,1)}, u32[]{:S(2)}, u32[]{:S(2)}) collective-permute-start(bf16[8,48,768]{2,1,0:T(8,128)(2,1)} %broadcast_select_fusion), channel_id=1, source_target_pairs={{0,1},{1,0},{2,3},{3,2},{4,5},{5,4},{6,7},{7,6},{8,9},{9,8},{10,11... | collective-permute-start | bytes 1769480 | tf_op jit(solution)/shard_map/ppermute | solution.py:347
  435.4 11.0 %collective-permute-start.13 = (f32[12,768]{1,0:T(8,128)S(1)}, f32[12,768]{1,0:T(8,128)S(1)}, u32[]{:S(2)}, u32[]{:S(2)}) collective-permute-start(f32[12,768]{1,0:T(8,128)S(1)} %add.256), channel_id=1, source_target_pairs={{0,1},{1,0},{2,3},{3,2},{4,5},{5,4},{6,7},{7,6},{8,9},{9,8},{10,11... | collective-permute-start | bytes 110600 | tf_op jit(solution)/shard_map/ppermute | solution.py:347
  447.9 25.1 %collective-permute-start.14 = (bf16[4,48,1152]{2,1,0:T(8,128)(2,1)S(1)}, bf16[4,48,1152]{2,1,0:T(8,128)(2,1)S(1)}, u32[]{:S(2)}, u32[]{:S(2)}) collective-permute-start(bf16[4,48,1152]{2,1,0:T(8,128)(2,1)S(1)} %select_bitcast_fusion.2), channel_id=1, source_target_pairs={{0,4},{2,6},{4,0},{6,2},{8,12},{10,14},{12,8},{14,10},{16,20},{18,... | collective-permute-start | bytes 1327112 | tf_op jit(solution)/shard_map/ppermute | solution.py:414
  449.7 48.9 %all-to-all-start.2 = ((bf16[16,64,768]{2,1,0:T(8,128)(2,1)}), bf16[16,64,768]{2,1,0:T(8,128)(2,1)}, u32[]{:S(2)}, u32[]{:S(2)}) async-start(bf16[16,64,768]{2,1,0:T(8,128)(2,1)} %bitcast.207), calls=%async_computation.2 | async-start | bytes 3145728 | tf_op jit(solution)/shard_map/all_to_all | solution.py:627
  454.1 18.8 %collective-permute-start.15 = (f32[12,768]{1,0:T(8,128)S(1)}, f32[12,768]{1,0:T(8,128)S(1)}, u32[]{:S(2)}, u32[]{:S(2)}) collective-permute-start(f32[12,768]{1,0:T(8,128)S(1)} %add.257), channel_id=1, source_target_pairs={{0,4},{2,6},{4,0},{6,2},{8,12},{10,14},{12,8},{14,10},{16,20},{18,... | collective-permute-start | bytes 110600 | tf_op jit(solution)/shard_map/ppermute | solution.py:414
  473.2 8.6 %collective-permute-start.17 = (f32[12,768]{1,0:T(8,128)S(1)}, f32[12,768]{1,0:T(8,128)S(1)}, u32[]{:S(2)}, u32[]{:S(2)}) collective-permute-start(f32[12,768]{1,0:T(8,128)S(1)} %add.259), channel_id=1, source_target_pairs={{0,8},{2,10},{4,12},{6,14},{8,0},{10,2},{12,4},{14,6},{16,24},{18,... | collective-permute-start | bytes 110600 | tf_op jit(solution)/shard_map/ppermute | solution.py:414
  473.3 14.9 %collective-permute-start.16 = (bf16[2,48,1152]{2,1,0:T(8,128)(2,1)S(1)}, bf16[2,48,1152]{2,1,0:T(8,128)(2,1)S(1)}, u32[]{:S(2)}, u32[]{:S(2)}) collective-permute-start(bf16[2,48,1152]{2,1,0:T(8,128)(2,1)S(1)} %fusion.63), channel_id=1, source_target_pairs={{0,8},{2,10},{4,12},{6,14},{8,0},{10,2},{12,4},{14,6},{16,24},{18,... | collective-permute-start | bytes 663560 | tf_op jit(solution)/shard_map/ppermute | solution.py:414
  488.3 8.5 %collective-permute-start.19 = (f32[12,768]{1,0:T(8,128)S(1)}, f32[12,768]{1,0:T(8,128)S(1)}, u32[]{:S(2)}, u32[]{:S(2)}) collective-permute-start(f32[12,768]{1,0:T(8,128)S(1)} %add.261), channel_id=1, source_target_pairs={{0,16},{2,18},{4,20},{6,22},{8,24},{10,26},{12,28},{14,30},{16,0},... | collective-permute-start | bytes 110600 | tf_op jit(solution)/shard_map/ppermute | solution.py:414
  498.7 36.3 %all-to-all-start.3 = ((bf16[16,64,768]{2,1,0:T(8,128)(2,1)}), bf16[16,64,768]{2,1,0:T(8,128)(2,1)S(1)}, u32[]{:S(2)}, u32[]{:S(2)}) async-start(bf16[16,64,768]{2,1,0:T(8,128)(2,1)} %bitcast.31), calls=%async_computation.3 | async-start | bytes 3145728 | tf_op jit(solution)/shard_map/all_to_all | solution.py:628
  513.6 24.9 %collective-permute-start.20 = (bf16[48,3456]{1,0:T(8,128)(2,1)}, bf16[48,3456]{1,0:T(8,128)(2,1)}, u32[]{:S(2)}, u32[]{:S(2)}) collective-permute-start(bf16[48,3456]{1,0:T(8,128)(2,1)} %pad_maximum_fusion.5), channel_id=1, source_target_pairs={{0,1},{1,0},{2,3},{3,2},{4,5},{5,4},{6,7},{7,6},{8,9},{9,8},{10,11... | collective-permute-start | bytes 995336 | tf_op jit(solution)/shard_map/ppermute | solution.py:347
  (54 other events, 692.1 us)
Sparse Core Ops, SparseCore 0:
  22.5 136.1 all-gather.1
  312.5 134.5 reduce-scatter.1
